TPU v7x, 128 devices: a whole 4x4x4 slice. The times are simulated.
128 devices in a mesh: dp: 32 (over y, x, core), head: 4 (over z).
Axes of the slice: x: 4, y: 4, z: 4, core: 2. Of those that a mesh axis runs over, the one named last changes fastest.
Arguments:
- tokens: bfloat16 [8192, 2048], P('dp', 'head'), may hold values from -6 to 6
- mixer_gain: float32 [2048], replicated, may hold values from 0.1 to 1.9
- query_weight: bfloat16 [2048, 1024], P(None, 'head'), may hold values from -0.125 to 0.125
- key_weight: bfloat16 [3, 2048, 1024], P(None, None, 'head'), may hold values from -0.125 to 0.125
- value_weight: bfloat16 [3, 2048, 1024], P(None, None, 'head'), may hold values from -0.125 to 0.125
- beta_weight: bfloat16 [2048, 24], P(None, 'head'), may hold values from -0.125 to 0.125
- head_gain: float32 [128], replicated, may hold values from 0.1 to 1.9
- output_weight: bfloat16 [1024, 2048], P('head'), may hold values from -0.1875 to 0.1875
- expert_gain: float32 [2048], replicated, may hold values from 0.1 to 1.9
- router_weight: float32 [2048, 64], replicated, may hold values from -0.125 to 0.125
- expert_ids: int32 [8192, 2], P(('dp', 'head')), may hold values from 0 to 63, all different within a row; in each aligned block of 64 rows (0 to 63, 64 to 127, ...) at most 4 rows name the same one
- gate_weight: bfloat16 [64, 2048, 1408], P('dp'), may hold values from -0.125 to 0.125
- up_weight: bfloat16 [64, 2048, 1408], P('dp'), may hold values from -0.125 to 0.125
- down_weight: bfloat16 [64, 1408, 2048], P('dp'), may hold values from -0.15625 to 0.15625
Outputs:
- layer_out: bfloat16 [8192, 2048], P(('dp', 'head'))
Inputs may be any that keep to these rules, and one draw needn't show every extreme that they name: `expert_ids`: taking the tokens in aligned blocks of 64 (the rows of one device), no expert is named by more than 4 rows of a block, a bound that some block reaches; a token's two experts differ.
All inputs are finite; a program needn't handle non-finite values.
Results may differ from a plain program's by a relative error of at most 0.012.
Values may be sent and summed in bfloat16 or wider, within the bound.
No kernel may reach another device: no remote copies, remote signals or barrier semaphores. Data moves between devices by JAX's collectives and lax.ppermute only.
A program may use at most 128 MiB of HBM per device.

v0:
```python
import jax
import jax.numpy as jnp
from jax import lax
from jax.experimental import pallas as pl
from jax.experimental.pallas import tpu as pltpu
from jax.sharding import PartitionSpec as P

DK = 128
NH = 3
CH = 32
SUB = CH * NH
BASE = 4
EPSILON = 1e-06
F32 = jnp.float32
BF16 = jnp.bfloat16
MIB = 1 << 20


def dot(a, b, dims=((1,), (0,))):
    return lax.dot_general(a, b, (dims, ((), ())), preferred_element_type=F32)


def split(a):
    high = a.astype(BF16)
    return high, (a - high.astype(F32)).astype(BF16)


def dot3(a, b, dims=((1,), (0,))):
    return dot(a[0], b[0], dims) + (dot(a[0], b[1], dims) + dot(a[1], b[0], dims))


def iota(shape, dim):
    return lax.broadcasted_iota(jnp.int32, shape, dim)


def rows_at(block, size):
    return pl.ds(pl.multiple_of(block * size, size), size)


def mixer_kernel(heads, place_ref, x0, x1, x2, x3, gain_ref, wq_ref, wk_ref, wv_ref, wb_ref, head_gain_ref,
                 wo_ref, o0, o1, o2, o3, normed, keys, beta_keys, rhs, queries, reduced, state_map, added, out_add, mixed):
    me = place_ref[0]
    xs = (x0, x1, x2, x3)
    count = len(xs)
    length, part = x0.shape
    sources = [lax.rem(me - k + count, count) for k in range(count)]
    total = 0.0
    for x in xs:
        wide = x[...].astype(F32)
        total = total + jnp.sum(wide * wide, -1, keepdims=True)
    scale = lax.rsqrt(total / (count * part) + EPSILON)
    for k in range(count):
        gain = gain_ref[pl.ds(sources[k], 1), :]
        normed[k] = (xs[k][...].astype(F32) * scale * gain).astype(BF16)

    def project(weight):
        return sum(dot(normed[k], weight(rows_at(sources[k], part))) for k in range(count))

    beta = sum(
        dot(normed[k], wb_ref[:, rows_at(sources[k], part)], ((1,), (1,))) for k in range(count)
    )
    beta = 2.0 / (1.0 + jnp.exp(-beta))
    blocks = length // CH
    query = project(lambda r: wq_ref[r, :])
    for h in range(heads):
        q = query[:, h * DK:(h + 1) * DK]
        q = q * lax.rsqrt(jnp.sum(q * q, -1, keepdims=True) + EPSILON) * DK ** (-0.5)
        queries[h] = q.reshape(blocks, CH, DK)
    for m in range(NH):
        key = project(lambda r: wk_ref[m, r, :])
        value = project(lambda r: wv_ref[m, r, :])
        for h in range(heads):
            b = beta[:, h * NH + m:h * NH + m + 1]
            k = key[:, h * DK:(h + 1) * DK]
            k = k * lax.rsqrt(jnp.sum(k * k, -1, keepdims=True) + EPSILON)
            keys[h, :, m * CH:(m + 1) * CH, :] = k.reshape(blocks, CH, DK)
            rhs[h, :, m * CH:(m + 1) * CH, :DK] = (k * b).astype(BF16).reshape(blocks, CH, DK)
            rhs[h, :, m * CH:(m + 1) * CH, DK:] = (value[:, h * DK:(h + 1) * DK] * b).astype(BF16).reshape(blocks, CH, DK)
            beta_keys[h, :, m * CH:(m + 1) * CH, :] = jnp.broadcast_to(b, (length, DK)).reshape(blocks, CH, DK)

    row, col = iota((SUB, SUB), 0), iota((SUB, SUB), 1)
    row_t, col_t = row % CH, col % CH
    causal = (col_t < row_t) | ((col_t == row_t) & (col < row))
    same = [row_t // s == col_t // s for s in (BASE, BASE * 2, BASE * 4, BASE * 8)]
    eye = (row == col).astype(F32)
    seen = iota((CH, SUB), 1) % CH <= iota((CH, SUB), 0)

    unroll = UNROLL
    for start in range(0, blocks, unroll):
        at = [(h, c) for c in range(start, start + unroll) for h in range(heads)]
        ks = [split(keys[i]) for i in at]
        lower = [
            jnp.where(causal, dot3(k, k, ((1,), (1,))) * beta_keys[i][:, :SUB], 0.0) for i, k in zip(at, ks)
        ]
        power = [jnp.where(same[0], -l, 0.0) for l in lower]
        inverse = [eye + p for p in power]
        span = 2
        while span < BASE * NH:
            power = [p.astype(BF16) for p in power]
            power = [dot(p, p) for p in power]
            inverse = [t + dot(t.astype(BF16), p.astype(BF16)) for t, p in zip(inverse, power)]
            span *= 2
        for small, large in zip(same[:-1], same[1:]):
            low = [t.astype(BF16) for t in inverse]
            step = [dot(jnp.where(large & ~small, l, 0.0).astype(BF16), t) for l, t in zip(lower, low)]
            inverse = [t - dot(b, s.astype(BF16)) for t, b, s in zip(inverse, low, step)]
        high = [split(t) for t in inverse]
        error = [eye - t - dot3(split(l), s) for t, l, s in zip(inverse, lower, high)]
        inverse = [t + dot(s[0], e.astype(BF16)) for t, s, e in zip(inverse, high, error)]
        solved = [dot(t.astype(BF16), rhs[i]).astype(BF16) for i, t in zip(at, inverse)]
        change = [dot(k[0], s, ((0,), (0,))) for k, s in zip(ks, solved)]
        qs = [queries[i] for i in at]
        attend = [jnp.where(seen, dot(q.astype(BF16), k[0], ((1,), (1,))), 0.0).astype(BF16) for q, k in zip(qs, ks)]
        effect = [dot(a, s) for a, s in zip(attend, solved)]
        for i, g, q, e in zip(at, change, qs, effect):
            state_map[i + (slice(0, CH),)] = (q - e[:, :DK]).astype(BF16)
            state_map[i + (slice(CH, CH + DK),)] = g[:, :DK].astype(BF16)
            added[i] = g[:, DK:]
            out_add[i] = e[:, DK:]

    states = [jnp.zeros((DK, DK), F32) for _ in range(heads)]
    for c in range(blocks):
        for h in range(heads):
            moved = dot(state_map[h, c], states[h].astype(BF16))
            out = moved[:CH] + out_add[h, c]
            states[h] = states[h] - moved[CH:] + added[h, c]
            out = out * lax.rsqrt(jnp.mean(out * out, -1, keepdims=True) + EPSILON) * head_gain_ref[...]
            mixed[c * CH:(c + 1) * CH, h * DK:(h + 1) * DK] = out.astype(BF16)
    own = length // count
    turned = jnp.concatenate([mixed[rows_at(lax.rem(me + k, count), own), :] for k in range(count)], 0)
    result = dot(turned, wo_ref[...]).astype(BF16)
    for k, o in enumerate((o0, o1, o2, o3)):
        o[...] = result[k * own:(k + 1) * own]


UNROLL = 8


def mixer(me, xs, gain, wq, wk, wv, wb, head_gain, wo):
    length, part = xs[0].shape
    heads = wq.shape[1] // DK
    blocks = length // CH
    own = length // len(xs)
    vmem = pl.BlockSpec(memory_space=pltpu.VMEM)
    return pl.pallas_call(
        lambda *refs: mixer_kernel(heads, *refs),
        out_shape=[jax.ShapeDtypeStruct((own, wo.shape[1]), BF16)] * len(xs),
        in_specs=[pl.BlockSpec(memory_space=pltpu.SMEM)] + [vmem] * 11,
        out_specs=[vmem] * len(xs),
        scratch_shapes=[
            pltpu.VMEM((len(xs), length, part), BF16),
            pltpu.VMEM((heads, blocks, SUB, DK), F32),
            pltpu.VMEM((heads, blocks, SUB, DK), F32),
            pltpu.VMEM((heads, blocks, SUB, 2 * DK), BF16),
            pltpu.VMEM((heads, blocks, CH, DK), F32),
            pltpu.VMEM((8, DK), F32),
            pltpu.VMEM((heads, blocks, CH + DK, DK), BF16),
            pltpu.VMEM((heads, blocks, DK, DK), F32),
            pltpu.VMEM((heads, blocks, CH, DK), F32),
            pltpu.VMEM((length, heads * DK), BF16),
        ],
        compiler_params=pltpu.CompilerParams(vmem_limit_bytes=32 * MIB),
        cost_estimate=pl.CostEstimate(flops=2 * 10 ** 10, bytes_accessed=10 ** 7, transcendentals=0),
        name="mixer",
    )(me, *xs, gain, wq, wk, wv, wb, head_gain, wo)


def slots(ids_ref, experts, capacity):
    tokens = ids_ref.shape[1]
    label = iota((experts, tokens), 0)
    chosen = [(label == ids_ref[k:k + 1, :]).astype(F32) for k in range(2)]
    count = chosen[0] + chosen[1]
    before = (iota((tokens, tokens), 0) < iota((tokens, tokens), 1)).astype(BF16)
    earlier = dot(count.astype(BF16), before)
    total = experts * capacity
    spread = (iota((total, experts), 0) // capacity == iota((total, experts), 1)).astype(BF16)
    place = dot(spread, earlier.astype(BF16))
    fits = place == (iota((total, tokens), 0) % capacity).astype(F32)
    return chosen, [jnp.where(fits, dot(spread, c.astype(BF16)), 0.0) for c in chosen]


def route_kernel(place_ref, p0, p1, p2, p3, x0, x1, x2, x3, gain_ref, ids_ref, residual_ref, routed_ref, send_ref):
    me = place_ref[0]
    xs = (x0, x1, x2, x3)
    count = len(xs)
    own, part = p0.shape[0], x0.shape[1]
    for k in range(count):
        columns = rows_at(lax.rem(me - k + count, count), part)
        residual_ref[:, columns] = xs[k][rows_at(me, own), :].astype(F32)
    arrived = [p[...].astype(F32) for p in (p0, p1, p2, p3)]
    residual = residual_ref[...] + ((arrived[0] + arrived[1]) + (arrived[2] + arrived[3]))
    residual_ref[...] = residual
    mean = jnp.mean(residual * residual, -1, keepdims=True)
    routed = residual * lax.rsqrt(mean + EPSILON) * gain_ref[...]
    routed_ref[...] = routed
    _, parts = slots(ids_ref, 64, send_ref.shape[0] // 64)
    chosen = (parts[0] + parts[1]).astype(BF16)
    send_ref[...] = dot(chosen, routed.astype(BF16)).astype(BF16)


def route(me, ps, xs, gain, ids, experts, capacity):
    own, width = ps[0].shape
    vmem = pl.BlockSpec(memory_space=pltpu.VMEM)
    return pl.pallas_call(
        route_kernel,
        out_shape=[
            jax.ShapeDtypeStruct((own, width), F32),
            jax.ShapeDtypeStruct((own, width), F32),
            jax.ShapeDtypeStruct((experts * capacity, width), BF16),
        ],
        in_specs=[pl.BlockSpec(memory_space=pltpu.SMEM)] + [vmem] * 10,
        out_specs=[vmem] * 3,
        compiler_params=pltpu.CompilerParams(vmem_limit_bytes=16 * MIB),
        cost_estimate=pl.CostEstimate(flops=10 ** 9, bytes_accessed=10 ** 7, transcendentals=0),
        name="route",
    )(me, *ps, *xs, gain, ids)


def weigh_kernel(routed_ref, router_ref, ids_ref, pick_ref, leading_ref):
    experts = router_ref.shape[0]
    chosen, parts = slots(ids_ref, experts, pick_ref.shape[1] // experts)
    tokens = routed_ref.shape[0]
    for k in range(2):
        pick_ref[k * tokens:(k + 1) * tokens, :] = jnp.transpose(parts[k]).astype(BF16)
    logits = lax.dot_general(
        router_ref[...], routed_ref[...], (((1,), (1,)), ((), ())),
        precision=lax.Precision.HIGHEST, preferred_element_type=F32,
    )
    gap = jnp.sum((chosen[0] - chosen[1]) * logits, 0, keepdims=True)
    leading = 1.0 / (1.0 + jnp.exp(-gap))
    leading_ref[...] = jnp.transpose(jnp.broadcast_to(leading, (128, tokens)))


def weigh(routed, router, ids, capacity):
    tokens = routed.shape[0]
    experts = router.shape[0]
    vmem = pl.BlockSpec(memory_space=pltpu.VMEM)
    return pl.pallas_call(
        weigh_kernel,
        out_shape=[
            jax.ShapeDtypeStruct((2 * tokens, experts * capacity), BF16),
            jax.ShapeDtypeStruct((tokens, 128), F32),
        ],
        in_specs=[vmem] * 3,
        out_specs=[vmem] * 2,
        compiler_params=pltpu.CompilerParams(vmem_limit_bytes=8 * MIB),
        cost_estimate=pl.CostEstimate(flops=10 ** 9, bytes_accessed=10 ** 6, transcendentals=0),
        name="weigh",
    )(routed, router, ids)


PIECES = 4


def load_kernel(*refs):
    half = (len(refs) - 1) // 2
    sems = refs[-1]
    copies = []
    for i in range(half):
        copies.append(pltpu.make_async_copy(refs[i], refs[half + i], sems.at[i]))
        copies[-1].start()
    for copy in copies:
        copy.wait()


def load(*weights):
    return pl.pallas_call(
        load_kernel,
        out_shape=[pltpu.VMEM(w.shape, w.dtype) for w in weights],
        in_specs=[pl.BlockSpec(memory_space=pltpu.HBM)] * len(weights),
        out_specs=[pl.BlockSpec(memory_space=pltpu.VMEM)] * len(weights),
        scratch_shapes=[pltpu.SemaphoreType.DMA((len(weights),))],
        compiler_params=pltpu.CompilerParams(vmem_limit_bytes=1 * MIB),
        cost_estimate=pl.CostEstimate(flops=2 * 10 ** 9, bytes_accessed=10 ** 6, transcendentals=0),
        name="load",
    )(*[pltpu.with_memory_space_constraint(w, pltpu.HBM) for w in weights])


def expert_kernel(rows_ref, gate_hbm, up_hbm, down_hbm, out_ref, gate_ref, up_ref, down_ref, sems):
    total = rows_ref.shape[0]
    here, width, middle = gate_hbm.shape
    per = total // here
    cap = 4
    deep, tall = width // PIECES, middle // PIECES
    copies = {}
    for e in range(here):
        for part, (source, target) in enumerate(((gate_hbm, gate_ref), (up_hbm, up_ref), (down_hbm, down_ref))):
            size = tall if part == 2 else deep
            for p in range(PIECES):
                at = (e, pl.ds(p * size, size))
                copies[e, part, p] = pltpu.make_async_copy(source.at[at], target.at[at], sems.at[e, part, p])
    for e in range(here):
        for p in range(PIECES):
            copies[e, 0, p].start()
            copies[e, 1, p].start()
        for p in range(PIECES):
            copies[e, 2, p].start()
    r, c = iota((total, total), 0), iota((total, total), 1)

    def source(i):
        return (i % per) // cap * (here * cap) + i // per * cap + i % cap

    by_expert = (source(r) == c).astype(BF16)
    by_source = (source(c) == r).astype(BF16)
    rows = dot(by_expert, rows_ref[...]).astype(BF16)
    results = []
    for e in range(here):
        mine = rows[e * per:(e + 1) * per]
        gate = up = 0.0
        for p in range(PIECES):
            at = slice(p * deep, (p + 1) * deep)
            copies[e, 0, p].wait()
            gate = gate + dot(mine[:, at], gate_ref[e, at])
            copies[e, 1, p].wait()
            up = up + dot(mine[:, at], up_ref[e, at])
        hidden = (gate / (1.0 + jnp.exp(-gate)) * up).astype(BF16)
        for p in range(PIECES):
            copies[e, 2, p].wait()
        results.append(dot(hidden, down_ref[e]).astype(BF16))
    out_ref[...] = dot(by_source, jnp.concatenate(results, 0)).astype(BF16)


def experts_here(rows, gate, up, down):
    vmem = pl.BlockSpec(memory_space=pltpu.VMEM)
    hbm = pl.BlockSpec(memory_space=pltpu.HBM)
    return pl.pallas_call(
        expert_kernel,
        out_shape=jax.ShapeDtypeStruct(rows.shape, BF16),
        in_specs=[vmem] + [hbm] * 3,
        out_specs=vmem,
        scratch_shapes=[
            pltpu.VMEM(gate.shape, BF16),
            pltpu.VMEM(up.shape, BF16),
            pltpu.VMEM(down.shape, BF16),
            pltpu.SemaphoreType.DMA((gate.shape[0], 3, PIECES)),
        ],
        compiler_params=pltpu.CompilerParams(vmem_limit_bytes=56 * MIB),
        cost_estimate=pl.CostEstimate(flops=5 * 10 ** 9, bytes_accessed=10 ** 7, transcendentals=0),
        name="experts",
    )(rows, *[pltpu.with_memory_space_constraint(w, pltpu.HBM) for w in (gate, up, down)])


def combine_kernel(residual_ref, leading_ref, pick_ref, back_ref, out_ref):
    tokens = residual_ref.shape[0]
    picked = dot(pick_ref[...], back_ref[...])
    leading = leading_ref[:, 0:1]
    blended = leading * picked[:tokens] + (1.0 - leading) * picked[tokens:]
    out_ref[...] = (residual_ref[...] + blended).astype(BF16)


def combine(residual, leading, pick, back):
    vmem = pl.BlockSpec(memory_space=pltpu.VMEM)
    return pl.pallas_call(
        combine_kernel,
        out_shape=jax.ShapeDtypeStruct(residual.shape, BF16),
        in_specs=[vmem] * 4,
        out_specs=vmem,
        compiler_params=pltpu.CompilerParams(vmem_limit_bytes=16 * MIB),
        cost_estimate=pl.CostEstimate(flops=10 ** 9, bytes_accessed=10 ** 6, transcendentals=0),
        name="combine",
    )(residual, leading, pick, back)


def turned(x, k, axis):
    size = lax.axis_size(axis)
    return lax.ppermute(x, axis, [(i, (i + k) % size) for i in range(size)])


def shards(tokens, mixer_gain, query_weight, key_weight, value_weight, beta_weight, head_gain, output_weight,
           expert_gain, router_weight, expert_ids, gate_weight, up_weight, down_weight):
    peers = lax.axis_size("head")
    owners = lax.axis_size("dp")
    me = lax.axis_index("head").reshape(1).astype(jnp.int32)
    xs = [tokens] + [turned(tokens, k, "head") for k in range(1, peers)]
    here = load(tokens, query_weight, key_weight, value_weight, beta_weight.T, head_gain.reshape(1, -1), output_weight)
    xs[0] = here[0]
    parts = mixer(me, xs, mixer_gain.reshape(peers, -1), *here[1:])
    parts = [parts[0]] + [turned(parts[k], k, "head") for k in range(1, peers)]
    experts = router_weight.shape[1]
    own = parts[0].shape[0]
    capacity = 4 * own // experts
    ids = expert_ids.T
    residual, routed, outgoing = route(me, parts, xs, expert_gain.reshape(1, -1), ids, experts, capacity)
    width = outgoing.shape[1]
    outgoing = outgoing.reshape(owners, -1, width)
    arrived = lax.all_to_all(outgoing, "dp", split_axis=0, concat_axis=0, tiled=True)
    pick, leading = weigh(routed, router_weight.T, ids, capacity)
    result = experts_here(arrived.reshape(-1, width), gate_weight, up_weight, down_weight)
    back = lax.all_to_all(result.reshape(owners, -1, width), "dp", split_axis=0, concat_axis=0, tiled=True)
    return combine(residual, leading, pick, back.reshape(-1, width))


def solution(mesh):
    return jax.shard_map(
        shards,
        mesh=mesh,
        in_specs=(
            P("dp", "head"),
            P(),
            P(None, "head"),
            P(None, None, "head"),
            P(None, None, "head"),
            P(None, "head"),
            P(),
            P("head", None),
            P(),
            P(),
            P(("dp", "head"), None),
            P("dp", None, None),
            P("dp", None, None),
            P("dp", None, None),
        ),
        out_specs=P(("dp", "head"), None),
        check_vma=False,
    )
```

profile of v0, /device:TPU:1, one launch (start us, length us, event | category | flops | bytes accessed | tf_op | source)
XLA Modules:
  0.0 103.5 jit_solution(6483883187966213743)
XLA Ops:
  0.0 2.5 %collective-permute-start = (bf16[256,512]{1,0:T(8,128)(2,1)}, bf16[256,512]{1,0:T(8,128)(2,1)S(1)}, u32[]{:S(2)}, u32[]{:S(2)}) collective-permute-start(bf16[256,512]{1,0:T(8,128)(2,1)} %refs_0_.1), channel_id=1, source_target_pairs={{0,1},{1,2},{2,3},{3,0},{4,5},{5,6},{6,7},{7,4},{8,9},{9,10},{10,1... | collective-permute-start | bytes 786440 | tf_op jit(solution)/shard_map/ppermute | solution.py:366
  2.5 2.1 %collective-permute-start.2 = (bf16[256,512]{1,0:T(8,128)(2,1)}, bf16[256,512]{1,0:T(8,128)(2,1)S(1)}, u32[]{:S(2)}, u32[]{:S(2)}) collective-permute-start(bf16[256,512]{1,0:T(8,128)(2,1)} %refs_0_.1), channel_id=1, source_target_pairs={{0,3},{1,0},{2,1},{3,2},{4,7},{5,4},{6,5},{7,6},{8,11},{9,8},{10,9... | collective-permute-start | bytes 786440 | tf_op jit(solution)/shard_map/ppermute | solution.py:366
  4.6 1.3 %collective-permute-start.1 = (bf16[256,512]{1,0:T(8,128)(2,1)}, bf16[256,512]{1,0:T(8,128)(2,1)S(1)}, u32[]{:S(2)}, u32[]{:S(2)}) collective-permute-start(bf16[256,512]{1,0:T(8,128)(2,1)} %refs_0_.1), channel_id=1, source_target_pairs={{0,2},{1,3},{2,0},{3,1},{4,6},{5,7},{6,4},{7,5},{8,10},{9,11},{10,... | collective-permute-start | bytes 786440 | tf_op jit(solution)/shard_map/ppermute | solution.py:366
  5.9 0.7 reshape.26.refs_5_
  6.6 3.6 %load.1 = (bf16[256,512]{1,0:T(8,128)(2,1)S(1)}, bf16[2048,256]{1,0:T(8,128)(2,1)S(1)}, bf16[3,2048,256]{2,1,0:T(8,128)(2,1)S(1)}, bf16[3,2048,256]{2,1,0:T(8,12...) custom-call(bf16[256,512]{1,0:T(8,128)(2,1)} %refs_0_.1, ...), custom_call_target="tpu_custom_call" | custom-call | flops 2000000000 | bytes 1000000 | tf_op jit(solution)/shard_map/load/pallas_call | solution.py:267
  10.2 0.6 collective-permute-done.refs_2_.x1
  10.8 0.0 collective-permute-done.2.refs_4_.x3
  10.8 6.5 %collective-permute-done.1.refs_3_.x2 = bf16[256,512]{1,0:T(8,128)(2,1)S(1)} collective-permute-done((bf16[256,512]{1,0:T(8,128)(2,1)}, bf16[256,512]{1,0:T(8,128)(2,1)S(1)}, u32[]{:S(2)}, u32[]{:S(2)}) %collective-permute-start.1) | collective-permute-done | bytes 262176 | tf_op jit(solution)/shard_map/ppermute | solution.py:366
  17.3 0.0 copy-start.1
  17.3 0.0 copy-start.2
  17.3 8.2 %mixer.1 = (bf16[64,2048]{1,0:T(8,128)(2,1)S(1)}, bf16[64,2048]{1,0:T(8,128)(2,1)S(1)}, bf16[64,2048]{1,0:T(8,128)(2,1)S(1)}, bf16[64,2048]{1,0:T(8,128)(2,1)S(1)}) custom-call(s32[1]{0:T(128)} %bitcast.refs_0_.place_ref, bf16[256,512]{1,0:T(8,128)(2,1)S(1)} %get-tuple-element.21.refs_1_.x0, bf16[256,512]{1,0:T(8,128)(2,1)S(1)} %collective-permute-done.refs_2_.x1, ...), custom_call_target="tpu_custom_call" | custom-call | flops 20000000000 | bytes 10000000 | tf_op jit(solution)/shard_map/mixer/pallas_call | solution.py:145
  25.5 0.7 collective-permute-start.3
  26.2 1.3 %collective-permute-start.4 = (bf16[64,2048]{1,0:T(8,128)(2,1)S(1)}, bf16[64,2048]{1,0:T(8,128)(2,1)S(1)}, u32[]{:S(2)}, u32[]{:S(2)}) collective-permute-start(bf16[64,2048]{1,0:T(8,128)(2,1)S(1)} %get-tuple-element.30), channel_id=1, source_target_pairs={{0,2},{1,3},{2,0},{3,1},{4,6},{5,7},{6,4},{7,5},{8,10},{9,11},{10,... | collective-permute-start | bytes 786440 | tf_op jit(solution)/shard_map/ppermute | solution.py:366
  27.5 1.2 %collective-permute-start.5 = (bf16[64,2048]{1,0:T(8,128)(2,1)S(1)}, bf16[64,2048]{1,0:T(8,128)(2,1)S(1)}, u32[]{:S(2)}, u32[]{:S(2)}) collective-permute-start(bf16[64,2048]{1,0:T(8,128)(2,1)S(1)} %get-tuple-element.31), channel_id=1, source_target_pairs={{0,3},{1,0},{2,1},{3,2},{4,7},{5,4},{6,5},{7,6},{8,11},{9,8},{10,9... | collective-permute-start | bytes 786440 | tf_op jit(solution)/shard_map/ppermute | solution.py:366
  28.7 6.0 %collective-permute-done.3.p1 = bf16[64,2048]{1,0:T(8,128)(2,1)S(1)} collective-permute-done((bf16[64,2048]{1,0:T(8,128)(2,1)S(1)}, bf16[64,2048]{1,0:T(8,128)(2,1)S(1)}, u32[]{:S(2)}, u32[]{:S(2)}) %collective-permute-start.3) | collective-permute-done | bytes 262176 | tf_op jit(solution)/shard_map/ppermute | solution.py:366
  34.6 2.6 %collective-permute-done.4.p2 = bf16[64,2048]{1,0:T(8,128)(2,1)S(1)} collective-permute-done((bf16[64,2048]{1,0:T(8,128)(2,1)S(1)}, bf16[64,2048]{1,0:T(8,128)(2,1)S(1)}, u32[]{:S(2)}, u32[]{:S(2)}) %collective-permute-start.4) | collective-permute-done | bytes 262176 | tf_op jit(solution)/shard_map/ppermute | solution.py:366
  37.2 3.0 %collective-permute-done.5.p3 = bf16[64,2048]{1,0:T(8,128)(2,1)S(1)} collective-permute-done((bf16[64,2048]{1,0:T(8,128)(2,1)S(1)}, bf16[64,2048]{1,0:T(8,128)(2,1)S(1)}, u32[]{:S(2)}, u32[]{:S(2)}) %collective-permute-start.5) | collective-permute-done | bytes 262176 | tf_op jit(solution)/shard_map/ppermute | solution.py:366
  40.2 0.0 copy-done.1
  40.2 0.0 copy-done.2
  40.2 0.8 route.1
  41.1 25.6 %all_to_all.10 = bf16[32,8,2048]{2,1,0:T(8,128)(2,1)} all-to-all(bf16[32,8,2048]{2,1,0:T(8,128)(2,1)S(1)} %bitcast.11), channel_id=1, replica_groups=mesh['dp'=32,'head'=4] {'dp'}, dimensions={0} | all-to-all | bytes 2097152 | tf_op jit(solution)/shard_map/all_to_all | solution.py:386
  66.7 0.0 copy-start
  66.7 14.7 %experts.1 = bf16[256,2048]{1,0:T(8,128)(2,1)} custom-call(bf16[256,2048]{1,0:T(8,128)(2,1)} %bitcast.17, bf16[2,2048,1408]{2,1,0:T(8,128)(2,1)} %gate_hbm.1, bf16[2,2048,1408]{2,1,0:T(8,128)(2,1)} %up_hbm.1, bf16[2,1408,2048]{2,1,0:T(8,128)(2,1)} %down_hbm.1), custom_call_target="tpu_custom_call" | custom-call | flops 5000000000 | bytes 10000000 | tf_op jit(solution)/shard_map/experts/pallas_call | solution.py:326
  81.3 4.0 %all-to-all-start.1 = ((bf16[32,8,2048]{2,1,0:T(8,128)(2,1)}), bf16[32,8,2048]{2,1,0:T(8,128)(2,1)S(1)}, u32[]{:S(2)}, u32[]{:S(2)}) async-start(bf16[32,8,2048]{2,1,0:T(8,128)(2,1)} %bitcast.16), calls=%async_computation.1 | async-start | bytes 2097152 | tf_op jit(solution)/shard_map/all_to_all | solution.py:389
  85.3 0.0 copy-done
  85.4 0.8 weigh.1
  86.2 16.3 %all-to-all-done.1 = bf16[32,8,2048]{2,1,0:T(8,128)(2,1)S(1)} async-done(((bf16[32,8,2048]{2,1,0:T(8,128)(2,1)}), bf16[32,8,2048]{2,1,0:T(8,128)(2,1)S(1)}, u32[]{:S(2)}, u32[]{:S(2)}) %all-to-all-start.1) | async-done | bytes 1048608 | tf_op jit(solution)/shard_map/all_to_all | solution.py:389
  102.5 1.0 combine.1
Async XLA Ops:
  0.0 10.8 %collective-permute-start = (bf16[256,512]{1,0:T(8,128)(2,1)}, bf16[256,512]{1,0:T(8,128)(2,1)S(1)}, u32[]{:S(2)}, u32[]{:S(2)}) collective-permute-start(bf16[256,512]{1,0:T(8,128)(2,1)} %refs_0_.1), channel_id=1, source_target_pairs={{0,1},{1,2},{2,3},{3,0},{4,5},{5,6},{6,7},{7,4},{8,9},{9,10},{10,1... | collective-permute-start | bytes 786440 | tf_op jit(solution)/shard_map/ppermute | solution.py:366
  2.5 8.3 %collective-permute-start.2 = (bf16[256,512]{1,0:T(8,128)(2,1)}, bf16[256,512]{1,0:T(8,128)(2,1)S(1)}, u32[]{:S(2)}, u32[]{:S(2)}) collective-permute-start(bf16[256,512]{1,0:T(8,128)(2,1)} %refs_0_.1), channel_id=1, source_target_pairs={{0,3},{1,0},{2,1},{3,2},{4,7},{5,4},{6,5},{7,6},{8,11},{9,8},{10,9... | collective-permute-start | bytes 786440 | tf_op jit(solution)/shard_map/ppermute | solution.py:366
  4.6 12.7 %collective-permute-start.1 = (bf16[256,512]{1,0:T(8,128)(2,1)}, bf16[256,512]{1,0:T(8,128)(2,1)S(1)}, u32[]{:S(2)}, u32[]{:S(2)}) collective-permute-start(bf16[256,512]{1,0:T(8,128)(2,1)} %refs_0_.1), channel_id=1, source_target_pairs={{0,2},{1,3},{2,0},{3,1},{4,6},{5,7},{6,4},{7,5},{8,10},{9,11},{10,... | collective-permute-start | bytes 786440 | tf_op jit(solution)/shard_map/ppermute | solution.py:366
  17.3 22.9 %copy-start.1 = (f32[2048]{0:T(1024)S(1)}, f32[2048]{0:T(1024)}, u32[]{:S(2)}) copy-start(f32[2048]{0:T(1024)} %param.22) | copy-start | bytes 24580
  17.3 22.9 %copy-start.2 = (s32[64,2]{0,1:T(2,128)S(1)}, s32[64,2]{0,1:T(2,128)}, u32[]{:S(2)}) copy-start(s32[64,2]{0,1:T(2,128)} %param.24) | copy-start | bytes 1540
  25.5 9.1 %collective-permute-start.3 = (bf16[64,2048]{1,0:T(8,128)(2,1)S(1)}, bf16[64,2048]{1,0:T(8,128)(2,1)S(1)}, u32[]{:S(2)}, u32[]{:S(2)}) collective-permute-start(bf16[64,2048]{1,0:T(8,128)(2,1)S(1)} %get-tuple-element.29), channel_id=1, source_target_pairs={{0,1},{1,2},{2,3},{3,0},{4,5},{5,6},{6,7},{7,4},{8,9},{9,10},{10,1... | collective-permute-start | bytes 786440 | tf_op jit(solution)/shard_map/ppermute | solution.py:366
  26.2 11.0 %collective-permute-start.4 = (bf16[64,2048]{1,0:T(8,128)(2,1)S(1)}, bf16[64,2048]{1,0:T(8,128)(2,1)S(1)}, u32[]{:S(2)}, u32[]{:S(2)}) collective-permute-start(bf16[64,2048]{1,0:T(8,128)(2,1)S(1)} %get-tuple-element.30), channel_id=1, source_target_pairs={{0,2},{1,3},{2,0},{3,1},{4,6},{5,7},{6,4},{7,5},{8,10},{9,11},{10,... | collective-permute-start | bytes 786440 | tf_op jit(solution)/shard_map/ppermute | solution.py:366
  27.5 12.7 %collective-permute-start.5 = (bf16[64,2048]{1,0:T(8,128)(2,1)S(1)}, bf16[64,2048]{1,0:T(8,128)(2,1)S(1)}, u32[]{:S(2)}, u32[]{:S(2)}) collective-permute-start(bf16[64,2048]{1,0:T(8,128)(2,1)S(1)} %get-tuple-element.31), channel_id=1, source_target_pairs={{0,3},{1,0},{2,1},{3,2},{4,7},{5,4},{6,5},{7,6},{8,11},{9,8},{10,9... | collective-permute-start | bytes 786440 | tf_op jit(solution)/shard_map/ppermute | solution.py:366
  66.7 18.7 %copy-start = (f32[2048,64]{0,1:T(8,128)S(1)}, f32[2048,64]{0,1:T(8,128)}, u32[]{:S(2)}) copy-start(f32[2048,64]{0,1:T(8,128)} %param.23) | copy-start | bytes 1572868
  81.3 21.2 %all-to-all-start.1 = ((bf16[32,8,2048]{2,1,0:T(8,128)(2,1)}), bf16[32,8,2048]{2,1,0:T(8,128)(2,1)S(1)}, u32[]{:S(2)}, u32[]{:S(2)}) async-start(bf16[32,8,2048]{2,1,0:T(8,128)(2,1)} %bitcast.16), calls=%async_computation.1 | async-start | bytes 2097152 | tf_op jit(solution)/shard_map/all_to_all | solution.py:389
where the time goes:
time: 104 us
  waiting for transfers between devices  35 us (34%)
  Pallas kernels  29.1 us (28%)
  blocking collectives  25.6 us (25%)
  starting transfers between devices  13 us (12%)
    all_to_all x1, blocking collectives, shards(): lax.all_to_all(outgoing, 'dp', split_axis=0, concat_axis=0, tiled=True)  25.6 us
    ppermute x6, waiting for transfers between devices, turned(): return lax.ppermute(x, axis, [(i, (i + k) % size) for i in range(size)])  18.7 us
    all_to_all x1, waiting for transfers between devices, shards(): lax.all_to_all(result.reshape(owners, -1, width), 'dp', split_axis=0, con...  16.3 us
    pallas_call x1, Pallas kernels, experts_here(): pl.pallas_call(expert_kernel, out_shape=jax.ShapeDtypeStruct(rows.shape,...  14.7 us
    ppermute x6, starting transfers between devices, turned(): return lax.ppermute(x, axis, [(i, (i + k) % size) for i in range(size)])  9.02 us
    pallas_call x1, Pallas kernels, mixer(): pl.pallas_call(lambda *refs: mixer_kernel(heads, *refs), out_shape=[jax.S...  8.2 us
    all_to_all x1, starting transfers between devices, shards(): lax.all_to_all(result.reshape(owners, -1, width), 'dp', split_axis=0, con...  3.99 us
    pallas_call x1, Pallas kernels, load(): pl.pallas_call(load_kernel, out_shape=[pltpu.VMEM(w.shape, w.dtype) for w...  3.57 us
  transfers between devices with their start and end apart: 7, of which 6 were waited for; matrix products, arithmetic and copies ran while one was open for 1% of the time, Pallas kernels for 4%

commit v1 on v0

--- a/solution.py
+++ b/solution.py
@@ -38,7 +38,7 @@
 
 
 def mixer_kernel(heads, place_ref, x0, x1, x2, x3, gain_ref, wq_ref, wk_ref, wv_ref, wb_ref, head_gain_ref,
-                 wo_ref, o0, o1, o2, o3, normed, keys, beta_keys, rhs, queries, reduced, state_map, added, out_add, mixed):
+                 wo_ref, out_ref, normed, keys, beta_keys, rhs, queries, reduced, state_map, added, out_add, mixed):
     me = place_ref[0]
     xs = (x0, x1, x2, x3)
     count = len(xs)
@@ -126,11 +126,7 @@
             states[h] = states[h] - moved[CH:] + added[h, c]
             out = out * lax.rsqrt(jnp.mean(out * out, -1, keepdims=True) + EPSILON) * head_gain_ref[...]
             mixed[c * CH:(c + 1) * CH, h * DK:(h + 1) * DK] = out.astype(BF16)
-    own = length // count
-    turned = jnp.concatenate([mixed[rows_at(lax.rem(me + k, count), own), :] for k in range(count)], 0)
-    result = dot(turned, wo_ref[...]).astype(BF16)
-    for k, o in enumerate((o0, o1, o2, o3)):
-        o[...] = result[k * own:(k + 1) * own]
+    out_ref[...] = dot(mixed[...], wo_ref[...]).astype(BF16)
 
 
 UNROLL = 8
@@ -140,13 +136,12 @@
     length, part = xs[0].shape
     heads = wq.shape[1] // DK
     blocks = length // CH
-    own = length // len(xs)
     vmem = pl.BlockSpec(memory_space=pltpu.VMEM)
     return pl.pallas_call(
         lambda *refs: mixer_kernel(heads, *refs),
-        out_shape=[jax.ShapeDtypeStruct((own, wo.shape[1]), BF16)] * len(xs),
+        out_shape=jax.ShapeDtypeStruct((length, wo.shape[1]), BF16),
         in_specs=[pl.BlockSpec(memory_space=pltpu.SMEM)] + [vmem] * 11,
-        out_specs=[vmem] * len(xs),
+        out_specs=vmem,
         scratch_shapes=[
             pltpu.VMEM((len(xs), length, part), BF16),
             pltpu.VMEM((heads, blocks, SUB, DK), F32),
@@ -179,27 +174,27 @@
     return chosen, [jnp.where(fits, dot(spread, c.astype(BF16)), 0.0) for c in chosen]
 
 
-def route_kernel(place_ref, p0, p1, p2, p3, x0, x1, x2, x3, gain_ref, ids_ref, residual_ref, routed_ref, send_ref):
+def route_kernel(place_ref, parts_ref, x0, x1, x2, x3, gain_ref, ids_ref, residual_ref, routed_ref, send_ref):
     me = place_ref[0]
     xs = (x0, x1, x2, x3)
     count = len(xs)
-    own, part = p0.shape[0], x0.shape[1]
+    own, part = parts_ref.shape[1], x0.shape[1]
     for k in range(count):
         columns = rows_at(lax.rem(me - k + count, count), part)
         residual_ref[:, columns] = xs[k][rows_at(me, own), :].astype(F32)
-    arrived = [p[...].astype(F32) for p in (p0, p1, p2, p3)]
+    arrived = [parts_ref[k].astype(F32) for k in range(count)]
     residual = residual_ref[...] + ((arrived[0] + arrived[1]) + (arrived[2] + arrived[3]))
     residual_ref[...] = residual
     mean = jnp.mean(residual * residual, -1, keepdims=True)
     routed = residual * lax.rsqrt(mean + EPSILON) * gain_ref[...]
     routed_ref[...] = routed
-    _, parts = slots(ids_ref, 64, send_ref.shape[0] // 64)
-    chosen = (parts[0] + parts[1]).astype(BF16)
+    _, chosen = slots(ids_ref, 64, send_ref.shape[0] // 64)
+    chosen = (chosen[0] + chosen[1]).astype(BF16)
     send_ref[...] = dot(chosen, routed.astype(BF16)).astype(BF16)
 
 
-def route(me, ps, xs, gain, ids, experts, capacity):
-    own, width = ps[0].shape
+def route(me, parts, xs, gain, ids, experts, capacity):
+    _, own, width = parts.shape
     vmem = pl.BlockSpec(memory_space=pltpu.VMEM)
     return pl.pallas_call(
         route_kernel,
@@ -208,15 +203,15 @@
             jax.ShapeDtypeStruct((own, width), F32),
             jax.ShapeDtypeStruct((experts * capacity, width), BF16),
         ],
-        in_specs=[pl.BlockSpec(memory_space=pltpu.SMEM)] + [vmem] * 10,
+        in_specs=[pl.BlockSpec(memory_space=pltpu.SMEM)] + [vmem] * 7,
         out_specs=[vmem] * 3,
         compiler_params=pltpu.CompilerParams(vmem_limit_bytes=16 * MIB),
         cost_estimate=pl.CostEstimate(flops=10 ** 9, bytes_accessed=10 ** 7, transcendentals=0),
         name="route",
-    )(me, *ps, *xs, gain, ids)
-
-
-def weigh_kernel(routed_ref, router_ref, ids_ref, pick_ref, leading_ref):
+    )(me, parts, *xs, gain, ids)
+
+
+def weigh(routed_ref, router_ref, ids_ref, pick_ref, leading_ref):
     experts = router_ref.shape[0]
     chosen, parts = slots(ids_ref, experts, pick_ref.shape[1] // experts)
     tokens = routed_ref.shape[0]
@@ -231,27 +226,6 @@
     leading_ref[...] = jnp.transpose(jnp.broadcast_to(leading, (128, tokens)))
 
 
-def weigh(routed, router, ids, capacity):
-    tokens = routed.shape[0]
-    experts = router.shape[0]
-    vmem = pl.BlockSpec(memory_space=pltpu.VMEM)
-    return pl.pallas_call(
-        weigh_kernel,
-        out_shape=[
-            jax.ShapeDtypeStruct((2 * tokens, experts * capacity), BF16),
-            jax.ShapeDtypeStruct((tokens, 128), F32),
-        ],
-        in_specs=[vmem] * 3,
-        out_specs=[vmem] * 2,
-        compiler_params=pltpu.CompilerParams(vmem_limit_bytes=8 * MIB),
-        cost_estimate=pl.CostEstimate(flops=10 ** 9, bytes_accessed=10 ** 6, transcendentals=0),
-        name="weigh",
-    )(routed, router, ids)
-
-
-PIECES = 4
-
-
 def load_kernel(*refs):
     half = (len(refs) - 1) // 2
     sems = refs[-1]
@@ -276,25 +250,34 @@
     )(*[pltpu.with_memory_space_constraint(w, pltpu.HBM) for w in weights])
 
 
-def expert_kernel(rows_ref, gate_hbm, up_hbm, down_hbm, out_ref, gate_ref, up_ref, down_ref, sems):
+def expert_kernel(rows_ref, gate_hbm, up_hbm, down_hbm, routed_ref, router_ref, ids_ref, out_ref, pick_ref, leading_ref,
+                  gate_ref, up_ref, down_ref, hidden_ref, finished_ref, sems):
     total = rows_ref.shape[0]
     here, width, middle = gate_hbm.shape
     per = total // here
-    cap = 4
+    experts = router_ref.shape[0]
+    cap = pick_ref.shape[1] // experts
     deep, tall = width // PIECES, middle // PIECES
-    copies = {}
+    copies, order = {}, []
     for e in range(here):
         for part, (source, target) in enumerate(((gate_hbm, gate_ref), (up_hbm, up_ref), (down_hbm, down_ref))):
             size = tall if part == 2 else deep
             for p in range(PIECES):
                 at = (e, pl.ds(p * size, size))
                 copies[e, part, p] = pltpu.make_async_copy(source.at[at], target.at[at], sems.at[e, part, p])
-    for e in range(here):
         for p in range(PIECES):
-            copies[e, 0, p].start()
-            copies[e, 1, p].start()
-        for p in range(PIECES):
-            copies[e, 2, p].start()
+            order += [(e, 0, p), (e, 1, p)]
+        order += [(e, 2, p) for p in range(PIECES)]
+    for key in order[:FLIGHT]:
+        copies[key].start()
+
+    def take(*key):
+        copies[key].wait()
+        following = order.index(key) + FLIGHT
+        if following < len(order):
+            copies[order[following]].start()
+
+    weigh(routed_ref, router_ref, ids_ref, pick_ref, leading_ref)
     r, c = iota((total, total), 0), iota((total, total), 1)
 
     def source(i):
@@ -303,41 +286,59 @@
     by_expert = (source(r) == c).astype(BF16)
     by_source = (source(c) == r).astype(BF16)
     rows = dot(by_expert, rows_ref[...]).astype(BF16)
-    results = []
     for e in range(here):
         mine = rows[e * per:(e + 1) * per]
         gate = up = 0.0
         for p in range(PIECES):
             at = slice(p * deep, (p + 1) * deep)
-            copies[e, 0, p].wait()
+            take(e, 0, p)
             gate = gate + dot(mine[:, at], gate_ref[e, at])
-            copies[e, 1, p].wait()
+            take(e, 1, p)
             up = up + dot(mine[:, at], up_ref[e, at])
-        hidden = (gate / (1.0 + jnp.exp(-gate)) * up).astype(BF16)
+        hidden_ref[...] = (gate / (1.0 + jnp.exp(-gate)) * up).astype(BF16)
+        result = 0.0
         for p in range(PIECES):
-            copies[e, 2, p].wait()
-        results.append(dot(hidden, down_ref[e]).astype(BF16))
-    out_ref[...] = dot(by_source, jnp.concatenate(results, 0)).astype(BF16)
-
-
-def experts_here(rows, gate, up, down):
+            take(e, 2, p)
+            at = slice(p * tall, (p + 1) * tall)
+            result = result + dot(hidden_ref[:, at], down_ref[e, at])
+        finished_ref[e * per:(e + 1) * per, :] = result.astype(BF16)
+    for start in range(0, width, 512):
+        at = slice(start, start + 512)
+        out_ref[:, at] = dot(by_source, finished_ref[:, at]).astype(BF16)
+
+
+PIECES = 4
+FLIGHT = 10
+
+
+def experts_here(rows, gate, up, down, routed, router, ids):
+    here, width, middle = gate.shape
+    per = rows.shape[0] // here
+    tokens, experts = routed.shape[0], router.shape[0]
+    capacity = 4 * tokens // experts
     vmem = pl.BlockSpec(memory_space=pltpu.VMEM)
     hbm = pl.BlockSpec(memory_space=pltpu.HBM)
     return pl.pallas_call(
         expert_kernel,
-        out_shape=jax.ShapeDtypeStruct(rows.shape, BF16),
-        in_specs=[vmem] + [hbm] * 3,
-        out_specs=vmem,
+        out_shape=[
+            jax.ShapeDtypeStruct(rows.shape, BF16),
+            jax.ShapeDtypeStruct((2 * tokens, experts * capacity), BF16),
+            jax.ShapeDtypeStruct((tokens, 128), F32),
+        ],
+        in_specs=[vmem] + [hbm] * 3 + [vmem] * 3,
+        out_specs=[vmem] * 3,
         scratch_shapes=[
             pltpu.VMEM(gate.shape, BF16),
             pltpu.VMEM(up.shape, BF16),
             pltpu.VMEM(down.shape, BF16),
-            pltpu.SemaphoreType.DMA((gate.shape[0], 3, PIECES)),
+            pltpu.VMEM((per, middle), BF16),
+            pltpu.VMEM(rows.shape, BF16),
+            pltpu.SemaphoreType.DMA((here, 3, PIECES)),
         ],
-        compiler_params=pltpu.CompilerParams(vmem_limit_bytes=56 * MIB),
+        compiler_params=pltpu.CompilerParams(vmem_limit_bytes=46 * MIB),
         cost_estimate=pl.CostEstimate(flops=5 * 10 ** 9, bytes_accessed=10 ** 7, transcendentals=0),
         name="experts",
-    )(rows, *[pltpu.with_memory_space_constraint(w, pltpu.HBM) for w in (gate, up, down)])
+    )(rows, *[pltpu.with_memory_space_constraint(w, pltpu.HBM) for w in (gate, up, down)], routed, router, ids)
 
 
 def combine_kernel(residual_ref, leading_ref, pick_ref, back_ref, out_ref):
@@ -375,17 +376,19 @@
     here = load(tokens, query_weight, key_weight, value_weight, beta_weight.T, head_gain.reshape(1, -1), output_weight)
     xs[0] = here[0]
     parts = mixer(me, xs, mixer_gain.reshape(peers, -1), *here[1:])
-    parts = [parts[0]] + [turned(parts[k], k, "head") for k in range(1, peers)]
+    parts = parts.reshape(peers, -1, parts.shape[1])
+    parts = lax.all_to_all(parts, "head", split_axis=0, concat_axis=0, tiled=True)
     experts = router_weight.shape[1]
-    own = parts[0].shape[0]
+    own = parts.shape[1]
     capacity = 4 * own // experts
     ids = expert_ids.T
     residual, routed, outgoing = route(me, parts, xs, expert_gain.reshape(1, -1), ids, experts, capacity)
     width = outgoing.shape[1]
     outgoing = outgoing.reshape(owners, -1, width)
     arrived = lax.all_to_all(outgoing, "dp", split_axis=0, concat_axis=0, tiled=True)
-    pick, leading = weigh(routed, router_weight.T, ids, capacity)
-    result = experts_here(arrived.reshape(-1, width), gate_weight, up_weight, down_weight)
+    result, pick, leading = experts_here(
+        arrived.reshape(-1, width), gate_weight, up_weight, down_weight, routed, router_weight.T, ids
+    )
     back = lax.all_to_all(result.reshape(owners, -1, width), "dp", split_axis=0, concat_axis=0, tiled=True)
     return combine(residual, leading, pick, back.reshape(-1, width))
 

time: 104 us -> 103 us (level)
  blocking collectives: 25.6 us -> 63.1 us
  waiting for transfers between devices: 35 us -> 7.15 us
  starting transfers between devices: 13 us -> 5.88 us
  Pallas kernels: 29.1 us -> 26.2 us
    all_to_all x0 -> x2, blocking collectives: none -> 36.3 us  [the longest x1 20.7 us: shards(): lax.all_to_all(result.reshape(owners, -1, width), 'dp', split_axis=0, con...]
    all_to_all x1 -> x0, waiting for transfers between devices: 16.3 us -> none  [shards(): lax.all_to_all(result.reshape(owners, -1, width), 'dp', split_axis=0, con...]
    ppermute x6 -> x3, waiting for transfers between devices: 18.7 us -> 7.15 us  [turned(): return lax.ppermute(x, axis, [(i, (i + k) % size) for i in range(size)])]
    all_to_all x1 -> x0, starting transfers between devices: 3.99 us -> none  [shards(): lax.all_to_all(result.reshape(owners, -1, width), 'dp', split_axis=0, con...]
    ppermute x6 -> x3, starting transfers between devices: 9.02 us -> 5.88 us  [turned(): return lax.ppermute(x, axis, [(i, (i + k) % size) for i in range(size)])]
    pallas_call x3 -> x2, Pallas kernels: 23.7 us -> 20.8 us  [the longest x1 12.6 us: experts_here(): pl.pallas_call(expert_kernel, out_shape=[jax.ShapeDtypeStruct(rows.shape,...]
    all_to_all x1, blocking collectives: 25.6 us -> 26.8 us  [shards(): lax.all_to_all(outgoing, 'dp', split_axis=0, concat_axis=0, tiled=True)]
  transfers between devices with their start and end apart: 7 -> 3, of which waited for: 6 -> 2; matrix products, arithmetic and copies ran while one was open for 1% -> 1% of each run, Pallas kernels for 4% -> 3%
where the time goes in v1:
time: 103 us
  blocking collectives  63.1 us (61%)
  Pallas kernels  26.2 us (25%)
  waiting for transfers between devices  7.15 us (7%)
  starting transfers between devices  5.88 us (6%)
    all_to_all x1, blocking collectives, shards(): lax.all_to_all(outgoing, 'dp', split_axis=0, concat_axis=0, tiled=True)  26.8 us
    all_to_all x1, blocking collectives, shards(): lax.all_to_all(result.reshape(owners, -1, width), 'dp', split_axis=0, con...  20.7 us
    all_to_all x1, blocking collectives, shards(): lax.all_to_all(parts, 'head', split_axis=0, concat_axis=0, tiled=True)  15.7 us
    pallas_call x1, Pallas kernels, experts_here(): pl.pallas_call(expert_kernel, out_shape=[jax.ShapeDtypeStruct(rows.shape,...  12.6 us
    pallas_call x1, Pallas kernels, mixer(): pl.pallas_call(lambda *refs: mixer_kernel(heads, *refs), out_shape=jax.Sh...  8.18 us
    ppermute x3, waiting for transfers between devices, turned(): return lax.ppermute(x, axis, [(i, (i + k) % size) for i in range(size)])  7.15 us
    ppermute x3, starting transfers between devices, turned(): return lax.ppermute(x, axis, [(i, (i + k) % size) for i in range(size)])  5.88 us
    pallas_call x1, Pallas kernels, load(): pl.pallas_call(load_kernel, out_shape=[pltpu.VMEM(w.shape, w.dtype) for w...  3.57 us
  transfers between devices with their start and end apart: 3, of which 2 were waited for; matrix products, arithmetic and copies ran while one was open for 1% of the time, Pallas kernels for 3%

profile of v1, /device:TPU:1, one launch (start us, length us, event | category | flops | bytes accessed | tf_op | source)
XLA Modules:
  0.0 103.1 jit_solution(13078876630529748404)
XLA Ops:
  0.0 2.5 %collective-permute-start = (bf16[256,512]{1,0:T(8,128)(2,1)}, bf16[256,512]{1,0:T(8,128)(2,1)S(1)}, u32[]{:S(2)}, u32[]{:S(2)}) collective-permute-start(bf16[256,512]{1,0:T(8,128)(2,1)} %refs_0_.1), channel_id=1, source_target_pairs={{0,1},{1,2},{2,3},{3,0},{4,5},{5,6},{6,7},{7,4},{8,9},{9,10},{10,1... | collective-permute-start | bytes 786440 | tf_op jit(solution)/shard_map/ppermute | solution.py:367
  2.5 2.1 %collective-permute-start.2 = (bf16[256,512]{1,0:T(8,128)(2,1)}, bf16[256,512]{1,0:T(8,128)(2,1)S(1)}, u32[]{:S(2)}, u32[]{:S(2)}) collective-permute-start(bf16[256,512]{1,0:T(8,128)(2,1)} %refs_0_.1), channel_id=1, source_target_pairs={{0,3},{1,0},{2,1},{3,2},{4,7},{5,4},{6,5},{7,6},{8,11},{9,8},{10,9... | collective-permute-start | bytes 786440 | tf_op jit(solution)/shard_map/ppermute | solution.py:367
  4.6 1.3 %collective-permute-start.1 = (bf16[256,512]{1,0:T(8,128)(2,1)}, bf16[256,512]{1,0:T(8,128)(2,1)S(1)}, u32[]{:S(2)}, u32[]{:S(2)}) collective-permute-start(bf16[256,512]{1,0:T(8,128)(2,1)} %refs_0_.1), channel_id=1, source_target_pairs={{0,2},{1,3},{2,0},{3,1},{4,6},{5,7},{6,4},{7,5},{8,10},{9,11},{10,... | collective-permute-start | bytes 786440 | tf_op jit(solution)/shard_map/ppermute | solution.py:367
  5.9 0.7 reshape.29.refs_5_
  6.6 3.6 %load.1 = (bf16[256,512]{1,0:T(8,128)(2,1)S(1)}, bf16[2048,256]{1,0:T(8,128)(2,1)S(1)}, bf16[3,2048,256]{2,1,0:T(8,128)(2,1)S(1)}, bf16[3,2048,256]{2,1,0:T(8,12...) custom-call(bf16[256,512]{1,0:T(8,128)(2,1)} %refs_0_.1, ...), custom_call_target="tpu_custom_call" | custom-call | flops 2000000000 | bytes 1000000 | tf_op jit(solution)/shard_map/load/pallas_call | solution.py:241
  10.2 0.6 collective-permute-done.refs_2_.x1
  10.8 0.0 collective-permute-done.2.refs_4_.x3
  10.8 6.5 %collective-permute-done.1.refs_3_.x2 = bf16[256,512]{1,0:T(8,128)(2,1)S(1)} collective-permute-done((bf16[256,512]{1,0:T(8,128)(2,1)}, bf16[256,512]{1,0:T(8,128)(2,1)S(1)}, u32[]{:S(2)}, u32[]{:S(2)}) %collective-permute-start.1) | collective-permute-done | bytes 262176 | tf_op jit(solution)/shard_map/ppermute | solution.py:367
  17.3 0.0 copy-start.1
  17.3 0.0 copy-start.2
  17.3 8.2 %mixer.1 = bf16[256,2048]{1,0:T(8,128)(2,1)S(1)} custom-call(s32[1]{0:T(128)} %bitcast.refs_0_.place_ref, bf16[256,512]{1,0:T(8,128)(2,1)S(1)} %get-tuple-element.18.refs_1_.x0, bf16[256,512]{1,0:T(8,128)(2,1)S(1)} %collective-permute-done.refs_2_.x1, bf16[256,512]{1,0:T(8,128)(2,1)S(1)} %collective-permute-done.1.refs_3_.x2, ...), custom_call_target="tpu_custom_call" | custom-call | flops 20000000000 | bytes 10000000 | tf_op jit(solution)/shard_map/mixer/pallas_call | solution.py:140
  25.5 15.7 %all_to_all.15.parts_ref = bf16[4,64,2048]{2,1,0:T(8,128)(2,1)S(1)} all-to-all(bf16[4,64,2048]{2,1,0:T(8,128)(2,1)S(1)} %bitcast.13), channel_id=1, replica_groups=mesh['dp'=32,'head'=4] {'head'}, dimensions={0} | all-to-all | bytes 2097152 | tf_op jit(solution)/shard_map/all_to_all | solution.py:380
  41.2 0.0 copy-start
  41.2 0.0 copy-done.1
  41.2 0.0 copy-done.2
  41.2 0.8 route.1
  42.0 26.8 %all_to_all.16 = bf16[32,8,2048]{2,1,0:T(8,128)(2,1)S(1)} all-to-all(bf16[32,8,2048]{2,1,0:T(8,128)(2,1)S(1)} %bitcast.12), channel_id=1, replica_groups=mesh['dp'=32,'head'=4] {'dp'}, dimensions={0} | all-to-all | bytes 2097152 | tf_op jit(solution)/shard_map/all_to_all | solution.py:388
  68.8 0.0 copy-done
  68.8 12.6 %experts.1 = (bf16[256,2048]{1,0:T(8,128)(2,1)S(1)}, bf16[128,256]{1,0:T(8,128)(2,1)S(1)}, f32[64,128]{1,0:T(8,128)S(1)}) custom-call(bf16[256,2048]{1,0:T(8,128)(2,1)S(1)} %bitcast.11, bf16[2,2048,1408]{2,1,0:T(8,128)(2,1)} %gate_hbm.1, bf16[2,2048,1408]{2,1,0:T(8,128)(2,1)} %up_hbm.1, bf16[2,1408,2048]{2,1,0:T(8,128)(2,1)} %down_hbm.1, ...), custom_call_target="tpu_custom_call" | custom-call | flops 5000000000 | bytes 10000000 | tf_op jit(solution)/shard_map/experts/pallas_call | solution.py:321
  81.4 20.7 %all_to_all.17 = bf16[32,8,2048]{2,1,0:T(8,128)(2,1)S(1)} all-to-all(bf16[32,8,2048]{2,1,0:T(8,128)(2,1)S(1)} %bitcast.15), channel_id=1, replica_groups=mesh['dp'=32,'head'=4] {'dp'}, dimensions={0} | all-to-all | bytes 2097152 | tf_op jit(solution)/shard_map/all_to_all | solution.py:392
  102.1 1.0 combine.1
Async XLA Ops:
  0.0 10.8 %collective-permute-start = (bf16[256,512]{1,0:T(8,128)(2,1)}, bf16[256,512]{1,0:T(8,128)(2,1)S(1)}, u32[]{:S(2)}, u32[]{:S(2)}) collective-permute-start(bf16[256,512]{1,0:T(8,128)(2,1)} %refs_0_.1), channel_id=1, source_target_pairs={{0,1},{1,2},{2,3},{3,0},{4,5},{5,6},{6,7},{7,4},{8,9},{9,10},{10,1... | collective-permute-start | bytes 786440 | tf_op jit(solution)/shard_map/ppermute | solution.py:367
  2.5 8.3 %collective-permute-start.2 = (bf16[256,512]{1,0:T(8,128)(2,1)}, bf16[256,512]{1,0:T(8,128)(2,1)S(1)}, u32[]{:S(2)}, u32[]{:S(2)}) collective-permute-start(bf16[256,512]{1,0:T(8,128)(2,1)} %refs_0_.1), channel_id=1, source_target_pairs={{0,3},{1,0},{2,1},{3,2},{4,7},{5,4},{6,5},{7,6},{8,11},{9,8},{10,9... | collective-permute-start | bytes 786440 | tf_op jit(solution)/shard_map/ppermute | solution.py:367
  4.6 12.7 %collective-permute-start.1 = (bf16[256,512]{1,0:T(8,128)(2,1)}, bf16[256,512]{1,0:T(8,128)(2,1)S(1)}, u32[]{:S(2)}, u32[]{:S(2)}) collective-permute-start(bf16[256,512]{1,0:T(8,128)(2,1)} %refs_0_.1), channel_id=1, source_target_pairs={{0,2},{1,3},{2,0},{3,1},{4,6},{5,7},{6,4},{7,5},{8,10},{9,11},{10,... | collective-permute-start | bytes 786440 | tf_op jit(solution)/shard_map/ppermute | solution.py:367
  17.3 23.8 %copy-start.1 = (s32[64,2]{0,1:T(2,128)S(1)}, s32[64,2]{0,1:T(2,128)}, u32[]{:S(2)}) copy-start(s32[64,2]{0,1:T(2,128)} %param.24) | copy-start | bytes 1540
  17.3 23.8 %copy-start.2 = (f32[2048]{0:T(1024)S(1)}, f32[2048]{0:T(1024)}, u32[]{:S(2)}) copy-start(f32[2048]{0:T(1024)} %param.22) | copy-start | bytes 24580
  41.2 27.6 %copy-start = (f32[2048,64]{0,1:T(8,128)S(1)}, f32[2048,64]{0,1:T(8,128)}, u32[]{:S(2)}) copy-start(f32[2048,64]{0,1:T(8,128)} %param.23) | copy-start | bytes 1572868

commit v2 on v1

--- a/solution.py
+++ b/solution.py
@@ -37,38 +37,105 @@
     return pl.ds(pl.multiple_of(block * size, size), size)
 
 
-def mixer_kernel(heads, place_ref, x0, x1, x2, x3, gain_ref, wq_ref, wk_ref, wv_ref, wb_ref, head_gain_ref,
-                 wo_ref, out_ref, normed, keys, beta_keys, rhs, queries, reduced, state_map, added, out_add, mixed):
+def gained(x_ref, gain_ref, source):
+    wide = x_ref[...].astype(F32)
+    return (wide * gain_ref[pl.ds(source, 1), :]).astype(BF16), jnp.sum(wide * wide, -1, keepdims=True)
+
+
+def products(x, source, wq_ref, wk_ref, wv_ref, wb_ref):
+    rows = rows_at(source, x.shape[1])
+    yield dot(x, wq_ref[rows, :])
+    for ref in (wk_ref, wv_ref):
+        for m in range(NH):
+            yield dot(x, ref[m, rows, :])
+    yield dot(x, wb_ref[:, rows], ((1,), (1,)))
+
+
+def first_kernel(place_ref, gain_ref, *refs):
+    count = (len(refs) - 4) // 2
+    here, there = refs[:count], refs[count:2 * count]
+    sums_ref, beta_ref, square_ref, sems = refs[2 * count:]
+    copies = [pltpu.make_async_copy(h, t, sems.at[i]) for i, (h, t) in enumerate(zip(here, there))]
+    for copy in copies:
+        copy.start()
+    for copy in copies:
+        copy.wait()
+    x, square_ref[...] = gained(there[0], gain_ref, place_ref[0])
+    for i, product in enumerate(products(x, place_ref[0], *there[1:5])):
+        if i < 1 + 2 * NH:
+            sums_ref[i] = product
+        else:
+            beta_ref[...] = product
+
+
+def first(me, gain, tokens, wq, wk, wv, wb, *others):
+    moved = (tokens, wq, wk, wv, wb, *others)
+    length = tokens.shape[0]
+    vmem = pl.BlockSpec(memory_space=pltpu.VMEM)
+    made = [
+        pltpu.VMEM((1 + 2 * NH, length, wq.shape[1]), F32),
+        pltpu.VMEM((length, wb.shape[0]), F32),
+        pltpu.VMEM((length, 1), F32),
+    ]
+    return pl.pallas_call(
+        first_kernel,
+        out_shape=[pltpu.VMEM(w.shape, w.dtype) for w in moved] + made,
+        in_specs=[pl.BlockSpec(memory_space=pltpu.SMEM), vmem] + [pl.BlockSpec(memory_space=pltpu.HBM)] * len(moved),
+        out_specs=[vmem] * (len(moved) + 3),
+        scratch_shapes=[pltpu.SemaphoreType.DMA((len(moved),))],
+        compiler_params=pltpu.CompilerParams(vmem_limit_bytes=4 * MIB),
+        cost_estimate=pl.CostEstimate(flops=2 * 10 ** 9, bytes_accessed=10 ** 6, transcendentals=0),
+        name="first",
+    )(me, gain, *[pltpu.with_memory_space_constraint(w, pltpu.HBM) for w in moved])
+
+
+def more_kernel(shift, place_ref, gain_ref, x_ref, wq_ref, wk_ref, wv_ref, wb_ref, sums_ref, beta_ref, square_ref,
+                new_sums_ref, new_beta_ref, new_square_ref):
+    source = (place_ref[0] + (gain_ref.shape[0] - shift)) % gain_ref.shape[0]
+    x, square = gained(x_ref, gain_ref, source)
+    new_square_ref[...] = square_ref[...] + square
+    for i, product in enumerate(products(x, source, wq_ref, wk_ref, wv_ref, wb_ref)):
+        if i < 1 + 2 * NH:
+            new_sums_ref[i] = sums_ref[i] + product
+        else:
+            new_beta_ref[...] = beta_ref[...] + product
+
+
+def more(shift, me, gain, x, weights, sums):
+    vmem = pl.BlockSpec(memory_space=pltpu.VMEM)
+    return pl.pallas_call(
+        lambda *refs: more_kernel(shift, *refs),
+        out_shape=[pltpu.VMEM(a.shape, a.dtype) for a in sums],
+        in_specs=[pl.BlockSpec(memory_space=pltpu.SMEM)] + [vmem] * 9,
+        out_specs=[vmem] * 3,
+        input_output_aliases={7: 0, 8: 1, 9: 2},
+        compiler_params=pltpu.CompilerParams(vmem_limit_bytes=4 * MIB),
+        cost_estimate=pl.CostEstimate(flops=10 ** 9, bytes_accessed=10 ** 6, transcendentals=0),
+        name="more",
+    )(me, gain, x, *weights, *sums)
+
+
+def mixer_kernel(heads, shift, place_ref, gain_ref, x_ref, wq_ref, wk_ref, wv_ref, wb_ref, sums_ref, beta_ref, square_ref,
+                 head_gain_ref, wo_ref, o0, o1, o2, o3, keys, beta_keys, rhs, queries, state_map, added, out_add, mixed):
     me = place_ref[0]
-    xs = (x0, x1, x2, x3)
-    count = len(xs)
-    length, part = x0.shape
-    sources = [lax.rem(me - k + count, count) for k in range(count)]
-    total = 0.0
-    for x in xs:
-        wide = x[...].astype(F32)
-        total = total + jnp.sum(wide * wide, -1, keepdims=True)
-    scale = lax.rsqrt(total / (count * part) + EPSILON)
-    for k in range(count):
-        gain = gain_ref[pl.ds(sources[k], 1), :]
-        normed[k] = (xs[k][...].astype(F32) * scale * gain).astype(BF16)
-
-    def project(weight):
-        return sum(dot(normed[k], weight(rows_at(sources[k], part))) for k in range(count))
-
-    beta = sum(
-        dot(normed[k], wb_ref[:, rows_at(sources[k], part)], ((1,), (1,))) for k in range(count)
-    )
+    count, part = gain_ref.shape
+    length = x_ref.shape[0]
+    source = lax.rem(me + (count - shift), count)
+    x, square = gained(x_ref, gain_ref, source)
+    scale = lax.rsqrt((square_ref[...] + square) / (count * part) + EPSILON)
+    last = products(x, source, wq_ref, wk_ref, wv_ref, wb_ref)
+    whole = [(sums_ref[i] + next(last)) * scale for i in range(1 + 2 * NH)]
+    beta = (beta_ref[...] + next(last)) * scale
     beta = 2.0 / (1.0 + jnp.exp(-beta))
     blocks = length // CH
-    query = project(lambda r: wq_ref[r, :])
+    query = whole[0]
     for h in range(heads):
         q = query[:, h * DK:(h + 1) * DK]
         q = q * lax.rsqrt(jnp.sum(q * q, -1, keepdims=True) + EPSILON) * DK ** (-0.5)
         queries[h] = q.reshape(blocks, CH, DK)
     for m in range(NH):
-        key = project(lambda r: wk_ref[m, r, :])
-        value = project(lambda r: wv_ref[m, r, :])
+        key = whole[1 + m]
+        value = whole[1 + NH + m]
         for h in range(heads):
             b = beta[:, h * NH + m:h * NH + m + 1]
             k = key[:, h * DK:(h + 1) * DK]
@@ -126,29 +193,33 @@
             states[h] = states[h] - moved[CH:] + added[h, c]
             out = out * lax.rsqrt(jnp.mean(out * out, -1, keepdims=True) + EPSILON) * head_gain_ref[...]
             mixed[c * CH:(c + 1) * CH, h * DK:(h + 1) * DK] = out.astype(BF16)
-    out_ref[...] = dot(mixed[...], wo_ref[...]).astype(BF16)
+    own = length // count
+    rolled = jnp.concatenate([mixed[rows_at(lax.rem(me + k, count), own), :] for k in range(count)], 0)
+    result = dot(rolled, wo_ref[...]).astype(BF16)
+    for k, o in enumerate((o0, o1, o2, o3)):
+        o[...] = result[k * own:(k + 1) * own]
 
 
 UNROLL = 8
 
 
-def mixer(me, xs, gain, wq, wk, wv, wb, head_gain, wo):
-    length, part = xs[0].shape
-    heads = wq.shape[1] // DK
+def mixer(me, gain, x, shift, weights, sums, head_gain, wo):
+    count = gain.shape[0]
+    length = x.shape[0]
+    heads = weights[0].shape[1] // DK
     blocks = length // CH
-    vmem = pl.BlockSpec(memory_space=pltpu.VMEM)
-    return pl.pallas_call(
-        lambda *refs: mixer_kernel(heads, *refs),
-        out_shape=jax.ShapeDtypeStruct((length, wo.shape[1]), BF16),
+    own = length // count
+    vmem = pl.BlockSpec(memory_space=pltpu.VMEM)
+    return pl.pallas_call(
+        lambda *refs: mixer_kernel(heads, shift, *refs),
+        out_shape=[jax.ShapeDtypeStruct((own, wo.shape[1]), BF16)] * count,
         in_specs=[pl.BlockSpec(memory_space=pltpu.SMEM)] + [vmem] * 11,
-        out_specs=vmem,
+        out_specs=[vmem] * count,
         scratch_shapes=[
-            pltpu.VMEM((len(xs), length, part), BF16),
             pltpu.VMEM((heads, blocks, SUB, DK), F32),
             pltpu.VMEM((heads, blocks, SUB, DK), F32),
             pltpu.VMEM((heads, blocks, SUB, 2 * DK), BF16),
             pltpu.VMEM((heads, blocks, CH, DK), F32),
-            pltpu.VMEM((8, DK), F32),
             pltpu.VMEM((heads, blocks, CH + DK, DK), BF16),
             pltpu.VMEM((heads, blocks, DK, DK), F32),
             pltpu.VMEM((heads, blocks, CH, DK), F32),
@@ -157,7 +228,7 @@
         compiler_params=pltpu.CompilerParams(vmem_limit_bytes=32 * MIB),
         cost_estimate=pl.CostEstimate(flops=2 * 10 ** 10, bytes_accessed=10 ** 7, transcendentals=0),
         name="mixer",
-    )(me, *xs, gain, wq, wk, wv, wb, head_gain, wo)
+    )(me, gain, x, *weights, *sums, head_gain, wo)
 
 
 def slots(ids_ref, experts, capacity):
@@ -174,15 +245,15 @@
     return chosen, [jnp.where(fits, dot(spread, c.astype(BF16)), 0.0) for c in chosen]
 
 
-def route_kernel(place_ref, parts_ref, x0, x1, x2, x3, gain_ref, ids_ref, residual_ref, routed_ref, send_ref):
+def route_kernel(place_ref, p0, p1, p2, p3, x0, x1, x2, x3, gain_ref, ids_ref, residual_ref, routed_ref, send_ref):
     me = place_ref[0]
     xs = (x0, x1, x2, x3)
     count = len(xs)
-    own, part = parts_ref.shape[1], x0.shape[1]
+    own, part = p0.shape[0], x0.shape[1]
     for k in range(count):
         columns = rows_at(lax.rem(me - k + count, count), part)
         residual_ref[:, columns] = xs[k][rows_at(me, own), :].astype(F32)
-    arrived = [parts_ref[k].astype(F32) for k in range(count)]
+    arrived = [p[...].astype(F32) for p in (p0, p1, p2, p3)]
     residual = residual_ref[...] + ((arrived[0] + arrived[1]) + (arrived[2] + arrived[3]))
     residual_ref[...] = residual
     mean = jnp.mean(residual * residual, -1, keepdims=True)
@@ -194,7 +265,7 @@
 
 
 def route(me, parts, xs, gain, ids, experts, capacity):
-    _, own, width = parts.shape
+    own, width = parts[0].shape
     vmem = pl.BlockSpec(memory_space=pltpu.VMEM)
     return pl.pallas_call(
         route_kernel,
@@ -203,12 +274,12 @@
             jax.ShapeDtypeStruct((own, width), F32),
             jax.ShapeDtypeStruct((experts * capacity, width), BF16),
         ],
-        in_specs=[pl.BlockSpec(memory_space=pltpu.SMEM)] + [vmem] * 7,
+        in_specs=[pl.BlockSpec(memory_space=pltpu.SMEM)] + [vmem] * 10,
         out_specs=[vmem] * 3,
         compiler_params=pltpu.CompilerParams(vmem_limit_bytes=16 * MIB),
         cost_estimate=pl.CostEstimate(flops=10 ** 9, bytes_accessed=10 ** 7, transcendentals=0),
         name="route",
-    )(me, parts, *xs, gain, ids)
+    )(me, *parts, *xs, gain, ids)
 
 
 def weigh(routed_ref, router_ref, ids_ref, pick_ref, leading_ref):
@@ -224,30 +295,6 @@
     gap = jnp.sum((chosen[0] - chosen[1]) * logits, 0, keepdims=True)
     leading = 1.0 / (1.0 + jnp.exp(-gap))
     leading_ref[...] = jnp.transpose(jnp.broadcast_to(leading, (128, tokens)))
-
-
-def load_kernel(*refs):
-    half = (len(refs) - 1) // 2
-    sems = refs[-1]
-    copies = []
-    for i in range(half):
-        copies.append(pltpu.make_async_copy(refs[i], refs[half + i], sems.at[i]))
-        copies[-1].start()
-    for copy in copies:
-        copy.wait()
-
-
-def load(*weights):
-    return pl.pallas_call(
-        load_kernel,
-        out_shape=[pltpu.VMEM(w.shape, w.dtype) for w in weights],
-        in_specs=[pl.BlockSpec(memory_space=pltpu.HBM)] * len(weights),
-        out_specs=[pl.BlockSpec(memory_space=pltpu.VMEM)] * len(weights),
-        scratch_shapes=[pltpu.SemaphoreType.DMA((len(weights),))],
-        compiler_params=pltpu.CompilerParams(vmem_limit_bytes=1 * MIB),
-        cost_estimate=pl.CostEstimate(flops=2 * 10 ** 9, bytes_accessed=10 ** 6, transcendentals=0),
-        name="load",
-    )(*[pltpu.with_memory_space_constraint(w, pltpu.HBM) for w in weights])
 
 
 def expert_kernel(rows_ref, gate_hbm, up_hbm, down_hbm, routed_ref, router_ref, ids_ref, out_ref, pick_ref, leading_ref,
@@ -373,13 +420,16 @@
     owners = lax.axis_size("dp")
     me = lax.axis_index("head").reshape(1).astype(jnp.int32)
     xs = [tokens] + [turned(tokens, k, "head") for k in range(1, peers)]
-    here = load(tokens, query_weight, key_weight, value_weight, beta_weight.T, head_gain.reshape(1, -1), output_weight)
-    xs[0] = here[0]
-    parts = mixer(me, xs, mixer_gain.reshape(peers, -1), *here[1:])
-    parts = parts.reshape(peers, -1, parts.shape[1])
-    parts = lax.all_to_all(parts, "head", split_axis=0, concat_axis=0, tiled=True)
+    gain = mixer_gain.reshape(peers, -1)
+    here = first(me, gain, tokens, query_weight, key_weight, value_weight, beta_weight.T, head_gain.reshape(1, -1),
+                 output_weight)
+    xs[0], weights, sums = here[0], here[1:5], here[7:]
+    for shift in (1, 3):
+        sums = more(shift, me, gain, xs[shift], weights, sums)
+    parts = mixer(me, gain, xs[2], 2, weights, sums, here[5], here[6])
+    parts = [parts[0]] + [turned(parts[k], k, "head") for k in range(1, peers)]
     experts = router_weight.shape[1]
-    own = parts.shape[1]
+    own = parts[0].shape[0]
     capacity = 4 * own // experts
     ids = expert_ids.T
     residual, routed, outgoing = route(me, parts, xs, expert_gain.reshape(1, -1), ids, experts, capacity)

time: 103 us -> 99.5 us (0.966)
  blocking collectives: 63.1 us -> 46.2 us
  waiting for transfers between devices: 7.15 us -> 16.2 us
  starting transfers between devices: 5.88 us -> 9.01 us
    all_to_all x1 -> x0, blocking collectives: 15.7 us -> none  [shards(): lax.all_to_all(parts, 'head', split_axis=0, concat_axis=0, tiled=True)]
    ppermute x3 -> x6, waiting for transfers between devices: 7.15 us -> 16.2 us  [turned(): return lax.ppermute(x, axis, [(i, (i + k) % size) for i in range(size)])]
    ppermute x3 -> x6, starting transfers between devices: 5.88 us -> 9.01 us  [turned(): return lax.ppermute(x, axis, [(i, (i + k) % size) for i in range(size)])]
    all_to_all x1, blocking collectives: 26.8 us -> 25.5 us  [shards(): lax.all_to_all(outgoing, 'dp', split_axis=0, concat_axis=0, tiled=True)]
    pallas_call x2 -> x4, Pallas kernels: 11.7 us -> 12.6 us  [the longest x1 6.61 us: mixer(): pl.pallas_call(lambda *refs: mixer_kernel(heads, shift, *refs), out_shape...]
  transfers between devices with their start and end apart: 3 -> 6, of which waited for: 2 -> 4; matrix products, arithmetic and copies ran while one was open for 1% -> 1% of each run, Pallas kernels for 3% -> 6%
where the time goes in v2:
time: 99.5 us; the launch traced here: 99.3 us
  blocking collectives  46.2 us (46%)
  Pallas kernels  27.1 us (27%)
  waiting for transfers between devices  16.2 us (16%)
  starting transfers between devices  9.01 us (9%)
    all_to_all x1, blocking collectives, shards(): lax.all_to_all(outgoing, 'dp', split_axis=0, concat_axis=0, tiled=True)  25.5 us
    all_to_all x1, blocking collectives, shards(): lax.all_to_all(result.reshape(owners, -1, width), 'dp', split_axis=0, con...  20.7 us
    ppermute x6, waiting for transfers between devices, turned(): return lax.ppermute(x, axis, [(i, (i + k) % size) for i in range(size)])  16.2 us
    pallas_call x1, Pallas kernels, experts_here(): pl.pallas_call(expert_kernel, out_shape=[jax.ShapeDtypeStruct(rows.shape,...  12.6 us
    ppermute x6, starting transfers between devices, turned(): return lax.ppermute(x, axis, [(i, (i + k) % size) for i in range(size)])  9.01 us
    pallas_call x1, Pallas kernels, mixer(): pl.pallas_call(lambda *refs: mixer_kernel(heads, shift, *refs), out_shape...  6.61 us
    pallas_call x1, Pallas kernels, first(): pl.pallas_call(first_kernel, out_shape=[pltpu.VMEM(w.shape, w.dtype) for...  4.29 us
  transfers between devices with their start and end apart: 6, of which 4 were waited for; matrix products, arithmetic and copies ran while one was open for 1% of the time, Pallas kernels for 6%

profile of v2, /device:TPU:1, one launch (start us, length us, event | category | flops | bytes accessed | tf_op | source)
XLA Modules:
  0.0 99.3 jit_solution(1686755634194804715)
XLA Ops:
  0.0 2.5 %collective-permute-start.2 = (bf16[256,512]{1,0:T(8,128)(2,1)}, bf16[256,512]{1,0:T(8,128)(2,1)S(1)}, u32[]{:S(2)}, u32[]{:S(2)}) collective-permute-start(bf16[256,512]{1,0:T(8,128)(2,1)} %refs_0_.1), channel_id=1, source_target_pairs={{0,1},{1,2},{2,3},{3,0},{4,5},{5,6},{6,7},{7,4},{8,9},{9,10},{10,1... | collective-permute-start | bytes 786440 | tf_op jit(solution)/shard_map/ppermute | solution.py:414
  2.5 2.1 %collective-permute-start.1 = (bf16[256,512]{1,0:T(8,128)(2,1)}, bf16[256,512]{1,0:T(8,128)(2,1)S(1)}, u32[]{:S(2)}, u32[]{:S(2)}) collective-permute-start(bf16[256,512]{1,0:T(8,128)(2,1)} %refs_0_.1), channel_id=1, source_target_pairs={{0,3},{1,0},{2,1},{3,2},{4,7},{5,4},{6,5},{7,6},{8,11},{9,8},{10,9... | collective-permute-start | bytes 786440 | tf_op jit(solution)/shard_map/ppermute | solution.py:414
  4.6 1.3 %collective-permute-start = (bf16[256,512]{1,0:T(8,128)(2,1)}, bf16[256,512]{1,0:T(8,128)(2,1)S(1)}, u32[]{:S(2)}, u32[]{:S(2)}) collective-permute-start(bf16[256,512]{1,0:T(8,128)(2,1)} %refs_0_.1), channel_id=1, source_target_pairs={{0,2},{1,3},{2,0},{3,1},{4,6},{5,7},{6,4},{7,5},{8,10},{9,11},{10,... | collective-permute-start | bytes 786440 | tf_op jit(solution)/shard_map/ppermute | solution.py:414
  5.9 0.7 reshape.25.gain_ref.refs_1_
  6.6 4.3 %first.1 = (bf16[256,512]{1,0:T(8,128)(2,1)S(1)}, bf16[2048,256]{1,0:T(8,128)(2,1)S(1)}, bf16[3,2048,256]{2,1,0:T(8,128)(2,1)S(1)}, bf16[3,2048,256]{2,1,0:T(8,1...) custom-call(s32[1]{0:T(128)} %bitcast.place_ref.refs_0_, ...), custom_call_target="tpu_custom_call" | custom-call | flops 2000000000 | bytes 1000000 | tf_op jit(solution)/shard_map/first/pallas_call | solution.py:80
  10.9 0.0 collective-permute-done.2.refs_2_.x1
  10.9 0.9 more.2
  11.8 0.0 collective-permute-done.1.refs_2_.x3
  11.8 0.8 more.3
  12.6 4.7 %collective-permute-done.refs_2_.x2 = bf16[256,512]{1,0:T(8,128)(2,1)S(1)} collective-permute-done((bf16[256,512]{1,0:T(8,128)(2,1)}, bf16[256,512]{1,0:T(8,128)(2,1)S(1)}, u32[]{:S(2)}, u32[]{:S(2)}) %collective-permute-start) | collective-permute-done | bytes 262176 | tf_op jit(solution)/shard_map/ppermute | solution.py:414
  17.3 0.0 copy-start.1
  17.3 0.0 copy-start.2
  17.3 6.6 %mixer.1 = (bf16[64,2048]{1,0:T(8,128)(2,1)S(1)}, bf16[64,2048]{1,0:T(8,128)(2,1)S(1)}, bf16[64,2048]{1,0:T(8,128)(2,1)S(1)}, bf16[64,2048]{1,0:T(8,128)(2,1)S(1)}) custom-call(s32[1]{0:T(128)} %bitcast.place_ref.refs_0_, f32[4,512]{1,0:T(4,128)S(1)} %reshape.25.gain_ref.refs_1_, bf16[256,512]{1,0:T(8,128)(2,1)S(1)} %collective-permute-done.refs_2_.x2, ...), custom_call_target="tpu_custom_call" | custom-call | flops 20000000000 | bytes 10000000 | tf_op jit(solution)/shard_map/mixer/pallas_call | solution.py:213
  23.9 0.0 copy-start
  23.9 0.6 collective-permute-start.3
  24.6 1.4 %collective-permute-start.4 = (bf16[64,2048]{1,0:T(8,128)(2,1)S(1)}, bf16[64,2048]{1,0:T(8,128)(2,1)S(1)}, u32[]{:S(2)}, u32[]{:S(2)}) collective-permute-start(bf16[64,2048]{1,0:T(8,128)(2,1)S(1)} %get-tuple-element.48), channel_id=1, source_target_pairs={{0,2},{1,3},{2,0},{3,1},{4,6},{5,7},{6,4},{7,5},{8,10},{9,11},{10,... | collective-permute-start | bytes 786440 | tf_op jit(solution)/shard_map/ppermute | solution.py:414
  26.0 1.1 %collective-permute-start.5 = (bf16[64,2048]{1,0:T(8,128)(2,1)S(1)}, bf16[64,2048]{1,0:T(8,128)(2,1)S(1)}, u32[]{:S(2)}, u32[]{:S(2)}) collective-permute-start(bf16[64,2048]{1,0:T(8,128)(2,1)S(1)} %get-tuple-element.49), channel_id=1, source_target_pairs={{0,3},{1,0},{2,1},{3,2},{4,7},{5,4},{6,5},{7,6},{8,11},{9,8},{10,9... | collective-permute-start | bytes 786440 | tf_op jit(solution)/shard_map/ppermute | solution.py:414
  27.1 6.9 %collective-permute-done.3.p1 = bf16[64,2048]{1,0:T(8,128)(2,1)S(1)} collective-permute-done((bf16[64,2048]{1,0:T(8,128)(2,1)S(1)}, bf16[64,2048]{1,0:T(8,128)(2,1)S(1)}, u32[]{:S(2)}, u32[]{:S(2)}) %collective-permute-start.3) | collective-permute-done | bytes 262176 | tf_op jit(solution)/shard_map/ppermute | solution.py:414
  33.9 0.6 collective-permute-done.4.p2
  34.5 4.1 %collective-permute-done.5.p3 = bf16[64,2048]{1,0:T(8,128)(2,1)S(1)} collective-permute-done((bf16[64,2048]{1,0:T(8,128)(2,1)S(1)}, bf16[64,2048]{1,0:T(8,128)(2,1)S(1)}, u32[]{:S(2)}, u32[]{:S(2)}) %collective-permute-start.5) | collective-permute-done | bytes 262176 | tf_op jit(solution)/shard_map/ppermute | solution.py:414
  38.6 0.0 copy-done.1
  38.6 0.0 copy-done.2
  38.6 0.8 route.1
  39.5 25.5 %all_to_all.10 = bf16[32,8,2048]{2,1,0:T(8,128)(2,1)S(1)} all-to-all(bf16[32,8,2048]{2,1,0:T(8,128)(2,1)S(1)} %bitcast.11), channel_id=1, replica_groups=mesh['dp'=32,'head'=4] {'dp'}, dimensions={0} | all-to-all | bytes 2097152 | tf_op jit(solution)/shard_map/all_to_all | solution.py:438
  65.0 0.0 copy-done
  65.0 12.6 %experts.1 = (bf16[256,2048]{1,0:T(8,128)(2,1)S(1)}, bf16[128,256]{1,0:T(8,128)(2,1)S(1)}, f32[64,128]{1,0:T(8,128)S(1)}) custom-call(bf16[256,2048]{1,0:T(8,128)(2,1)S(1)} %bitcast.10, bf16[2,2048,1408]{2,1,0:T(8,128)(2,1)} %gate_hbm.1, bf16[2,2048,1408]{2,1,0:T(8,128)(2,1)} %up_hbm.1, bf16[2,1408,2048]{2,1,0:T(8,128)(2,1)} %down_hbm.1, ...), custom_call_target="tpu_custom_call" | custom-call | flops 5000000000 | bytes 10000000 | tf_op jit(solution)/shard_map/experts/pallas_call | solution.py:368
  77.6 20.7 %all_to_all.11 = bf16[32,8,2048]{2,1,0:T(8,128)(2,1)S(1)} all-to-all(bf16[32,8,2048]{2,1,0:T(8,128)(2,1)S(1)} %bitcast.13), channel_id=1, replica_groups=mesh['dp'=32,'head'=4] {'dp'}, dimensions={0} | all-to-all | bytes 2097152 | tf_op jit(solution)/shard_map/all_to_all | solution.py:442
  98.3 1.0 %combine.1 = bf16[64,2048]{1,0:T(8,128)(2,1)} custom-call(f32[64,2048]{1,0:T(8,128)S(1)} %get-tuple-element.51.residual_ref, f32[64,128]{1,0:T(8,128)S(1)} %get-tuple-element.54.leading_ref, bf16[128,256]{1,0:T(8,128)(2,1)S(1)} %get-tuple-element.55.pick_ref, bf16[256,2048]{1,0:T(8,128)(2,1)S(1)} %bitcast.12), custom_call_target="tpu_custom_call" | custom-call | flops 1000000000 | bytes 1000000 | tf_op jit(solution)/shard_map/combine/pallas_call | solution.py:401
Async XLA Ops:
  0.0 10.9 %collective-permute-start.2 = (bf16[256,512]{1,0:T(8,128)(2,1)}, bf16[256,512]{1,0:T(8,128)(2,1)S(1)}, u32[]{:S(2)}, u32[]{:S(2)}) collective-permute-start(bf16[256,512]{1,0:T(8,128)(2,1)} %refs_0_.1), channel_id=1, source_target_pairs={{0,1},{1,2},{2,3},{3,0},{4,5},{5,6},{6,7},{7,4},{8,9},{9,10},{10,1... | collective-permute-start | bytes 786440 | tf_op jit(solution)/shard_map/ppermute | solution.py:414
  2.5 9.3 %collective-permute-start.1 = (bf16[256,512]{1,0:T(8,128)(2,1)}, bf16[256,512]{1,0:T(8,128)(2,1)S(1)}, u32[]{:S(2)}, u32[]{:S(2)}) collective-permute-start(bf16[256,512]{1,0:T(8,128)(2,1)} %refs_0_.1), channel_id=1, source_target_pairs={{0,3},{1,0},{2,1},{3,2},{4,7},{5,4},{6,5},{7,6},{8,11},{9,8},{10,9... | collective-permute-start | bytes 786440 | tf_op jit(solution)/shard_map/ppermute | solution.py:414
  4.6 12.7 %collective-permute-start = (bf16[256,512]{1,0:T(8,128)(2,1)}, bf16[256,512]{1,0:T(8,128)(2,1)S(1)}, u32[]{:S(2)}, u32[]{:S(2)}) collective-permute-start(bf16[256,512]{1,0:T(8,128)(2,1)} %refs_0_.1), channel_id=1, source_target_pairs={{0,2},{1,3},{2,0},{3,1},{4,6},{5,7},{6,4},{7,5},{8,10},{9,11},{10,... | collective-permute-start | bytes 786440 | tf_op jit(solution)/shard_map/ppermute | solution.py:414
  17.3 21.3 %copy-start.1 = (s32[64,2]{0,1:T(2,128)S(1)}, s32[64,2]{0,1:T(2,128)}, u32[]{:S(2)}) copy-start(s32[64,2]{0,1:T(2,128)} %param.24) | copy-start | bytes 1540
  17.3 21.3 %copy-start.2 = (f32[2048]{0:T(1024)S(1)}, f32[2048]{0:T(1024)}, u32[]{:S(2)}) copy-start(f32[2048]{0:T(1024)} %param.22) | copy-start | bytes 24580
  23.9 41.1 %copy-start = (f32[2048,64]{0,1:T(8,128)S(1)}, f32[2048,64]{0,1:T(8,128)}, u32[]{:S(2)}) copy-start(f32[2048,64]{0,1:T(8,128)} %param.23) | copy-start | bytes 1572868
  23.9 10.0 %collective-permute-start.3 = (bf16[64,2048]{1,0:T(8,128)(2,1)S(1)}, bf16[64,2048]{1,0:T(8,128)(2,1)S(1)}, u32[]{:S(2)}, u32[]{:S(2)}) collective-permute-start(bf16[64,2048]{1,0:T(8,128)(2,1)S(1)} %get-tuple-element.47), channel_id=1, source_target_pairs={{0,1},{1,2},{2,3},{3,0},{4,5},{5,6},{6,7},{7,4},{8,9},{9,10},{10,1... | collective-permute-start | bytes 786440 | tf_op jit(solution)/shard_map/ppermute | solution.py:414
  24.6 9.9 %collective-permute-start.4 = (bf16[64,2048]{1,0:T(8,128)(2,1)S(1)}, bf16[64,2048]{1,0:T(8,128)(2,1)S(1)}, u32[]{:S(2)}, u32[]{:S(2)}) collective-permute-start(bf16[64,2048]{1,0:T(8,128)(2,1)S(1)} %get-tuple-element.48), channel_id=1, source_target_pairs={{0,2},{1,3},{2,0},{3,1},{4,6},{5,7},{6,4},{7,5},{8,10},{9,11},{10,... | collective-permute-start | bytes 786440 | tf_op jit(solution)/shard_map/ppermute | solution.py:414
  26.0 12.7 %collective-permute-start.5 = (bf16[64,2048]{1,0:T(8,128)(2,1)S(1)}, bf16[64,2048]{1,0:T(8,128)(2,1)S(1)}, u32[]{:S(2)}, u32[]{:S(2)}) collective-permute-start(bf16[64,2048]{1,0:T(8,128)(2,1)S(1)} %get-tuple-element.49), channel_id=1, source_target_pairs={{0,3},{1,0},{2,1},{3,2},{4,7},{5,4},{6,5},{7,6},{8,11},{9,8},{10,9... | collective-permute-start | bytes 786440 | tf_op jit(solution)/shard_map/ppermute | solution.py:414

commit v3 on v2

--- a/solution.py
+++ b/solution.py
@@ -9,6 +9,7 @@
 NH = 3
 CH = 32
 SUB = CH * NH
+WIDE = 128
 BASE = 4
 EPSILON = 1e-06
 F32 = jnp.float32
@@ -133,6 +134,8 @@
         q = query[:, h * DK:(h + 1) * DK]
         q = q * lax.rsqrt(jnp.sum(q * q, -1, keepdims=True) + EPSILON) * DK ** (-0.5)
         queries[h] = q.reshape(blocks, CH, DK)
+    for edge in (SUB, WIDE + SUB):
+        keys[:, :, edge:edge + WIDE - SUB, :] = jnp.zeros((heads, blocks, WIDE - SUB, DK), BF16)
     for m in range(NH):
         key = whole[1 + m]
         value = whole[1 + NH + m]
@@ -140,44 +143,67 @@
             b = beta[:, h * NH + m:h * NH + m + 1]
             k = key[:, h * DK:(h + 1) * DK]
             k = k * lax.rsqrt(jnp.sum(k * k, -1, keepdims=True) + EPSILON)
-            keys[h, :, m * CH:(m + 1) * CH, :] = k.reshape(blocks, CH, DK)
+            high, low = split(k)
+            keys[h, :, m * CH:(m + 1) * CH, :] = high.reshape(blocks, CH, DK)
+            keys[h, :, WIDE + m * CH:WIDE + (m + 1) * CH, :] = low.reshape(blocks, CH, DK)
             rhs[h, :, m * CH:(m + 1) * CH, :DK] = (k * b).astype(BF16).reshape(blocks, CH, DK)
             rhs[h, :, m * CH:(m + 1) * CH, DK:] = (value[:, h * DK:(h + 1) * DK] * b).astype(BF16).reshape(blocks, CH, DK)
             beta_keys[h, :, m * CH:(m + 1) * CH, :] = jnp.broadcast_to(b, (length, DK)).reshape(blocks, CH, DK)
 
-    row, col = iota((SUB, SUB), 0), iota((SUB, SUB), 1)
+    row, col = iota((SUB, WIDE), 0), iota((SUB, WIDE), 1)
+    inside = col < SUB
     row_t, col_t = row % CH, col % CH
-    causal = (col_t < row_t) | ((col_t == row_t) & (col < row))
-    same = [row_t // s == col_t // s for s in (BASE, BASE * 2, BASE * 4, BASE * 8)]
+    causal = inside & ((col_t < row_t) | ((col_t == row_t) & (col < row)))
+    near = row_t // BASE == col_t // BASE
     eye = (row == col).astype(F32)
     seen = iota((CH, SUB), 1) % CH <= iota((CH, SUB), 0)
+    blank = jnp.zeros((WIDE - SUB, WIDE), F32)
+
+    def square(p):
+        return dot(p[:, :SUB], p)
+
+    def both(p, t):
+        made = dot(p[:, :SUB], jnp.concatenate([p, t.astype(BF16)], 1))
+        return made[:, :WIDE].astype(BF16), t + made[:, WIDE:]
+
+    def doubled(powers, sums, terms):
+        span = 2
+        while 2 * span < terms:
+            stepped = [both(p, t) for p, t in zip(powers, sums)]
+            powers, sums = [p for p, _ in stepped], [t for _, t in stepped]
+            span *= 2
+        return [t + dot(p[:, :SUB], t.astype(BF16)) for p, t in zip(powers, sums)]
 
     unroll = UNROLL
     for start in range(0, blocks, unroll):
         at = [(h, c) for c in range(start, start + unroll) for h in range(heads)]
-        ks = [split(keys[i]) for i in at]
-        lower = [
-            jnp.where(causal, dot3(k, k, ((1,), (1,))) * beta_keys[i][:, :SUB], 0.0) for i, k in zip(at, ks)
+        pairs = [keys[i] for i in at]
+        alike = [dot(k[:SUB], k, ((1,), (1,))) for k in pairs]
+        alike = [
+            a[:, :WIDE] + a[:, WIDE:] + jnp.transpose(jnp.concatenate([a[:, WIDE:], blank], 0))[:SUB] for a in alike
         ]
-        power = [jnp.where(same[0], -l, 0.0) for l in lower]
+        lower = [jnp.where(causal, a * beta_keys[i], 0.0) for i, a in zip(at, alike)]
+        power = [jnp.where(near, -l, 0.0) for l in lower]
         inverse = [eye + p for p in power]
-        span = 2
-        while span < BASE * NH:
-            power = [p.astype(BF16) for p in power]
-            power = [dot(p, p) for p in power]
-            inverse = [t + dot(t.astype(BF16), p.astype(BF16)) for t, p in zip(inverse, power)]
-            span *= 2
-        for small, large in zip(same[:-1], same[1:]):
-            low = [t.astype(BF16) for t in inverse]
-            step = [dot(jnp.where(large & ~small, l, 0.0).astype(BF16), t) for l, t in zip(lower, low)]
-            inverse = [t - dot(b, s.astype(BF16)) for t, b, s in zip(inverse, low, step)]
+        power = [square(p.astype(BF16)).astype(BF16) for p in power]
+        inverse = doubled(power, inverse, BASE * NH)
+        low = [t.astype(BF16) for t in inverse]
+        power = [
+            -dot(t[:, :SUB], jnp.where(near, 0.0, l).astype(BF16)) for t, l in zip(low, lower)
+        ]
+        power = [p.astype(BF16) for p in power]
+        stepped = [both(p, t) for p, t in zip(power, inverse)]
+        inverse = doubled([p for p, _ in stepped], [t for _, t in stepped], CH // BASE)
         high = [split(t) for t in inverse]
-        error = [eye - t - dot3(split(l), s) for t, l, s in zip(inverse, lower, high)]
-        inverse = [t + dot(s[0], e.astype(BF16)) for t, s, e in zip(inverse, high, error)]
-        solved = [dot(t.astype(BF16), rhs[i]).astype(BF16) for i, t in zip(at, inverse)]
-        change = [dot(k[0], s, ((0,), (0,))) for k, s in zip(ks, solved)]
+        parts = [split(l) for l in lower]
+        made = [dot(l[0][:, :SUB], jnp.concatenate([s[0], s[1]], 1)) for l, s in zip(parts, high)]
+        rest = [dot(l[1][:, :SUB], s[0]) for l, s in zip(parts, high)]
+        error = [eye - t - (m[:, :WIDE] + (m[:, WIDE:] + r)) for t, m, r in zip(inverse, made, rest)]
+        inverse = [t + dot(s[0][:, :SUB], e.astype(BF16)) for t, s, e in zip(inverse, high, error)]
+        solved = [dot(t[:, :SUB].astype(BF16), rhs[i]).astype(BF16) for i, t in zip(at, inverse)]
+        change = [dot(k[:SUB], s, ((0,), (0,))) for k, s in zip(pairs, solved)]
         qs = [queries[i] for i in at]
-        attend = [jnp.where(seen, dot(q.astype(BF16), k[0], ((1,), (1,))), 0.0).astype(BF16) for q, k in zip(qs, ks)]
+        attend = [jnp.where(seen, dot(q.astype(BF16), k[:SUB], ((1,), (1,))), 0.0).astype(BF16) for q, k in zip(qs, pairs)]
         effect = [dot(a, s) for a, s in zip(attend, solved)]
         for i, g, q, e in zip(at, change, qs, effect):
             state_map[i + (slice(0, CH),)] = (q - e[:, :DK]).astype(BF16)
@@ -216,7 +242,7 @@
         in_specs=[pl.BlockSpec(memory_space=pltpu.SMEM)] + [vmem] * 11,
         out_specs=[vmem] * count,
         scratch_shapes=[
-            pltpu.VMEM((heads, blocks, SUB, DK), F32),
+            pltpu.VMEM((heads, blocks, 2 * WIDE, DK), BF16),
             pltpu.VMEM((heads, blocks, SUB, DK), F32),
             pltpu.VMEM((heads, blocks, SUB, 2 * DK), BF16),
             pltpu.VMEM((heads, blocks, CH, DK), F32),

time: 99.5 us -> 98.7 us (level)
  no operation moved by 1% of the time
where the time goes in v3:
time: 98.7 us; the launch traced here: 98.5 us
  blocking collectives  46.2 us (47%)
  Pallas kernels  26.3 us (27%)
  waiting for transfers between devices  16.2 us (16%)
  starting transfers between devices  9.02 us (9%)
    all_to_all x1, blocking collectives, shards(): lax.all_to_all(outgoing, 'dp', split_axis=0, concat_axis=0, tiled=True)  25.5 us
    all_to_all x1, blocking collectives, shards(): lax.all_to_all(result.reshape(owners, -1, width), 'dp', split_axis=0, con...  20.7 us
    ppermute x6, waiting for transfers between devices, turned(): return lax.ppermute(x, axis, [(i, (i + k) % size) for i in range(size)])  16.2 us
    pallas_call x1, Pallas kernels, experts_here(): pl.pallas_call(expert_kernel, out_shape=[jax.ShapeDtypeStruct(rows.shape,...  12.6 us
    ppermute x6, starting transfers between devices, turned(): return lax.ppermute(x, axis, [(i, (i + k) % size) for i in range(size)])  9.02 us
    pallas_call x1, Pallas kernels, mixer(): pl.pallas_call(lambda *refs: mixer_kernel(heads, shift, *refs), out_shape...  5.79 us
    pallas_call x1, Pallas kernels, first(): pl.pallas_call(first_kernel, out_shape=[pltpu.VMEM(w.shape, w.dtype) for...  4.29 us
  transfers between devices with their start and end apart: 6, of which 4 were waited for; matrix products, arithmetic and copies ran while one was open for 1% of the time, Pallas kernels for 6%

profile of v3, /device:TPU:1, one launch (start us, length us, event | category | flops | bytes accessed | tf_op | source)
XLA Modules:
  0.0 98.5 jit_solution(9205290403854947322)
XLA Ops:
  0.0 2.5 %collective-permute-start.2 = (bf16[256,512]{1,0:T(8,128)(2,1)}, bf16[256,512]{1,0:T(8,128)(2,1)S(1)}, u32[]{:S(2)}, u32[]{:S(2)}) collective-permute-start(bf16[256,512]{1,0:T(8,128)(2,1)} %refs_0_.1), channel_id=1, source_target_pairs={{0,1},{1,2},{2,3},{3,0},{4,5},{5,6},{6,7},{7,4},{8,9},{9,10},{10,1... | collective-permute-start | bytes 786440 | tf_op jit(solution)/shard_map/ppermute | solution.py:440
  2.5 2.1 %collective-permute-start.1 = (bf16[256,512]{1,0:T(8,128)(2,1)}, bf16[256,512]{1,0:T(8,128)(2,1)S(1)}, u32[]{:S(2)}, u32[]{:S(2)}) collective-permute-start(bf16[256,512]{1,0:T(8,128)(2,1)} %refs_0_.1), channel_id=1, source_target_pairs={{0,3},{1,0},{2,1},{3,2},{4,7},{5,4},{6,5},{7,6},{8,11},{9,8},{10,9... | collective-permute-start | bytes 786440 | tf_op jit(solution)/shard_map/ppermute | solution.py:440
  4.6 1.3 %collective-permute-start = (bf16[256,512]{1,0:T(8,128)(2,1)}, bf16[256,512]{1,0:T(8,128)(2,1)S(1)}, u32[]{:S(2)}, u32[]{:S(2)}) collective-permute-start(bf16[256,512]{1,0:T(8,128)(2,1)} %refs_0_.1), channel_id=1, source_target_pairs={{0,2},{1,3},{2,0},{3,1},{4,6},{5,7},{6,4},{7,5},{8,10},{9,11},{10,... | collective-permute-start | bytes 786440 | tf_op jit(solution)/shard_map/ppermute | solution.py:440
  5.9 0.7 reshape.25.gain_ref.refs_1_
  6.6 4.3 %first.1 = (bf16[256,512]{1,0:T(8,128)(2,1)S(1)}, bf16[2048,256]{1,0:T(8,128)(2,1)S(1)}, bf16[3,2048,256]{2,1,0:T(8,128)(2,1)S(1)}, bf16[3,2048,256]{2,1,0:T(8,1...) custom-call(s32[1]{0:T(128)} %bitcast.place_ref.refs_0_, ...), custom_call_target="tpu_custom_call" | custom-call | flops 2000000000 | bytes 1000000 | tf_op jit(solution)/shard_map/first/pallas_call | solution.py:81
  10.9 0.0 collective-permute-done.2.refs_2_.x1
  10.9 0.9 more.2
  11.8 0.0 collective-permute-done.1.refs_2_.x3
  11.8 0.8 more.3
  12.6 4.7 %collective-permute-done.refs_2_.x2 = bf16[256,512]{1,0:T(8,128)(2,1)S(1)} collective-permute-done((bf16[256,512]{1,0:T(8,128)(2,1)}, bf16[256,512]{1,0:T(8,128)(2,1)S(1)}, u32[]{:S(2)}, u32[]{:S(2)}) %collective-permute-start) | collective-permute-done | bytes 262176 | tf_op jit(solution)/shard_map/ppermute | solution.py:440
  17.3 0.0 copy-start.1
  17.3 0.0 copy-start.2
  17.3 5.8 %mixer.1 = (bf16[64,2048]{1,0:T(8,128)(2,1)S(1)}, bf16[64,2048]{1,0:T(8,128)(2,1)S(1)}, bf16[64,2048]{1,0:T(8,128)(2,1)S(1)}, bf16[64,2048]{1,0:T(8,128)(2,1)S(1)}) custom-call(s32[1]{0:T(128)} %bitcast.place_ref.refs_0_, f32[4,512]{1,0:T(4,128)S(1)} %reshape.25.gain_ref.refs_1_, bf16[256,512]{1,0:T(8,128)(2,1)S(1)} %collective-permute-done.refs_2_.x2, ...), custom_call_target="tpu_custom_call" | custom-call | flops 20000000000 | bytes 10000000 | tf_op jit(solution)/shard_map/mixer/pallas_call | solution.py:239
  23.1 0.0 copy-start
  23.1 0.7 collective-permute-start.3
  23.8 1.3 %collective-permute-start.4 = (bf16[64,2048]{1,0:T(8,128)(2,1)S(1)}, bf16[64,2048]{1,0:T(8,128)(2,1)S(1)}, u32[]{:S(2)}, u32[]{:S(2)}) collective-permute-start(bf16[64,2048]{1,0:T(8,128)(2,1)S(1)} %get-tuple-element.48), channel_id=1, source_target_pairs={{0,2},{1,3},{2,0},{3,1},{4,6},{5,7},{6,4},{7,5},{8,10},{9,11},{10,... | collective-permute-start | bytes 786440 | tf_op jit(solution)/shard_map/ppermute | solution.py:440
  25.1 1.2 %collective-permute-start.5 = (bf16[64,2048]{1,0:T(8,128)(2,1)S(1)}, bf16[64,2048]{1,0:T(8,128)(2,1)S(1)}, u32[]{:S(2)}, u32[]{:S(2)}) collective-permute-start(bf16[64,2048]{1,0:T(8,128)(2,1)S(1)} %get-tuple-element.49), channel_id=1, source_target_pairs={{0,3},{1,0},{2,1},{3,2},{4,7},{5,4},{6,5},{7,6},{8,11},{9,8},{10,9... | collective-permute-start | bytes 786440 | tf_op jit(solution)/shard_map/ppermute | solution.py:440
  26.3 6.9 %collective-permute-done.3.p1 = bf16[64,2048]{1,0:T(8,128)(2,1)S(1)} collective-permute-done((bf16[64,2048]{1,0:T(8,128)(2,1)S(1)}, bf16[64,2048]{1,0:T(8,128)(2,1)S(1)}, u32[]{:S(2)}, u32[]{:S(2)}) %collective-permute-start.3) | collective-permute-done | bytes 262176 | tf_op jit(solution)/shard_map/ppermute | solution.py:440
  33.2 0.5 collective-permute-done.4.p2
  33.6 4.2 %collective-permute-done.5.p3 = bf16[64,2048]{1,0:T(8,128)(2,1)S(1)} collective-permute-done((bf16[64,2048]{1,0:T(8,128)(2,1)S(1)}, bf16[64,2048]{1,0:T(8,128)(2,1)S(1)}, u32[]{:S(2)}, u32[]{:S(2)}) %collective-permute-start.5) | collective-permute-done | bytes 262176 | tf_op jit(solution)/shard_map/ppermute | solution.py:440
  37.8 0.0 copy-done.1
  37.8 0.0 copy-done.2
  37.8 0.9 route.1
  38.7 25.5 %all_to_all.10 = bf16[32,8,2048]{2,1,0:T(8,128)(2,1)S(1)} all-to-all(bf16[32,8,2048]{2,1,0:T(8,128)(2,1)S(1)} %bitcast.11), channel_id=1, replica_groups=mesh['dp'=32,'head'=4] {'dp'}, dimensions={0} | all-to-all | bytes 2097152 | tf_op jit(solution)/shard_map/all_to_all | solution.py:464
  64.2 0.0 copy-done
  64.2 12.6 %experts.1 = (bf16[256,2048]{1,0:T(8,128)(2,1)S(1)}, bf16[128,256]{1,0:T(8,128)(2,1)S(1)}, f32[64,128]{1,0:T(8,128)S(1)}) custom-call(bf16[256,2048]{1,0:T(8,128)(2,1)S(1)} %bitcast.10, bf16[2,2048,1408]{2,1,0:T(8,128)(2,1)} %gate_hbm.1, bf16[2,2048,1408]{2,1,0:T(8,128)(2,1)} %up_hbm.1, bf16[2,1408,2048]{2,1,0:T(8,128)(2,1)} %down_hbm.1, ...), custom_call_target="tpu_custom_call" | custom-call | flops 5000000000 | bytes 10000000 | tf_op jit(solution)/shard_map/experts/pallas_call | solution.py:394
  76.8 20.7 %all_to_all.11 = bf16[32,8,2048]{2,1,0:T(8,128)(2,1)S(1)} all-to-all(bf16[32,8,2048]{2,1,0:T(8,128)(2,1)S(1)} %bitcast.13), channel_id=1, replica_groups=mesh['dp'=32,'head'=4] {'dp'}, dimensions={0} | all-to-all | bytes 2097152 | tf_op jit(solution)/shard_map/all_to_all | solution.py:468
  97.5 1.0 %combine.1 = bf16[64,2048]{1,0:T(8,128)(2,1)} custom-call(f32[64,2048]{1,0:T(8,128)S(1)} %get-tuple-element.51.residual_ref, f32[64,128]{1,0:T(8,128)S(1)} %get-tuple-element.54.leading_ref, bf16[128,256]{1,0:T(8,128)(2,1)S(1)} %get-tuple-element.55.pick_ref, bf16[256,2048]{1,0:T(8,128)(2,1)S(1)} %bitcast.12), custom_call_target="tpu_custom_call" | custom-call | flops 1000000000 | bytes 1000000 | tf_op jit(solution)/shard_map/combine/pallas_call | solution.py:427
Async XLA Ops:
  0.0 10.9 %collective-permute-start.2 = (bf16[256,512]{1,0:T(8,128)(2,1)}, bf16[256,512]{1,0:T(8,128)(2,1)S(1)}, u32[]{:S(2)}, u32[]{:S(2)}) collective-permute-start(bf16[256,512]{1,0:T(8,128)(2,1)} %refs_0_.1), channel_id=1, source_target_pairs={{0,1},{1,2},{2,3},{3,0},{4,5},{5,6},{6,7},{7,4},{8,9},{9,10},{10,1... | collective-permute-start | bytes 786440 | tf_op jit(solution)/shard_map/ppermute | solution.py:440
  2.5 9.3 %collective-permute-start.1 = (bf16[256,512]{1,0:T(8,128)(2,1)}, bf16[256,512]{1,0:T(8,128)(2,1)S(1)}, u32[]{:S(2)}, u32[]{:S(2)}) collective-permute-start(bf16[256,512]{1,0:T(8,128)(2,1)} %refs_0_.1), channel_id=1, source_target_pairs={{0,3},{1,0},{2,1},{3,2},{4,7},{5,4},{6,5},{7,6},{8,11},{9,8},{10,9... | collective-permute-start | bytes 786440 | tf_op jit(solution)/shard_map/ppermute | solution.py:440
  4.6 12.7 %collective-permute-start = (bf16[256,512]{1,0:T(8,128)(2,1)}, bf16[256,512]{1,0:T(8,128)(2,1)S(1)}, u32[]{:S(2)}, u32[]{:S(2)}) collective-permute-start(bf16[256,512]{1,0:T(8,128)(2,1)} %refs_0_.1), channel_id=1, source_target_pairs={{0,2},{1,3},{2,0},{3,1},{4,6},{5,7},{6,4},{7,5},{8,10},{9,11},{10,... | collective-permute-start | bytes 786440 | tf_op jit(solution)/shard_map/ppermute | solution.py:440
  17.3 20.5 %copy-start.1 = (s32[64,2]{0,1:T(2,128)S(1)}, s32[64,2]{0,1:T(2,128)}, u32[]{:S(2)}) copy-start(s32[64,2]{0,1:T(2,128)} %param.24) | copy-start | bytes 1540
  17.3 20.5 %copy-start.2 = (f32[2048]{0:T(1024)S(1)}, f32[2048]{0:T(1024)}, u32[]{:S(2)}) copy-start(f32[2048]{0:T(1024)} %param.22) | copy-start | bytes 24580
  23.1 41.1 %copy-start = (f32[2048,64]{0,1:T(8,128)S(1)}, f32[2048,64]{0,1:T(8,128)}, u32[]{:S(2)}) copy-start(f32[2048,64]{0,1:T(8,128)} %param.23) | copy-start | bytes 1572868
  23.1 10.1 %collective-permute-start.3 = (bf16[64,2048]{1,0:T(8,128)(2,1)S(1)}, bf16[64,2048]{1,0:T(8,128)(2,1)S(1)}, u32[]{:S(2)}, u32[]{:S(2)}) collective-permute-start(bf16[64,2048]{1,0:T(8,128)(2,1)S(1)} %get-tuple-element.47), channel_id=1, source_target_pairs={{0,1},{1,2},{2,3},{3,0},{4,5},{5,6},{6,7},{7,4},{8,9},{9,10},{10,1... | collective-permute-start | bytes 786440 | tf_op jit(solution)/shard_map/ppermute | solution.py:440
  23.8 9.9 %collective-permute-start.4 = (bf16[64,2048]{1,0:T(8,128)(2,1)S(1)}, bf16[64,2048]{1,0:T(8,128)(2,1)S(1)}, u32[]{:S(2)}, u32[]{:S(2)}) collective-permute-start(bf16[64,2048]{1,0:T(8,128)(2,1)S(1)} %get-tuple-element.48), channel_id=1, source_target_pairs={{0,2},{1,3},{2,0},{3,1},{4,6},{5,7},{6,4},{7,5},{8,10},{9,11},{10,... | collective-permute-start | bytes 786440 | tf_op jit(solution)/shard_map/ppermute | solution.py:440
  25.1 12.7 %collective-permute-start.5 = (bf16[64,2048]{1,0:T(8,128)(2,1)S(1)}, bf16[64,2048]{1,0:T(8,128)(2,1)S(1)}, u32[]{:S(2)}, u32[]{:S(2)}) collective-permute-start(bf16[64,2048]{1,0:T(8,128)(2,1)S(1)} %get-tuple-element.49), channel_id=1, source_target_pairs={{0,3},{1,0},{2,1},{3,2},{4,7},{5,4},{6,5},{7,6},{8,11},{9,8},{10,9... | collective-permute-start | bytes 786440 | tf_op jit(solution)/shard_map/ppermute | solution.py:440

commit v4 on v3

--- a/solution.py
+++ b/solution.py
@@ -90,9 +90,9 @@
     )(me, gain, *[pltpu.with_memory_space_constraint(w, pltpu.HBM) for w in moved])
 
 
-def more_kernel(shift, place_ref, gain_ref, x_ref, wq_ref, wk_ref, wv_ref, wb_ref, sums_ref, beta_ref, square_ref,
+def more_kernel(place_ref, gain_ref, x_ref, wq_ref, wk_ref, wv_ref, wb_ref, sums_ref, beta_ref, square_ref,
                 new_sums_ref, new_beta_ref, new_square_ref):
-    source = (place_ref[0] + (gain_ref.shape[0] - shift)) % gain_ref.shape[0]
+    source = place_ref[1]
     x, square = gained(x_ref, gain_ref, source)
     new_square_ref[...] = square_ref[...] + square
     for i, product in enumerate(products(x, source, wq_ref, wk_ref, wv_ref, wb_ref)):
@@ -102,10 +102,10 @@
             new_beta_ref[...] = beta_ref[...] + product
 
 
-def more(shift, me, gain, x, weights, sums):
-    vmem = pl.BlockSpec(memory_space=pltpu.VMEM)
-    return pl.pallas_call(
-        lambda *refs: more_kernel(shift, *refs),
+def more(me, gain, x, weights, sums):
+    vmem = pl.BlockSpec(memory_space=pltpu.VMEM)
+    return pl.pallas_call(
+        more_kernel,
         out_shape=[pltpu.VMEM(a.shape, a.dtype) for a in sums],
         in_specs=[pl.BlockSpec(memory_space=pltpu.SMEM)] + [vmem] * 9,
         out_specs=[vmem] * 3,
@@ -116,17 +116,18 @@
     )(me, gain, x, *weights, *sums)
 
 
-def mixer_kernel(heads, shift, place_ref, gain_ref, x_ref, wq_ref, wk_ref, wv_ref, wb_ref, sums_ref, beta_ref, square_ref,
+def mixer_kernel(heads, place_ref, gain_ref, x2, x3, wq_ref, wk_ref, wv_ref, wb_ref, sums_ref, beta_ref, square_ref,
                  head_gain_ref, wo_ref, o0, o1, o2, o3, keys, beta_keys, rhs, queries, state_map, added, out_add, mixed):
-    me = place_ref[0]
     count, part = gain_ref.shape
-    length = x_ref.shape[0]
-    source = lax.rem(me + (count - shift), count)
-    x, square = gained(x_ref, gain_ref, source)
-    scale = lax.rsqrt((square_ref[...] + square) / (count * part) + EPSILON)
-    last = products(x, source, wq_ref, wk_ref, wv_ref, wb_ref)
-    whole = [(sums_ref[i] + next(last)) * scale for i in range(1 + 2 * NH)]
-    beta = (beta_ref[...] + next(last)) * scale
+    length = x2.shape[0]
+    total, last = square_ref[...], []
+    for x_ref, source in ((x2, place_ref[2]), (x3, place_ref[3])):
+        x, square = gained(x_ref, gain_ref, source)
+        total = total + square
+        last.append(products(x, source, wq_ref, wk_ref, wv_ref, wb_ref))
+    scale = lax.rsqrt(total / (count * part) + EPSILON)
+    whole = [(sums_ref[i] + (next(last[0]) + next(last[1]))) * scale for i in range(1 + 2 * NH)]
+    beta = (beta_ref[...] + (next(last[0]) + next(last[1]))) * scale
     beta = 2.0 / (1.0 + jnp.exp(-beta))
     blocks = length // CH
     query = whole[0]
@@ -220,7 +221,7 @@
             out = out * lax.rsqrt(jnp.mean(out * out, -1, keepdims=True) + EPSILON) * head_gain_ref[...]
             mixed[c * CH:(c + 1) * CH, h * DK:(h + 1) * DK] = out.astype(BF16)
     own = length // count
-    rolled = jnp.concatenate([mixed[rows_at(lax.rem(me + k, count), own), :] for k in range(count)], 0)
+    rolled = jnp.concatenate([mixed[rows_at(place_ref[k], own), :] for k in range(count)], 0)
     result = dot(rolled, wo_ref[...]).astype(BF16)
     for k, o in enumerate((o0, o1, o2, o3)):
         o[...] = result[k * own:(k + 1) * own]
@@ -229,17 +230,17 @@
 UNROLL = 8
 
 
-def mixer(me, gain, x, shift, weights, sums, head_gain, wo):
+def mixer(me, gain, x2, x3, weights, sums, head_gain, wo):
     count = gain.shape[0]
-    length = x.shape[0]
+    length = x2.shape[0]
     heads = weights[0].shape[1] // DK
     blocks = length // CH
     own = length // count
     vmem = pl.BlockSpec(memory_space=pltpu.VMEM)
     return pl.pallas_call(
-        lambda *refs: mixer_kernel(heads, shift, *refs),
+        lambda *refs: mixer_kernel(heads, *refs),
         out_shape=[jax.ShapeDtypeStruct((own, wo.shape[1]), BF16)] * count,
-        in_specs=[pl.BlockSpec(memory_space=pltpu.SMEM)] + [vmem] * 11,
+        in_specs=[pl.BlockSpec(memory_space=pltpu.SMEM)] + [vmem] * 12,
         out_specs=[vmem] * count,
         scratch_shapes=[
             pltpu.VMEM((heads, blocks, 2 * WIDE, DK), BF16),
@@ -254,63 +255,80 @@
         compiler_params=pltpu.CompilerParams(vmem_limit_bytes=32 * MIB),
         cost_estimate=pl.CostEstimate(flops=2 * 10 ** 10, bytes_accessed=10 ** 7, transcendentals=0),
         name="mixer",
-    )(me, gain, x, *weights, *sums, head_gain, wo)
-
-
-def slots(ids_ref, experts, capacity):
+    )(me, gain, x2, x3, *weights, *sums, head_gain, wo)
+
+
+def slots(ids_ref, experts, total):
     tokens = ids_ref.shape[1]
+    capacity = total // experts
     label = iota((experts, tokens), 0)
     chosen = [(label == ids_ref[k:k + 1, :]).astype(F32) for k in range(2)]
     count = chosen[0] + chosen[1]
     before = (iota((tokens, tokens), 0) < iota((tokens, tokens), 1)).astype(BF16)
     earlier = dot(count.astype(BF16), before)
-    total = experts * capacity
     spread = (iota((total, experts), 0) // capacity == iota((total, experts), 1)).astype(BF16)
     place = dot(spread, earlier.astype(BF16))
     fits = place == (iota((total, tokens), 0) % capacity).astype(F32)
     return chosen, [jnp.where(fits, dot(spread, c.astype(BF16)), 0.0) for c in chosen]
 
 
-def route_kernel(place_ref, p0, p1, p2, p3, x0, x1, x2, x3, gain_ref, ids_ref, residual_ref, routed_ref, send_ref):
-    me = place_ref[0]
-    xs = (x0, x1, x2, x3)
-    count = len(xs)
-    own, part = p0.shape[0], x0.shape[1]
-    for k in range(count):
-        columns = rows_at(lax.rem(me - k + count, count), part)
-        residual_ref[:, columns] = xs[k][rows_at(me, own), :].astype(F32)
-    arrived = [p[...].astype(F32) for p in (p0, p1, p2, p3)]
-    residual = residual_ref[...] + ((arrived[0] + arrived[1]) + (arrived[2] + arrived[3]))
+def ready_kernel(experts, place_ref, part_ref, x0, x1, x2, x3, ids_ref, base_ref, chosen_ref):
+    own, part = part_ref.shape[0], x0.shape[1]
+    for k, x in enumerate((x0, x1, x2, x3)):
+        columns = rows_at(place_ref[k], part)
+        base_ref[:, columns] = x[rows_at(place_ref[0], own), :].astype(F32)
+    base_ref[...] = base_ref[...] + part_ref[...].astype(F32)
+    _, chosen = slots(ids_ref, experts, chosen_ref.shape[0])
+    chosen_ref[...] = (chosen[0] + chosen[1]).astype(BF16)
+
+
+def ready(me, part, xs, ids, experts, capacity):
+    own, width = part.shape
+    vmem = pl.BlockSpec(memory_space=pltpu.VMEM)
+    return pl.pallas_call(
+        lambda *refs: ready_kernel(experts, *refs),
+        out_shape=[
+            jax.ShapeDtypeStruct((own, width), F32),
+            jax.ShapeDtypeStruct((experts * capacity, own), BF16),
+        ],
+        in_specs=[pl.BlockSpec(memory_space=pltpu.SMEM)] + [vmem] * 6,
+        out_specs=[vmem] * 2,
+        compiler_params=pltpu.CompilerParams(vmem_limit_bytes=8 * MIB),
+        cost_estimate=pl.CostEstimate(flops=2 * 10 ** 9, bytes_accessed=10 ** 6, transcendentals=0),
+        name="ready",
+    )(me, part, *xs, ids)
+
+
+def route_kernel(base_ref, p1, p2, p3, gain_ref, chosen_ref, residual_ref, routed_ref, send_ref):
+    arrived = [p[...].astype(F32) for p in (p1, p2, p3)]
+    residual = (base_ref[...] + arrived[0]) + (arrived[1] + arrived[2])
     residual_ref[...] = residual
     mean = jnp.mean(residual * residual, -1, keepdims=True)
     routed = residual * lax.rsqrt(mean + EPSILON) * gain_ref[...]
     routed_ref[...] = routed
-    _, chosen = slots(ids_ref, 64, send_ref.shape[0] // 64)
-    chosen = (chosen[0] + chosen[1]).astype(BF16)
-    send_ref[...] = dot(chosen, routed.astype(BF16)).astype(BF16)
-
-
-def route(me, parts, xs, gain, ids, experts, capacity):
-    own, width = parts[0].shape
+    send_ref[...] = dot(chosen_ref[...], routed.astype(BF16)).astype(BF16)
+
+
+def route(base, parts, gain, chosen):
+    own, width = base.shape
     vmem = pl.BlockSpec(memory_space=pltpu.VMEM)
     return pl.pallas_call(
         route_kernel,
         out_shape=[
             jax.ShapeDtypeStruct((own, width), F32),
             jax.ShapeDtypeStruct((own, width), F32),
-            jax.ShapeDtypeStruct((experts * capacity, width), BF16),
+            jax.ShapeDtypeStruct((chosen.shape[0], width), BF16),
         ],
-        in_specs=[pl.BlockSpec(memory_space=pltpu.SMEM)] + [vmem] * 10,
+        in_specs=[vmem] * 6,
         out_specs=[vmem] * 3,
-        compiler_params=pltpu.CompilerParams(vmem_limit_bytes=16 * MIB),
+        compiler_params=pltpu.CompilerParams(vmem_limit_bytes=8 * MIB),
         cost_estimate=pl.CostEstimate(flops=10 ** 9, bytes_accessed=10 ** 7, transcendentals=0),
         name="route",
-    )(me, *parts, *xs, gain, ids)
+    )(base, *parts, gain, chosen)
 
 
 def weigh(routed_ref, router_ref, ids_ref, pick_ref, leading_ref):
-    experts = router_ref.shape[0]
-    chosen, parts = slots(ids_ref, experts, pick_ref.shape[1] // experts)
+    chosen, parts = slots(ids_ref, router_ref.shape[0], pick_ref.shape[1])
     tokens = routed_ref.shape[0]
     for k in range(2):
         pick_ref[k * tokens:(k + 1) * tokens, :] = jnp.transpose(parts[k]).astype(BF16)
@@ -323,8 +341,8 @@
     leading_ref[...] = jnp.transpose(jnp.broadcast_to(leading, (128, tokens)))
 
 
-def expert_kernel(rows_ref, gate_hbm, up_hbm, down_hbm, routed_ref, router_ref, ids_ref, out_ref, pick_ref, leading_ref,
-                  gate_ref, up_ref, down_ref, hidden_ref, finished_ref, sems):
+def expert_kernel(rows_ref, gate_hbm, up_hbm, down_hbm, routed_ref, router_ref, ids_ref, out_ref, pick_ref,
+                  leading_ref, gate_ref, up_ref, down_ref, hidden_ref, finished_ref, sems):
     total = rows_ref.shape[0]
     here, width, middle = gate_hbm.shape
     per = total // here
@@ -435,38 +453,59 @@
     )(residual, leading, pick, back)
 
 
-def turned(x, k, axis):
-    size = lax.axis_size(axis)
-    return lax.ppermute(x, axis, [(i, (i + k) % size) for i in range(size)])
+def swapped(x, step, axes=("dp", "head")):
+    owners, peers = (lax.axis_size(a) for a in axes)
+    pairs = [(d * peers + z, d * peers + (z ^ step(d))) for d in range(owners) for z in range(peers)]
+    return lax.ppermute(x, axes, pairs)
+
+
+def near(owner):
+    return 1 if owner >= EDGE else 3
+
+
+def far(owner):
+    return 3 if owner >= EDGE else 1
+
+
+def across(owner):
+    return 2
+
+
+EDGE = 8
+STEPS = (near, far, across)
 
 
 def shards(tokens, mixer_gain, query_weight, key_weight, value_weight, beta_weight, head_gain, output_weight,
            expert_gain, router_weight, expert_ids, gate_weight, up_weight, down_weight):
-    peers = lax.axis_size("head")
     owners = lax.axis_size("dp")
-    me = lax.axis_index("head").reshape(1).astype(jnp.int32)
-    xs = [tokens] + [turned(tokens, k, "head") for k in range(1, peers)]
-    gain = mixer_gain.reshape(peers, -1)
+    me = lax.axis_index("head").astype(jnp.int32)
+    edge = lax.axis_index("dp") < EDGE
+    one, three = jnp.where(edge, 3, 1), jnp.where(edge, 1, 3)
+    me = jnp.stack([me, me ^ one, me ^ three, me ^ 2]).astype(jnp.int32)
+    xs = [tokens] + [swapped(tokens, step) for step in STEPS]
+    gain = mixer_gain.reshape(lax.axis_size("head"), -1)
     here = first(me, gain, tokens, query_weight, key_weight, value_weight, beta_weight.T, head_gain.reshape(1, -1),
                  output_weight)
     xs[0], weights, sums = here[0], here[1:5], here[7:]
-    for shift in (1, 3):
-        sums = more(shift, me, gain, xs[shift], weights, sums)
-    parts = mixer(me, gain, xs[2], 2, weights, sums, here[5], here[6])
-    parts = [parts[0]] + [turned(parts[k], k, "head") for k in range(1, peers)]
+    sums = more(me, gain, xs[1], weights, sums)
+    parts = mixer(me, gain, xs[2], xs[3], weights, sums, here[5], here[6])
+    arriving = [swapped(part, step) for part, step in zip(parts[1:], STEPS)]
     experts = router_weight.shape[1]
-    own = parts[0].shape[0]
-    capacity = 4 * own // experts
+    capacity = 4 * parts[0].shape[0] // experts
     ids = expert_ids.T
-    residual, routed, outgoing = route(me, parts, xs, expert_gain.reshape(1, -1), ids, experts, capacity)
+    base, chosen = ready(me, parts[0], xs, ids, experts, capacity)
+    residual, routed, outgoing = route(base, arriving, expert_gain.reshape(1, -1), chosen)
     width = outgoing.shape[1]
-    outgoing = outgoing.reshape(owners, -1, width)
-    arrived = lax.all_to_all(outgoing, "dp", split_axis=0, concat_axis=0, tiled=True)
+
+    def exchanged(rows):
+        rows = rows.reshape(owners, -1, width)
+        rows = lax.all_to_all(rows, "dp", split_axis=0, concat_axis=0, tiled=True)
+        return rows.reshape(-1, width)
+
     result, pick, leading = experts_here(
-        arrived.reshape(-1, width), gate_weight, up_weight, down_weight, routed, router_weight.T, ids
+        exchanged(outgoing), gate_weight, up_weight, down_weight, routed, router_weight.T, ids
     )
-    back = lax.all_to_all(result.reshape(owners, -1, width), "dp", split_axis=0, concat_axis=0, tiled=True)
-    return combine(residual, leading, pick, back.reshape(-1, width))
+    return combine(residual, leading, pick, exchanged(result))
 
 
 def solution(mesh):

time: 98.7 us -> 99 us (level)
  waiting for transfers between devices: 16.2 us -> 13.7 us
  Pallas kernels: 26.3 us -> 28.3 us
    ppermute x6, waiting for transfers between devices: 16.2 us -> 13.7 us  [swapped(): return lax.ppermute(x, axes, pairs)]
    pallas_call x3, Pallas kernels: 7.49 us -> 9.11 us  [the longest x1 6.79 us: mixer(): pl.pallas_call(lambda *refs: mixer_kernel(heads, *refs), out_shape=[jax.S...]
  transfers between devices with their start and end apart: 6 -> 6, of which waited for: 4 -> 4; matrix products, arithmetic and copies ran while one was open for 1% -> 1% of each run, Pallas kernels for 6% -> 7%
where the time goes in v4:
time: 99 us; the launch traced here: 98.7 us
  blocking collectives  46.2 us (47%)
  Pallas kernels  28.3 us (29%)
  waiting for transfers between devices  13.7 us (14%)
  starting transfers between devices  9.7 us (10%)
    all_to_all x2, blocking collectives, exchanged(): rows = lax.all_to_all(rows, 'dp', split_axis=0, concat_axis=0, tiled=True)  46.2 us
    ppermute x6, waiting for transfers between devices, swapped(): return lax.ppermute(x, axes, pairs)  13.7 us
    pallas_call x1, Pallas kernels, experts_here(): pl.pallas_call(expert_kernel, out_shape=[jax.ShapeDtypeStruct(rows.shape,...  12.6 us
    ppermute x6, starting transfers between devices, swapped(): return lax.ppermute(x, axes, pairs)  9.7 us
    pallas_call x1, Pallas kernels, mixer(): pl.pallas_call(lambda *refs: mixer_kernel(heads, *refs), out_shape=[jax.S...  6.79 us
    pallas_call x1, Pallas kernels, first(): pl.pallas_call(first_kernel, out_shape=[pltpu.VMEM(w.shape, w.dtype) for...  4.84 us
  transfers between devices with their start and end apart: 6, of which 4 were waited for; matrix products, arithmetic and copies ran while one was open for 1% of the time, Pallas kernels for 7%

profile of v4, /device:TPU:1, one launch (start us, length us, event | category | flops | bytes accessed | tf_op | source)
XLA Modules:
  0.0 98.7 jit_solution(12388691610872918291)
XLA Ops:
  0.0 4.6 %collective-permute-start.2 = (bf16[256,512]{1,0:T(8,128)(2,1)}, bf16[256,512]{1,0:T(8,128)(2,1)S(1)}, u32[]{:S(2)}, u32[]{:S(2)}) collective-permute-start(bf16[256,512]{1,0:T(8,128)(2,1)} %refs_0_.1), channel_id=1, source_target_pairs={{0,3},{1,2},{2,1},{3,0},{4,7},{5,6},{6,5},{7,4},{8,11},{9,10},{10,... | collective-permute-start | bytes 786440 | tf_op jit(solution)/shard_map/ppermute | solution.py:459
  4.6 0.0 collective-permute-start
  4.6 1.2 %collective-permute-start.1 = (bf16[256,512]{1,0:T(8,128)(2,1)}, bf16[256,512]{1,0:T(8,128)(2,1)S(1)}, u32[]{:S(2)}, u32[]{:S(2)}) collective-permute-start(bf16[256,512]{1,0:T(8,128)(2,1)} %refs_0_.1), channel_id=1, source_target_pairs={{0,2},{1,3},{2,0},{3,1},{4,6},{5,7},{6,4},{7,5},{8,10},{9,11},{10,... | collective-permute-start | bytes 786440 | tf_op jit(solution)/shard_map/ppermute | solution.py:459
  5.8 0.7 reshape.21.gain_ref.refs_1_
  6.5 0.1 pad_add_fusion.place_ref.refs_0_
  6.5 4.8 %first.1 = (bf16[256,512]{1,0:T(8,128)(2,1)S(1)}, bf16[2048,256]{1,0:T(8,128)(2,1)S(1)}, bf16[3,2048,256]{2,1,0:T(8,128)(2,1)S(1)}, bf16[3,2048,256]{2,1,0:T(8,1...) custom-call(s32[4]{0:T(128)S(1)} %pad_add_fusion.place_ref.refs_0_, ...), custom_call_target="tpu_custom_call" | custom-call | flops 2000000000 | bytes 1000000 | tf_op jit(solution)/shard_map/first/pallas_call | solution.py:81
  11.4 0.0 collective-permute-done.2.x_ref.refs_3_
  11.4 1.4 %more.1 = (f32[7,256,256]{2,1,0:T(8,128)S(1)}, f32[256,6]{1,0:T(8,128)S(1)}, f32[256,1]{1,0:T(8,128)S(1)}) custom-call(s32[4]{0:T(128)S(1)} %pad_add_fusion.place_ref.refs_0_, f32[4,512]{1,0:T(4,128)S(1)} %reshape.21.gain_ref.refs_1_, ...), custom_call_target="tpu_custom_call", output_to_operand_aliasing={{0}: (7, {}), {1}: (8, {}), {2}: (9, {})} | custom-call | flops 1000000000 | bytes 1000000 | tf_op jit(solution)/shard_map/more/pallas_call | solution.py:107
  12.8 0.0 collective-permute-done.refs_2_.refs_4_
  12.8 4.5 %collective-permute-done.1.refs_3_.refs_5_ = bf16[256,512]{1,0:T(8,128)(2,1)S(1)} collective-permute-done((bf16[256,512]{1,0:T(8,128)(2,1)}, bf16[256,512]{1,0:T(8,128)(2,1)S(1)}, u32[]{:S(2)}, u32[]{:S(2)}) %collective-permute-start.1) | collective-permute-done | bytes 262176 | tf_op jit(solution)/shard_map/ppermute | solution.py:459
  17.3 0.0 copy-start.1
  17.3 6.8 %mixer.1 = (bf16[64,2048]{1,0:T(8,128)(2,1)S(1)}, bf16[64,2048]{1,0:T(8,128)(2,1)S(1)}, bf16[64,2048]{1,0:T(8,128)(2,1)S(1)}, bf16[64,2048]{1,0:T(8,128)(2,1)S(1)}) custom-call(s32[4]{0:T(128)S(1)} %pad_add_fusion.place_ref.refs_0_, f32[4,512]{1,0:T(4,128)S(1)} %reshape.21.gain_ref.refs_1_, bf16[256,512]{1,0:T(8,128)(2,1)S(1)} %collective-permute-done.refs_2_.refs_4_, ...), custom_call_target="tpu_custom_call" | custom-call | flops 20000000000 | bytes 10000000 | tf_op jit(solution)/shard_map/mixer/pallas_call | solution.py:240
  24.1 2.5 %collective-permute-start.3 = (bf16[64,2048]{1,0:T(8,128)(2,1)S(1)}, bf16[64,2048]{1,0:T(8,128)(2,1)S(1)}, u32[]{:S(2)}, u32[]{:S(2)}) collective-permute-start(bf16[64,2048]{1,0:T(8,128)(2,1)S(1)} %get-tuple-element.45), channel_id=1, source_target_pairs={{0,3},{1,2},{2,1},{3,0},{4,7},{5,6},{6,5},{7,4},{8,11},{9,10},{10,... | collective-permute-start | bytes 786440 | tf_op jit(solution)/shard_map/ppermute | solution.py:459
  26.6 0.0 collective-permute-start.4
  26.6 1.5 %collective-permute-start.5 = (bf16[64,2048]{1,0:T(8,128)(2,1)S(1)}, bf16[64,2048]{1,0:T(8,128)(2,1)S(1)}, u32[]{:S(2)}, u32[]{:S(2)}) collective-permute-start(bf16[64,2048]{1,0:T(8,128)(2,1)S(1)} %get-tuple-element.47), channel_id=1, source_target_pairs={{0,2},{1,3},{2,0},{3,1},{4,6},{5,7},{6,4},{7,5},{8,10},{9,11},{10,... | collective-permute-start | bytes 786440 | tf_op jit(solution)/shard_map/ppermute | solution.py:459
  28.1 0.0 copy-done.1
  28.1 0.0 copy-start.2
  28.1 0.9 ready.1
  29.0 0.0 copy-start
  29.0 2.7 %collective-permute-done.3.p1 = bf16[64,2048]{1,0:T(8,128)(2,1)S(1)} collective-permute-done((bf16[64,2048]{1,0:T(8,128)(2,1)S(1)}, bf16[64,2048]{1,0:T(8,128)(2,1)S(1)}, u32[]{:S(2)}, u32[]{:S(2)}) %collective-permute-start.3) | collective-permute-done | bytes 262176 | tf_op jit(solution)/shard_map/ppermute | solution.py:459
  31.7 0.6 collective-permute-done.4.p2
  32.4 5.9 %collective-permute-done.5.p3 = bf16[64,2048]{1,0:T(8,128)(2,1)S(1)} collective-permute-done((bf16[64,2048]{1,0:T(8,128)(2,1)S(1)}, bf16[64,2048]{1,0:T(8,128)(2,1)S(1)}, u32[]{:S(2)}, u32[]{:S(2)}) %collective-permute-start.5) | collective-permute-done | bytes 262176 | tf_op jit(solution)/shard_map/ppermute | solution.py:459
  38.3 0.0 copy-done.2
  38.3 0.7 route.1
  38.9 25.5 %all_to_all.10 = bf16[32,8,2048]{2,1,0:T(8,128)(2,1)S(1)} all-to-all(bf16[32,8,2048]{2,1,0:T(8,128)(2,1)S(1)} %bitcast.14), channel_id=1, replica_groups=mesh['dp'=32,'head'=4] {'dp'}, dimensions={0} | all-to-all | bytes 2097152 | tf_op jit(solution)/shard_map/all_to_all | solution.py:502
  64.4 0.0 copy-done
  64.4 12.6 %experts.1 = (bf16[256,2048]{1,0:T(8,128)(2,1)S(1)}, bf16[128,256]{1,0:T(8,128)(2,1)S(1)}, f32[64,128]{1,0:T(8,128)S(1)}) custom-call(bf16[256,2048]{1,0:T(8,128)(2,1)S(1)} %bitcast.13, bf16[2,2048,1408]{2,1,0:T(8,128)(2,1)} %gate_hbm.1, bf16[2,2048,1408]{2,1,0:T(8,128)(2,1)} %up_hbm.1, bf16[2,1408,2048]{2,1,0:T(8,128)(2,1)} %down_hbm.1, ...), custom_call_target="tpu_custom_call" | custom-call | flops 5000000000 | bytes 10000000 | tf_op jit(solution)/shard_map/experts/pallas_call | solution.py:412
  77.1 20.7 %all_to_all.11 = bf16[32,8,2048]{2,1,0:T(8,128)(2,1)S(1)} all-to-all(bf16[32,8,2048]{2,1,0:T(8,128)(2,1)S(1)} %bitcast.16), channel_id=1, replica_groups=mesh['dp'=32,'head'=4] {'dp'}, dimensions={0} | all-to-all | bytes 2097152 | tf_op jit(solution)/shard_map/all_to_all | solution.py:502
  97.7 1.0 %combine.1 = bf16[64,2048]{1,0:T(8,128)(2,1)} custom-call(f32[64,2048]{1,0:T(8,128)S(1)} %get-tuple-element.49.residual_ref, f32[64,128]{1,0:T(8,128)S(1)} %get-tuple-element.52.leading_ref, bf16[128,256]{1,0:T(8,128)(2,1)S(1)} %get-tuple-element.53.pick_ref, bf16[256,2048]{1,0:T(8,128)(2,1)S(1)} %bitcast.15), custom_call_target="tpu_custom_call" | custom-call | flops 1000000000 | bytes 1000000 | tf_op jit(solution)/shard_map/combine/pallas_call | solution.py:445
Async XLA Ops:
  0.0 11.4 %collective-permute-start.2 = (bf16[256,512]{1,0:T(8,128)(2,1)}, bf16[256,512]{1,0:T(8,128)(2,1)S(1)}, u32[]{:S(2)}, u32[]{:S(2)}) collective-permute-start(bf16[256,512]{1,0:T(8,128)(2,1)} %refs_0_.1), channel_id=1, source_target_pairs={{0,3},{1,2},{2,1},{3,0},{4,7},{5,6},{6,5},{7,4},{8,11},{9,10},{10,... | collective-permute-start | bytes 786440 | tf_op jit(solution)/shard_map/ppermute | solution.py:459
  4.6 8.2 %collective-permute-start = (bf16[256,512]{1,0:T(8,128)(2,1)}, bf16[256,512]{1,0:T(8,128)(2,1)S(1)}, u32[]{:S(2)}, u32[]{:S(2)}) collective-permute-start(bf16[256,512]{1,0:T(8,128)(2,1)} %refs_0_.1), channel_id=1, source_target_pairs={{0,1},{1,0},{2,3},{3,2},{4,5},{5,4},{6,7},{7,6},{8,9},{9,8},{10,11... | collective-permute-start | bytes 786440 | tf_op jit(solution)/shard_map/ppermute | solution.py:459
  4.6 12.7 %collective-permute-start.1 = (bf16[256,512]{1,0:T(8,128)(2,1)}, bf16[256,512]{1,0:T(8,128)(2,1)S(1)}, u32[]{:S(2)}, u32[]{:S(2)}) collective-permute-start(bf16[256,512]{1,0:T(8,128)(2,1)} %refs_0_.1), channel_id=1, source_target_pairs={{0,2},{1,3},{2,0},{3,1},{4,6},{5,7},{6,4},{7,5},{8,10},{9,11},{10,... | collective-permute-start | bytes 786440 | tf_op jit(solution)/shard_map/ppermute | solution.py:459
  17.3 10.7 %copy-start.1 = (s32[64,2]{0,1:T(2,128)S(1)}, s32[64,2]{0,1:T(2,128)}, u32[]{:S(2)}) copy-start(s32[64,2]{0,1:T(2,128)} %param.24) | copy-start | bytes 1540
  24.1 7.6 %collective-permute-start.3 = (bf16[64,2048]{1,0:T(8,128)(2,1)S(1)}, bf16[64,2048]{1,0:T(8,128)(2,1)S(1)}, u32[]{:S(2)}, u32[]{:S(2)}) collective-permute-start(bf16[64,2048]{1,0:T(8,128)(2,1)S(1)} %get-tuple-element.45), channel_id=1, source_target_pairs={{0,3},{1,2},{2,1},{3,0},{4,7},{5,6},{6,5},{7,4},{8,11},{9,10},{10,... | collective-permute-start | bytes 786440 | tf_op jit(solution)/shard_map/ppermute | solution.py:459
  26.6 5.8 %collective-permute-start.4 = (bf16[64,2048]{1,0:T(8,128)(2,1)S(1)}, bf16[64,2048]{1,0:T(8,128)(2,1)S(1)}, u32[]{:S(2)}, u32[]{:S(2)}) collective-permute-start(bf16[64,2048]{1,0:T(8,128)(2,1)S(1)} %get-tuple-element.46), channel_id=1, source_target_pairs={{0,1},{1,0},{2,3},{3,2},{4,5},{5,4},{6,7},{7,6},{8,9},{9,8},{10,11... | collective-permute-start | bytes 786440 | tf_op jit(solution)/shard_map/ppermute | solution.py:459
  26.6 11.7 %collective-permute-start.5 = (bf16[64,2048]{1,0:T(8,128)(2,1)S(1)}, bf16[64,2048]{1,0:T(8,128)(2,1)S(1)}, u32[]{:S(2)}, u32[]{:S(2)}) collective-permute-start(bf16[64,2048]{1,0:T(8,128)(2,1)S(1)} %get-tuple-element.47), channel_id=1, source_target_pairs={{0,2},{1,3},{2,0},{3,1},{4,6},{5,7},{6,4},{7,5},{8,10},{9,11},{10,... | collective-permute-start | bytes 786440 | tf_op jit(solution)/shard_map/ppermute | solution.py:459
  28.1 10.2 %copy-start.2 = (f32[2048]{0:T(1024)S(1)}, f32[2048]{0:T(1024)}, u32[]{:S(2)}) copy-start(f32[2048]{0:T(1024)} %param.22) | copy-start | bytes 24580
  29.0 35.4 %copy-start = (f32[2048,64]{0,1:T(8,128)S(1)}, f32[2048,64]{0,1:T(8,128)}, u32[]{:S(2)}) copy-start(f32[2048,64]{0,1:T(8,128)} %param.23) | copy-start | bytes 1572868

commit v5 on v4

--- a/solution.py
+++ b/solution.py
@@ -38,6 +38,18 @@
     return pl.ds(pl.multiple_of(block * size, size), size)
 
 
+EDGE = 8
+STEPS = ((3, 1, 2), (1, 3, 2))
+
+
+def step(owner_ref, slot):
+    return jnp.where(owner_ref[0] < EDGE, STEPS[1][slot], STEPS[0][slot])
+
+
+def source_of(me_ref, owner_ref, slot, count):
+    return lax.rem(me_ref[0] + (count - step(owner_ref, slot)), count)
+
+
 def gained(x_ref, gain_ref, source):
     wide = x_ref[...].astype(F32)
     return (wide * gain_ref[pl.ds(source, 1), :]).astype(BF16), jnp.sum(wide * wide, -1, keepdims=True)
@@ -52,7 +64,7 @@
     yield dot(x, wb_ref[:, rows], ((1,), (1,)))
 
 
-def first_kernel(place_ref, gain_ref, *refs):
+def first_kernel(me_ref, owner_ref, gain_ref, *refs):
     count = (len(refs) - 4) // 2
     here, there = refs[:count], refs[count:2 * count]
     sums_ref, beta_ref, square_ref, sems = refs[2 * count:]
@@ -61,15 +73,15 @@
         copy.start()
     for copy in copies:
         copy.wait()
-    x, square_ref[...] = gained(there[0], gain_ref, place_ref[0])
-    for i, product in enumerate(products(x, place_ref[0], *there[1:5])):
+    x, square_ref[...] = gained(there[0], gain_ref, me_ref[0])
+    for i, product in enumerate(products(x, me_ref[0], *there[1:5])):
         if i < 1 + 2 * NH:
             sums_ref[i] = product
         else:
             beta_ref[...] = product
 
 
-def first(me, gain, tokens, wq, wk, wv, wb, *others):
+def first(me, owner, gain, tokens, wq, wk, wv, wb, *others):
     moved = (tokens, wq, wk, wv, wb, *others)
     length = tokens.shape[0]
     vmem = pl.BlockSpec(memory_space=pltpu.VMEM)
@@ -81,18 +93,18 @@
     return pl.pallas_call(
         first_kernel,
         out_shape=[pltpu.VMEM(w.shape, w.dtype) for w in moved] + made,
-        in_specs=[pl.BlockSpec(memory_space=pltpu.SMEM), vmem] + [pl.BlockSpec(memory_space=pltpu.HBM)] * len(moved),
+        in_specs=[pl.BlockSpec(memory_space=pltpu.SMEM)] * 2 + [vmem] + [pl.BlockSpec(memory_space=pltpu.HBM)] * len(moved),
         out_specs=[vmem] * (len(moved) + 3),
         scratch_shapes=[pltpu.SemaphoreType.DMA((len(moved),))],
         compiler_params=pltpu.CompilerParams(vmem_limit_bytes=4 * MIB),
         cost_estimate=pl.CostEstimate(flops=2 * 10 ** 9, bytes_accessed=10 ** 6, transcendentals=0),
         name="first",
-    )(me, gain, *[pltpu.with_memory_space_constraint(w, pltpu.HBM) for w in moved])
-
-
-def more_kernel(place_ref, gain_ref, x_ref, wq_ref, wk_ref, wv_ref, wb_ref, sums_ref, beta_ref, square_ref,
+    )(me, owner, gain, *[pltpu.with_memory_space_constraint(w, pltpu.HBM) for w in moved])
+
+
+def more_kernel(slot, me_ref, owner_ref, gain_ref, x_ref, wq_ref, wk_ref, wv_ref, wb_ref, sums_ref, beta_ref, square_ref,
                 new_sums_ref, new_beta_ref, new_square_ref):
-    source = place_ref[1]
+    source = source_of(me_ref, owner_ref, slot, gain_ref.shape[0])
     x, square = gained(x_ref, gain_ref, source)
     new_square_ref[...] = square_ref[...] + square
     for i, product in enumerate(products(x, source, wq_ref, wk_ref, wv_ref, wb_ref)):
@@ -102,32 +114,30 @@
             new_beta_ref[...] = beta_ref[...] + product
 
 
-def more(me, gain, x, weights, sums):
-    vmem = pl.BlockSpec(memory_space=pltpu.VMEM)
-    return pl.pallas_call(
-        more_kernel,
+def more(slot, me, owner, gain, x, weights, sums):
+    vmem = pl.BlockSpec(memory_space=pltpu.VMEM)
+    return pl.pallas_call(
+        lambda *refs: more_kernel(slot, *refs),
         out_shape=[pltpu.VMEM(a.shape, a.dtype) for a in sums],
-        in_specs=[pl.BlockSpec(memory_space=pltpu.SMEM)] + [vmem] * 9,
+        in_specs=[pl.BlockSpec(memory_space=pltpu.SMEM)] * 2 + [vmem] * 9,
         out_specs=[vmem] * 3,
-        input_output_aliases={7: 0, 8: 1, 9: 2},
+        input_output_aliases={8: 0, 9: 1, 10: 2},
         compiler_params=pltpu.CompilerParams(vmem_limit_bytes=4 * MIB),
         cost_estimate=pl.CostEstimate(flops=10 ** 9, bytes_accessed=10 ** 6, transcendentals=0),
         name="more",
-    )(me, gain, x, *weights, *sums)
-
-
-def mixer_kernel(heads, place_ref, gain_ref, x2, x3, wq_ref, wk_ref, wv_ref, wb_ref, sums_ref, beta_ref, square_ref,
+    )(me, owner, gain, x, *weights, *sums)
+
+
+def mixer_kernel(heads, me_ref, owner_ref, gain_ref, x_ref, wq_ref, wk_ref, wv_ref, wb_ref, sums_ref, beta_ref, square_ref,
                  head_gain_ref, wo_ref, o0, o1, o2, o3, keys, beta_keys, rhs, queries, state_map, added, out_add, mixed):
     count, part = gain_ref.shape
-    length = x2.shape[0]
-    total, last = square_ref[...], []
-    for x_ref, source in ((x2, place_ref[2]), (x3, place_ref[3])):
-        x, square = gained(x_ref, gain_ref, source)
-        total = total + square
-        last.append(products(x, source, wq_ref, wk_ref, wv_ref, wb_ref))
-    scale = lax.rsqrt(total / (count * part) + EPSILON)
-    whole = [(sums_ref[i] + (next(last[0]) + next(last[1]))) * scale for i in range(1 + 2 * NH)]
-    beta = (beta_ref[...] + (next(last[0]) + next(last[1]))) * scale
+    length = x_ref.shape[0]
+    source = source_of(me_ref, owner_ref, count - 2, count)
+    x, square = gained(x_ref, gain_ref, source)
+    scale = lax.rsqrt((square_ref[...] + square) / (count * part) + EPSILON)
+    last = products(x, source, wq_ref, wk_ref, wv_ref, wb_ref)
+    whole = [(sums_ref[i] + next(last)) * scale for i in range(1 + 2 * NH)]
+    beta = (beta_ref[...] + next(last)) * scale
     beta = 2.0 / (1.0 + jnp.exp(-beta))
     blocks = length // CH
     query = whole[0]
@@ -197,9 +207,15 @@
         inverse = doubled([p for p, _ in stepped], [t for _, t in stepped], CH // BASE)
         high = [split(t) for t in inverse]
         parts = [split(l) for l in lower]
-        made = [dot(l[0][:, :SUB], jnp.concatenate([s[0], s[1]], 1)) for l, s in zip(parts, high)]
-        rest = [dot(l[1][:, :SUB], s[0]) for l, s in zip(parts, high)]
-        error = [eye - t - (m[:, :WIDE] + (m[:, WIDE:] + r)) for t, m, r in zip(inverse, made, rest)]
+        none, gap = jnp.zeros((SUB, WIDE), BF16), jnp.zeros((WIDE - SUB, 2 * WIDE), BF16)
+        made = [
+            dot(
+                jnp.concatenate([l[0], l[1]], 1),
+                jnp.concatenate([jnp.concatenate(s, 1), gap, jnp.concatenate([s[0], none], 1), gap], 0),
+            )
+            for l, s in zip(parts, high)
+        ]
+        error = [eye - t - (m[:, :WIDE] + m[:, WIDE:]) for t, m in zip(inverse, made)]
         inverse = [t + dot(s[0][:, :SUB], e.astype(BF16)) for t, s, e in zip(inverse, high, error)]
         solved = [dot(t[:, :SUB].astype(BF16), rhs[i]).astype(BF16) for i, t in zip(at, inverse)]
         change = [dot(k[:SUB], s, ((0,), (0,))) for k, s in zip(pairs, solved)]
@@ -221,7 +237,8 @@
             out = out * lax.rsqrt(jnp.mean(out * out, -1, keepdims=True) + EPSILON) * head_gain_ref[...]
             mixed[c * CH:(c + 1) * CH, h * DK:(h + 1) * DK] = out.astype(BF16)
     own = length // count
-    rolled = jnp.concatenate([mixed[rows_at(place_ref[k], own), :] for k in range(count)], 0)
+    targets = [me_ref[0]] + [lax.rem(me_ref[0] + step(owner_ref, k), count) for k in range(count - 1)]
+    rolled = jnp.concatenate([mixed[rows_at(block, own), :] for block in targets], 0)
     result = dot(rolled, wo_ref[...]).astype(BF16)
     for k, o in enumerate((o0, o1, o2, o3)):
         o[...] = result[k * own:(k + 1) * own]
@@ -230,9 +247,9 @@
 UNROLL = 8
 
 
-def mixer(me, gain, x2, x3, weights, sums, head_gain, wo):
+def mixer(me, owner, gain, x, weights, sums, head_gain, wo):
     count = gain.shape[0]
-    length = x2.shape[0]
+    length = x.shape[0]
     heads = weights[0].shape[1] // DK
     blocks = length // CH
     own = length // count
@@ -240,7 +257,7 @@
     return pl.pallas_call(
         lambda *refs: mixer_kernel(heads, *refs),
         out_shape=[jax.ShapeDtypeStruct((own, wo.shape[1]), BF16)] * count,
-        in_specs=[pl.BlockSpec(memory_space=pltpu.SMEM)] + [vmem] * 12,
+        in_specs=[pl.BlockSpec(memory_space=pltpu.SMEM)] * 2 + [vmem] * 11,
         out_specs=[vmem] * count,
         scratch_shapes=[
             pltpu.VMEM((heads, blocks, 2 * WIDE, DK), BF16),
@@ -255,7 +272,7 @@
         compiler_params=pltpu.CompilerParams(vmem_limit_bytes=32 * MIB),
         cost_estimate=pl.CostEstimate(flops=2 * 10 ** 10, bytes_accessed=10 ** 7, transcendentals=0),
         name="mixer",
-    )(me, gain, x2, x3, *weights, *sums, head_gain, wo)
+    )(me, owner, gain, x, *weights, *sums, head_gain, wo)
 
 
 def slots(ids_ref, experts, total):
@@ -272,17 +289,17 @@
     return chosen, [jnp.where(fits, dot(spread, c.astype(BF16)), 0.0) for c in chosen]
 
 
-def ready_kernel(experts, place_ref, part_ref, x0, x1, x2, x3, ids_ref, base_ref, chosen_ref):
+def ready_kernel(experts, me_ref, owner_ref, part_ref, x0, x1, x2, x3, ids_ref, base_ref, chosen_ref):
     own, part = part_ref.shape[0], x0.shape[1]
     for k, x in enumerate((x0, x1, x2, x3)):
-        columns = rows_at(place_ref[k], part)
-        base_ref[:, columns] = x[rows_at(place_ref[0], own), :].astype(F32)
+        block = me_ref[0] if k == 0 else source_of(me_ref, owner_ref, k - 1, 4)
+        base_ref[:, rows_at(block, part)] = x[rows_at(me_ref[0], own), :].astype(F32)
     base_ref[...] = base_ref[...] + part_ref[...].astype(F32)
     _, chosen = slots(ids_ref, experts, chosen_ref.shape[0])
     chosen_ref[...] = (chosen[0] + chosen[1]).astype(BF16)
 
 
-def ready(me, part, xs, ids, experts, capacity):
+def ready(me, owner, part, xs, ids, experts, capacity):
     own, width = part.shape
     vmem = pl.BlockSpec(memory_space=pltpu.VMEM)
     return pl.pallas_call(
@@ -291,12 +308,12 @@
             jax.ShapeDtypeStruct((own, width), F32),
             jax.ShapeDtypeStruct((experts * capacity, own), BF16),
         ],
-        in_specs=[pl.BlockSpec(memory_space=pltpu.SMEM)] + [vmem] * 6,
+        in_specs=[pl.BlockSpec(memory_space=pltpu.SMEM)] * 2 + [vmem] * 6,
         out_specs=[vmem] * 2,
         compiler_params=pltpu.CompilerParams(vmem_limit_bytes=8 * MIB),
         cost_estimate=pl.CostEstimate(flops=2 * 10 ** 9, bytes_accessed=10 ** 6, transcendentals=0),
         name="ready",
-    )(me, part, *xs, ids)
+    )(me, owner, part, *xs, ids)
 
 
 def route_kernel(base_ref, p1, p2, p3, gain_ref, chosen_ref, residual_ref, routed_ref, send_ref):
@@ -453,47 +470,30 @@
     )(residual, leading, pick, back)
 
 
-def swapped(x, step, axes=("dp", "head")):
+def passed(x, slot, axes=("dp", "head")):
     owners, peers = (lax.axis_size(a) for a in axes)
-    pairs = [(d * peers + z, d * peers + (z ^ step(d))) for d in range(owners) for z in range(peers)]
+    pairs = [(d * peers + z, d * peers + (z + STEPS[d < EDGE][slot]) % peers) for d in range(owners) for z in range(peers)]
     return lax.ppermute(x, axes, pairs)
-
-
-def near(owner):
-    return 1 if owner >= EDGE else 3
-
-
-def far(owner):
-    return 3 if owner >= EDGE else 1
-
-
-def across(owner):
-    return 2
-
-
-EDGE = 8
-STEPS = (near, far, across)
 
 
 def shards(tokens, mixer_gain, query_weight, key_weight, value_weight, beta_weight, head_gain, output_weight,
            expert_gain, router_weight, expert_ids, gate_weight, up_weight, down_weight):
     owners = lax.axis_size("dp")
-    me = lax.axis_index("head").astype(jnp.int32)
-    edge = lax.axis_index("dp") < EDGE
-    one, three = jnp.where(edge, 3, 1), jnp.where(edge, 1, 3)
-    me = jnp.stack([me, me ^ one, me ^ three, me ^ 2]).astype(jnp.int32)
-    xs = [tokens] + [swapped(tokens, step) for step in STEPS]
+    me = lax.axis_index("head").reshape(1).astype(jnp.int32)
+    owner = lax.axis_index("dp").reshape(1).astype(jnp.int32)
+    xs = [tokens] + [passed(tokens, slot) for slot in range(3)]
     gain = mixer_gain.reshape(lax.axis_size("head"), -1)
-    here = first(me, gain, tokens, query_weight, key_weight, value_weight, beta_weight.T, head_gain.reshape(1, -1),
+    here = first(me, owner, gain, tokens, query_weight, key_weight, value_weight, beta_weight.T, head_gain.reshape(1, -1),
                  output_weight)
     xs[0], weights, sums = here[0], here[1:5], here[7:]
-    sums = more(me, gain, xs[1], weights, sums)
-    parts = mixer(me, gain, xs[2], xs[3], weights, sums, here[5], here[6])
-    arriving = [swapped(part, step) for part, step in zip(parts[1:], STEPS)]
+    for slot in (0, 1):
+        sums = more(slot, me, owner, gain, xs[slot + 1], weights, sums)
+    parts = mixer(me, owner, gain, xs[3], weights, sums, here[5], here[6])
+    arriving = [passed(part, slot) for slot, part in enumerate(parts[1:])]
     experts = router_weight.shape[1]
     capacity = 4 * parts[0].shape[0] // experts
     ids = expert_ids.T
-    base, chosen = ready(me, parts[0], xs, ids, experts, capacity)
+    base, chosen = ready(me, owner, parts[0], xs, ids, experts, capacity)
     residual, routed, outgoing = route(base, arriving, expert_gain.reshape(1, -1), chosen)
     width = outgoing.shape[1]
 

time: 99 us -> 101 us (1.020)
  blocking collectives: 46.2 us -> 50.9 us
  Pallas kernels: 28.3 us -> 26.4 us
  starting transfers between devices: 9.7 us -> 8.63 us
    all_to_all x2, blocking collectives: 46.2 us -> 50.9 us  [exchanged(): rows = lax.all_to_all(rows, 'dp', split_axis=0, concat_axis=0, tiled=True)]
    pallas_call x1, Pallas kernels: 6.79 us -> 5.69 us  [mixer(): pl.pallas_call(lambda *refs: mixer_kernel(heads, *refs), out_shape=[jax.S...]
    ppermute x6, starting transfers between devices: 9.7 us -> 8.63 us  [passed(): return lax.ppermute(x, axes, pairs)]
  transfers between devices with their start and end apart: 6 -> 6, of which waited for: 4 -> 3; matrix products, arithmetic and copies ran while one was open for 1% -> 1% of each run, Pallas kernels for 7% -> 6%
where the time goes in v5:
time: 101 us
  blocking collectives  50.9 us (50%)
  Pallas kernels  26.4 us (26%)
  waiting for transfers between devices  14.1 us (14%)
  starting transfers between devices  8.63 us (9%)
    all_to_all x2, blocking collectives, exchanged(): rows = lax.all_to_all(rows, 'dp', split_axis=0, concat_axis=0, tiled=True)  50.9 us
    ppermute x6, waiting for transfers between devices, passed(): return lax.ppermute(x, axes, pairs)  14.1 us
    pallas_call x1, Pallas kernels, experts_here(): pl.pallas_call(expert_kernel, out_shape=[jax.ShapeDtypeStruct(rows.shape,...  12.6 us
    ppermute x6, starting transfers between devices, passed(): return lax.ppermute(x, axes, pairs)  8.63 us
    pallas_call x1, Pallas kernels, mixer(): pl.pallas_call(lambda *refs: mixer_kernel(heads, *refs), out_shape=[jax.S...  5.69 us
    pallas_call x1, Pallas kernels, first(): pl.pallas_call(first_kernel, out_shape=[pltpu.VMEM(w.shape, w.dtype) for...  4.28 us
  transfers between devices with their start and end apart: 6, of which 3 were waited for; matrix products, arithmetic and copies ran while one was open for 1% of the time, Pallas kernels for 6%

profile of v5, /device:TPU:1, one launch (start us, length us, event | category | flops | bytes accessed | tf_op | source)
XLA Modules:
  0.0 100.8 jit_solution(10945048497156946748)
XLA Ops:
  0.0 2.5 %collective-permute-start.2 = (bf16[256,512]{1,0:T(8,128)(2,1)}, bf16[256,512]{1,0:T(8,128)(2,1)S(1)}, u32[]{:S(2)}, u32[]{:S(2)}) collective-permute-start(bf16[256,512]{1,0:T(8,128)(2,1)} %refs_0_.1), channel_id=1, source_target_pairs={{0,1},{1,2},{2,3},{3,0},{4,5},{5,6},{6,7},{7,4},{8,9},{9,10},{10,1... | collective-permute-start | bytes 786440 | tf_op jit(solution)/shard_map/ppermute | solution.py:476
  2.5 2.1 %collective-permute-start.1 = (bf16[256,512]{1,0:T(8,128)(2,1)}, bf16[256,512]{1,0:T(8,128)(2,1)S(1)}, u32[]{:S(2)}, u32[]{:S(2)}) collective-permute-start(bf16[256,512]{1,0:T(8,128)(2,1)} %refs_0_.1), channel_id=1, source_target_pairs={{0,3},{1,0},{2,1},{3,2},{4,7},{5,4},{6,5},{7,6},{8,11},{9,8},{10,9... | collective-permute-start | bytes 786440 | tf_op jit(solution)/shard_map/ppermute | solution.py:476
  4.6 1.3 %collective-permute-start = (bf16[256,512]{1,0:T(8,128)(2,1)}, bf16[256,512]{1,0:T(8,128)(2,1)S(1)}, u32[]{:S(2)}, u32[]{:S(2)}) collective-permute-start(bf16[256,512]{1,0:T(8,128)(2,1)} %refs_0_.1), channel_id=1, source_target_pairs={{0,2},{1,3},{2,0},{3,1},{4,6},{5,7},{6,4},{7,5},{8,10},{9,11},{10,... | collective-permute-start | bytes 786440 | tf_op jit(solution)/shard_map/ppermute | solution.py:476
  5.9 0.7 reshape.29.gain_ref.refs_2_
  6.6 4.3 %first.1 = (bf16[256,512]{1,0:T(8,128)(2,1)S(1)}, bf16[2048,256]{1,0:T(8,128)(2,1)S(1)}, bf16[3,2048,256]{2,1,0:T(8,128)(2,1)S(1)}, bf16[3,2048,256]{2,1,0:T(8,1...) custom-call(s32[1]{0:T(128)} %bitcast.me_ref.refs_0_, ...), custom_call_target="tpu_custom_call" | custom-call | flops 2000000000 | bytes 1000000 | tf_op jit(solution)/shard_map/first/pallas_call | solution.py:93
  10.9 0.0 collective-permute-done.2.refs_3_.refs_4_
  10.9 0.8 more.2
  11.7 0.0 collective-permute-done.1.refs_3_.refs_5_
  11.7 0.8 more.3
  12.6 4.7 %collective-permute-done.refs_3_.refs_6_ = bf16[256,512]{1,0:T(8,128)(2,1)S(1)} collective-permute-done((bf16[256,512]{1,0:T(8,128)(2,1)}, bf16[256,512]{1,0:T(8,128)(2,1)S(1)}, u32[]{:S(2)}, u32[]{:S(2)}) %collective-permute-start) | collective-permute-done | bytes 262176 | tf_op jit(solution)/shard_map/ppermute | solution.py:476
  17.3 0.0 copy-start.1
  17.3 5.7 %mixer.1 = (bf16[64,2048]{1,0:T(8,128)(2,1)S(1)}, bf16[64,2048]{1,0:T(8,128)(2,1)S(1)}, bf16[64,2048]{1,0:T(8,128)(2,1)S(1)}, bf16[64,2048]{1,0:T(8,128)(2,1)S(1)}) custom-call(s32[1]{0:T(128)} %bitcast.me_ref.refs_0_, s32[1]{0:T(128)} %bitcast.1.owner_ref.refs_1_, f32[4,512]{1,0:T(4,128)S(1)} %reshape.29.gain_ref.refs_2_, ...), custom_call_target="tpu_custom_call" | custom-call | flops 20000000000 | bytes 10000000 | tf_op jit(solution)/shard_map/mixer/pallas_call | solution.py:257
  23.0 0.7 collective-permute-start.3
  23.7 2.1 %collective-permute-start.4 = (bf16[64,2048]{1,0:T(8,128)(2,1)S(1)}, bf16[64,2048]{1,0:T(8,128)(2,1)S(1)}, u32[]{:S(2)}, u32[]{:S(2)}) collective-permute-start(bf16[64,2048]{1,0:T(8,128)(2,1)S(1)} %get-tuple-element.52), channel_id=1, source_target_pairs={{0,3},{1,0},{2,1},{3,2},{4,7},{5,4},{6,5},{7,6},{8,11},{9,8},{10,9... | collective-permute-start | bytes 786440 | tf_op jit(solution)/shard_map/ppermute | solution.py:476
  25.8 0.0 collective-permute-start.5
  25.8 0.0 copy-done.1
  25.8 0.0 copy-start.2
  25.8 0.4 ready.1
  26.2 0.0 copy-start
  26.2 5.1 %collective-permute-done.3.p1 = bf16[64,2048]{1,0:T(8,128)(2,1)S(1)} collective-permute-done((bf16[64,2048]{1,0:T(8,128)(2,1)S(1)}, bf16[64,2048]{1,0:T(8,128)(2,1)S(1)}, u32[]{:S(2)}, u32[]{:S(2)}) %collective-permute-start.3) | collective-permute-done | bytes 262176 | tf_op jit(solution)/shard_map/ppermute | solution.py:476
  31.3 0.0 collective-permute-done.4.p2
  31.3 4.3 %collective-permute-done.5.p3 = bf16[64,2048]{1,0:T(8,128)(2,1)S(1)} collective-permute-done((bf16[64,2048]{1,0:T(8,128)(2,1)S(1)}, bf16[64,2048]{1,0:T(8,128)(2,1)S(1)}, u32[]{:S(2)}, u32[]{:S(2)}) %collective-permute-start.5) | collective-permute-done | bytes 262176 | tf_op jit(solution)/shard_map/ppermute | solution.py:476
  35.6 0.0 copy-done.2
  35.6 0.6 route.1
  36.2 30.2 %all_to_all.10 = bf16[32,8,2048]{2,1,0:T(8,128)(2,1)S(1)} all-to-all(bf16[32,8,2048]{2,1,0:T(8,128)(2,1)S(1)} %bitcast.12), channel_id=1, replica_groups=mesh['dp'=32,'head'=4] {'dp'}, dimensions={0} | all-to-all | bytes 2097152 | tf_op jit(solution)/shard_map/all_to_all | solution.py:502
  66.4 0.0 copy-done
  66.4 12.6 %experts.1 = (bf16[256,2048]{1,0:T(8,128)(2,1)S(1)}, bf16[128,256]{1,0:T(8,128)(2,1)S(1)}, f32[64,128]{1,0:T(8,128)S(1)}) custom-call(bf16[256,2048]{1,0:T(8,128)(2,1)S(1)} %bitcast.11, bf16[2,2048,1408]{2,1,0:T(8,128)(2,1)} %gate_hbm.1, bf16[2,2048,1408]{2,1,0:T(8,128)(2,1)} %up_hbm.1, bf16[2,1408,2048]{2,1,0:T(8,128)(2,1)} %down_hbm.1, ...), custom_call_target="tpu_custom_call" | custom-call | flops 5000000000 | bytes 10000000 | tf_op jit(solution)/shard_map/experts/pallas_call | solution.py:429
  79.1 20.7 %all_to_all.11 = bf16[32,8,2048]{2,1,0:T(8,128)(2,1)S(1)} all-to-all(bf16[32,8,2048]{2,1,0:T(8,128)(2,1)S(1)} %bitcast.14), channel_id=1, replica_groups=mesh['dp'=32,'head'=4] {'dp'}, dimensions={0} | all-to-all | bytes 2097152 | tf_op jit(solution)/shard_map/all_to_all | solution.py:502
  99.7 1.0 %combine.1 = bf16[64,2048]{1,0:T(8,128)(2,1)} custom-call(f32[64,2048]{1,0:T(8,128)S(1)} %get-tuple-element.55.residual_ref, f32[64,128]{1,0:T(8,128)S(1)} %get-tuple-element.58.leading_ref, bf16[128,256]{1,0:T(8,128)(2,1)S(1)} %get-tuple-element.59.pick_ref, bf16[256,2048]{1,0:T(8,128)(2,1)S(1)} %bitcast.13), custom_call_target="tpu_custom_call" | custom-call | flops 1000000000 | bytes 1000000 | tf_op jit(solution)/shard_map/combine/pallas_call | solution.py:462
Async XLA Ops:
  0.0 10.9 %collective-permute-start.2 = (bf16[256,512]{1,0:T(8,128)(2,1)}, bf16[256,512]{1,0:T(8,128)(2,1)S(1)}, u32[]{:S(2)}, u32[]{:S(2)}) collective-permute-start(bf16[256,512]{1,0:T(8,128)(2,1)} %refs_0_.1), channel_id=1, source_target_pairs={{0,1},{1,2},{2,3},{3,0},{4,5},{5,6},{6,7},{7,4},{8,9},{9,10},{10,1... | collective-permute-start | bytes 786440 | tf_op jit(solution)/shard_map/ppermute | solution.py:476
  2.5 9.3 %collective-permute-start.1 = (bf16[256,512]{1,0:T(8,128)(2,1)}, bf16[256,512]{1,0:T(8,128)(2,1)S(1)}, u32[]{:S(2)}, u32[]{:S(2)}) collective-permute-start(bf16[256,512]{1,0:T(8,128)(2,1)} %refs_0_.1), channel_id=1, source_target_pairs={{0,3},{1,0},{2,1},{3,2},{4,7},{5,4},{6,5},{7,6},{8,11},{9,8},{10,9... | collective-permute-start | bytes 786440 | tf_op jit(solution)/shard_map/ppermute | solution.py:476
  4.6 12.7 %collective-permute-start = (bf16[256,512]{1,0:T(8,128)(2,1)}, bf16[256,512]{1,0:T(8,128)(2,1)S(1)}, u32[]{:S(2)}, u32[]{:S(2)}) collective-permute-start(bf16[256,512]{1,0:T(8,128)(2,1)} %refs_0_.1), channel_id=1, source_target_pairs={{0,2},{1,3},{2,0},{3,1},{4,6},{5,7},{6,4},{7,5},{8,10},{9,11},{10,... | collective-permute-start | bytes 786440 | tf_op jit(solution)/shard_map/ppermute | solution.py:476
  17.3 8.5 %copy-start.1 = (s32[64,2]{0,1:T(2,128)S(1)}, s32[64,2]{0,1:T(2,128)}, u32[]{:S(2)}) copy-start(s32[64,2]{0,1:T(2,128)} %param.24) | copy-start | bytes 1540
  23.0 8.3 %collective-permute-start.3 = (bf16[64,2048]{1,0:T(8,128)(2,1)S(1)}, bf16[64,2048]{1,0:T(8,128)(2,1)S(1)}, u32[]{:S(2)}, u32[]{:S(2)}) collective-permute-start(bf16[64,2048]{1,0:T(8,128)(2,1)S(1)} %get-tuple-element.51), channel_id=1, source_target_pairs={{0,1},{1,2},{2,3},{3,0},{4,5},{5,6},{6,7},{7,4},{8,9},{9,10},{10,1... | collective-permute-start | bytes 786440 | tf_op jit(solution)/shard_map/ppermute | solution.py:476
  23.7 7.6 %collective-permute-start.4 = (bf16[64,2048]{1,0:T(8,128)(2,1)S(1)}, bf16[64,2048]{1,0:T(8,128)(2,1)S(1)}, u32[]{:S(2)}, u32[]{:S(2)}) collective-permute-start(bf16[64,2048]{1,0:T(8,128)(2,1)S(1)} %get-tuple-element.52), channel_id=1, source_target_pairs={{0,3},{1,0},{2,1},{3,2},{4,7},{5,4},{6,5},{7,6},{8,11},{9,8},{10,9... | collective-permute-start | bytes 786440 | tf_op jit(solution)/shard_map/ppermute | solution.py:476
  25.8 9.8 %collective-permute-start.5 = (bf16[64,2048]{1,0:T(8,128)(2,1)S(1)}, bf16[64,2048]{1,0:T(8,128)(2,1)S(1)}, u32[]{:S(2)}, u32[]{:S(2)}) collective-permute-start(bf16[64,2048]{1,0:T(8,128)(2,1)S(1)} %get-tuple-element.53), channel_id=1, source_target_pairs={{0,2},{1,3},{2,0},{3,1},{4,6},{5,7},{6,4},{7,5},{8,10},{9,11},{10,... | collective-permute-start | bytes 786440 | tf_op jit(solution)/shard_map/ppermute | solution.py:476
  25.8 9.8 %copy-start.2 = (f32[2048]{0:T(1024)S(1)}, f32[2048]{0:T(1024)}, u32[]{:S(2)}) copy-start(f32[2048]{0:T(1024)} %param.22) | copy-start | bytes 24580
  26.2 40.3 %copy-start = (f32[2048,64]{0,1:T(8,128)S(1)}, f32[2048,64]{0,1:T(8,128)}, u32[]{:S(2)}) copy-start(f32[2048,64]{0,1:T(8,128)} %param.23) | copy-start | bytes 1572868

commit v6 on v5

--- a/solution.py
+++ b/solution.py
@@ -38,16 +38,12 @@
     return pl.ds(pl.multiple_of(block * size, size), size)
 
 
-EDGE = 8
-STEPS = ((3, 1, 2), (1, 3, 2))
-
-
-def step(owner_ref, slot):
-    return jnp.where(owner_ref[0] < EDGE, STEPS[1][slot], STEPS[0][slot])
-
-
-def source_of(me_ref, owner_ref, slot, count):
-    return lax.rem(me_ref[0] + (count - step(owner_ref, slot)), count)
+NEAR = (1, 3)
+SENT = (1, 2, 3)
+
+
+def source_of(me_ref, shift, count):
+    return lax.rem(me_ref[0] + (count - shift), count)
 
 
 def gained(x_ref, gain_ref, source):
@@ -64,7 +60,7 @@
     yield dot(x, wb_ref[:, rows], ((1,), (1,)))
 
 
-def first_kernel(me_ref, owner_ref, gain_ref, *refs):
+def first_kernel(me_ref, gain_ref, *refs):
     count = (len(refs) - 4) // 2
     here, there = refs[:count], refs[count:2 * count]
     sums_ref, beta_ref, square_ref, sems = refs[2 * count:]
@@ -81,7 +77,7 @@
             beta_ref[...] = product
 
 
-def first(me, owner, gain, tokens, wq, wk, wv, wb, *others):
+def first(me, gain, tokens, wq, wk, wv, wb, *others):
     moved = (tokens, wq, wk, wv, wb, *others)
     length = tokens.shape[0]
     vmem = pl.BlockSpec(memory_space=pltpu.VMEM)
@@ -93,18 +89,18 @@
     return pl.pallas_call(
         first_kernel,
         out_shape=[pltpu.VMEM(w.shape, w.dtype) for w in moved] + made,
-        in_specs=[pl.BlockSpec(memory_space=pltpu.SMEM)] * 2 + [vmem] + [pl.BlockSpec(memory_space=pltpu.HBM)] * len(moved),
+        in_specs=[pl.BlockSpec(memory_space=pltpu.SMEM), vmem] + [pl.BlockSpec(memory_space=pltpu.HBM)] * len(moved),
         out_specs=[vmem] * (len(moved) + 3),
         scratch_shapes=[pltpu.SemaphoreType.DMA((len(moved),))],
         compiler_params=pltpu.CompilerParams(vmem_limit_bytes=4 * MIB),
         cost_estimate=pl.CostEstimate(flops=2 * 10 ** 9, bytes_accessed=10 ** 6, transcendentals=0),
         name="first",
-    )(me, owner, gain, *[pltpu.with_memory_space_constraint(w, pltpu.HBM) for w in moved])
-
-
-def more_kernel(slot, me_ref, owner_ref, gain_ref, x_ref, wq_ref, wk_ref, wv_ref, wb_ref, sums_ref, beta_ref, square_ref,
+    )(me, gain, *[pltpu.with_memory_space_constraint(w, pltpu.HBM) for w in moved])
+
+
+def more_kernel(shift, me_ref, gain_ref, x_ref, wq_ref, wk_ref, wv_ref, wb_ref, sums_ref, beta_ref, square_ref,
                 new_sums_ref, new_beta_ref, new_square_ref):
-    source = source_of(me_ref, owner_ref, slot, gain_ref.shape[0])
+    source = source_of(me_ref, shift, gain_ref.shape[0])
     x, square = gained(x_ref, gain_ref, source)
     new_square_ref[...] = square_ref[...] + square
     for i, product in enumerate(products(x, source, wq_ref, wk_ref, wv_ref, wb_ref)):
@@ -114,26 +110,26 @@
             new_beta_ref[...] = beta_ref[...] + product
 
 
-def more(slot, me, owner, gain, x, weights, sums):
-    vmem = pl.BlockSpec(memory_space=pltpu.VMEM)
-    return pl.pallas_call(
-        lambda *refs: more_kernel(slot, *refs),
+def more(shift, me, gain, x, weights, sums):
+    vmem = pl.BlockSpec(memory_space=pltpu.VMEM)
+    return pl.pallas_call(
+        lambda *refs: more_kernel(shift, *refs),
         out_shape=[pltpu.VMEM(a.shape, a.dtype) for a in sums],
-        in_specs=[pl.BlockSpec(memory_space=pltpu.SMEM)] * 2 + [vmem] * 9,
+        in_specs=[pl.BlockSpec(memory_space=pltpu.SMEM)] + [vmem] * 9,
         out_specs=[vmem] * 3,
-        input_output_aliases={8: 0, 9: 1, 10: 2},
+        input_output_aliases={7: 0, 8: 1, 9: 2},
         compiler_params=pltpu.CompilerParams(vmem_limit_bytes=4 * MIB),
         cost_estimate=pl.CostEstimate(flops=10 ** 9, bytes_accessed=10 ** 6, transcendentals=0),
         name="more",
-    )(me, owner, gain, x, *weights, *sums)
-
-
-def mixer_kernel(heads, me_ref, owner_ref, gain_ref, x_ref, wq_ref, wk_ref, wv_ref, wb_ref, sums_ref, beta_ref, square_ref,
+    )(me, gain, x, *weights, *sums)
+
+
+def mixer_kernel(heads, me_ref, gain_ref, top_ref, bottom_ref, wq_ref, wk_ref, wv_ref, wb_ref, sums_ref, beta_ref, square_ref,
                  head_gain_ref, wo_ref, o0, o1, o2, o3, keys, beta_keys, rhs, queries, state_map, added, out_add, mixed):
     count, part = gain_ref.shape
-    length = x_ref.shape[0]
-    source = source_of(me_ref, owner_ref, count - 2, count)
-    x, square = gained(x_ref, gain_ref, source)
+    length = 2 * top_ref.shape[0]
+    source = source_of(me_ref, count // 2, count)
+    x, square = gained(jnp.concatenate([top_ref[...], bottom_ref[...]], 0), gain_ref, source)
     scale = lax.rsqrt((square_ref[...] + square) / (count * part) + EPSILON)
     last = products(x, source, wq_ref, wk_ref, wv_ref, wb_ref)
     whole = [(sums_ref[i] + next(last)) * scale for i in range(1 + 2 * NH)]
@@ -237,7 +233,7 @@
             out = out * lax.rsqrt(jnp.mean(out * out, -1, keepdims=True) + EPSILON) * head_gain_ref[...]
             mixed[c * CH:(c + 1) * CH, h * DK:(h + 1) * DK] = out.astype(BF16)
     own = length // count
-    targets = [me_ref[0]] + [lax.rem(me_ref[0] + step(owner_ref, k), count) for k in range(count - 1)]
+    targets = [me_ref[0]] + [lax.rem(me_ref[0] + shift, count) for shift in SENT]
     rolled = jnp.concatenate([mixed[rows_at(block, own), :] for block in targets], 0)
     result = dot(rolled, wo_ref[...]).astype(BF16)
     for k, o in enumerate((o0, o1, o2, o3)):
@@ -247,9 +243,9 @@
 UNROLL = 8
 
 
-def mixer(me, owner, gain, x, weights, sums, head_gain, wo):
+def mixer(me, gain, top, bottom, weights, sums, head_gain, wo):
     count = gain.shape[0]
-    length = x.shape[0]
+    length = 2 * top.shape[0]
     heads = weights[0].shape[1] // DK
     blocks = length // CH
     own = length // count
@@ -257,7 +253,7 @@
     return pl.pallas_call(
         lambda *refs: mixer_kernel(heads, *refs),
         out_shape=[jax.ShapeDtypeStruct((own, wo.shape[1]), BF16)] * count,
-        in_specs=[pl.BlockSpec(memory_space=pltpu.SMEM)] * 2 + [vmem] * 11,
+        in_specs=[pl.BlockSpec(memory_space=pltpu.SMEM)] + [vmem] * 12,
         out_specs=[vmem] * count,
         scratch_shapes=[
             pltpu.VMEM((heads, blocks, 2 * WIDE, DK), BF16),
@@ -272,7 +268,7 @@
         compiler_params=pltpu.CompilerParams(vmem_limit_bytes=32 * MIB),
         cost_estimate=pl.CostEstimate(flops=2 * 10 ** 10, bytes_accessed=10 ** 7, transcendentals=0),
         name="mixer",
-    )(me, owner, gain, x, *weights, *sums, head_gain, wo)
+    )(me, gain, top, bottom, *weights, *sums, head_gain, wo)
 
 
 def slots(ids_ref, experts, total):
@@ -289,17 +285,22 @@
     return chosen, [jnp.where(fits, dot(spread, c.astype(BF16)), 0.0) for c in chosen]
 
 
-def ready_kernel(experts, me_ref, owner_ref, part_ref, x0, x1, x2, x3, ids_ref, base_ref, chosen_ref):
+def ready_kernel(experts, me_ref, part_ref, x0, x1, x3, top_ref, bottom_ref, ids_ref, base_ref, chosen_ref):
     own, part = part_ref.shape[0], x0.shape[1]
-    for k, x in enumerate((x0, x1, x2, x3)):
-        block = me_ref[0] if k == 0 else source_of(me_ref, owner_ref, k - 1, 4)
-        base_ref[:, rows_at(block, part)] = x[rows_at(me_ref[0], own), :].astype(F32)
+    me, count = me_ref[0], x0.shape[0] // part_ref.shape[0]
+    for shift, x in ((0, x0), (1, x1), (3, x3)):
+        block = me if shift == 0 else source_of(me_ref, shift, count)
+        base_ref[:, rows_at(block, part)] = x[rows_at(me, own), :].astype(F32)
+    half = count // 2
+    inner = rows_at(lax.rem(me, half), own)
+    far = jnp.where(me < half, top_ref[inner, :].astype(F32), bottom_ref[inner, :].astype(F32))
+    base_ref[:, rows_at(source_of(me_ref, half, count), part)] = far
     base_ref[...] = base_ref[...] + part_ref[...].astype(F32)
     _, chosen = slots(ids_ref, experts, chosen_ref.shape[0])
     chosen_ref[...] = (chosen[0] + chosen[1]).astype(BF16)
 
 
-def ready(me, owner, part, xs, ids, experts, capacity):
+def ready(me, part, xs, ids, experts, capacity):
     own, width = part.shape
     vmem = pl.BlockSpec(memory_space=pltpu.VMEM)
     return pl.pallas_call(
@@ -308,12 +309,12 @@
             jax.ShapeDtypeStruct((own, width), F32),
             jax.ShapeDtypeStruct((experts * capacity, own), BF16),
         ],
-        in_specs=[pl.BlockSpec(memory_space=pltpu.SMEM)] * 2 + [vmem] * 6,
+        in_specs=[pl.BlockSpec(memory_space=pltpu.SMEM)] + [vmem] * 7,
         out_specs=[vmem] * 2,
         compiler_params=pltpu.CompilerParams(vmem_limit_bytes=8 * MIB),
         cost_estimate=pl.CostEstimate(flops=2 * 10 ** 9, bytes_accessed=10 ** 6, transcendentals=0),
         name="ready",
-    )(me, owner, part, *xs, ids)
+    )(me, part, *xs, ids)
 
 
 def route_kernel(base_ref, p1, p2, p3, gain_ref, chosen_ref, residual_ref, routed_ref, send_ref):
@@ -470,30 +471,30 @@
     )(residual, leading, pick, back)
 
 
-def passed(x, slot, axes=("dp", "head")):
-    owners, peers = (lax.axis_size(a) for a in axes)
-    pairs = [(d * peers + z, d * peers + (z + STEPS[d < EDGE][slot]) % peers) for d in range(owners) for z in range(peers)]
-    return lax.ppermute(x, axes, pairs)
+def passed(x, k, axis):
+    size = lax.axis_size(axis)
+    return lax.ppermute(x, axis, [(i, (i + k) % size) for i in range(size)])
 
 
 def shards(tokens, mixer_gain, query_weight, key_weight, value_weight, beta_weight, head_gain, output_weight,
            expert_gain, router_weight, expert_ids, gate_weight, up_weight, down_weight):
     owners = lax.axis_size("dp")
     me = lax.axis_index("head").reshape(1).astype(jnp.int32)
-    owner = lax.axis_index("dp").reshape(1).astype(jnp.int32)
-    xs = [tokens] + [passed(tokens, slot) for slot in range(3)]
+    left, right = (passed(tokens, shift, "head") for shift in NEAR)
+    half = tokens.shape[0] // 2
+    top, bottom = passed(left[:half], NEAR[0], "head"), passed(right[half:], NEAR[1], "head")
     gain = mixer_gain.reshape(lax.axis_size("head"), -1)
-    here = first(me, owner, gain, tokens, query_weight, key_weight, value_weight, beta_weight.T, head_gain.reshape(1, -1),
+    here = first(me, gain, tokens, query_weight, key_weight, value_weight, beta_weight.T, head_gain.reshape(1, -1),
                  output_weight)
-    xs[0], weights, sums = here[0], here[1:5], here[7:]
-    for slot in (0, 1):
-        sums = more(slot, me, owner, gain, xs[slot + 1], weights, sums)
-    parts = mixer(me, owner, gain, xs[3], weights, sums, here[5], here[6])
-    arriving = [passed(part, slot) for slot, part in enumerate(parts[1:])]
+    weights, sums = here[1:5], here[7:]
+    for shift, x in zip(NEAR, (left, right)):
+        sums = more(shift, me, gain, x, weights, sums)
+    parts = mixer(me, gain, top, bottom, weights, sums, here[5], here[6])
+    arriving = [passed(part, shift, "head") for shift, part in zip(SENT, parts[1:])]
     experts = router_weight.shape[1]
     capacity = 4 * parts[0].shape[0] // experts
     ids = expert_ids.T
-    base, chosen = ready(me, owner, parts[0], xs, ids, experts, capacity)
+    base, chosen = ready(me, parts[0], (here[0], left, right, top, bottom), ids, experts, capacity)
     residual, routed, outgoing = route(base, arriving, expert_gain.reshape(1, -1), chosen)
     width = outgoing.shape[1]
 

time: 101 us -> 97.6 us (0.966)
  blocking collectives: 50.9 us -> 47.4 us
  starting transfers between devices: 8.63 us -> 11.4 us
  waiting for transfers between devices: 14.1 us -> 11.4 us
    all_to_all x2, blocking collectives: 50.9 us -> 47.4 us  [exchanged(): rows = lax.all_to_all(rows, 'dp', split_axis=0, concat_axis=0, tiled=True)]
    ppermute x6 -> x7, starting transfers between devices: 8.63 us -> 11.4 us  [passed(): return lax.ppermute(x, axis, [(i, (i + k) % size) for i in range(size)])]
    ppermute x6 -> x7, waiting for transfers between devices: 14.1 us -> 11.4 us  [passed(): return lax.ppermute(x, axis, [(i, (i + k) % size) for i in range(size)])]
  transfers between devices with their start and end apart: 6 -> 7, of which waited for: 3 -> 5; matrix products, arithmetic and copies ran while one was open for 1% -> 1% of each run, Pallas kernels for 6% -> 7%
where the time goes in v6:
time: 97.6 us; the launch traced here: 97.4 us
  blocking collectives  47.4 us (49%)
  Pallas kernels  26.4 us (27%)
  starting transfers between devices  11.4 us (12%)
  waiting for transfers between devices  11.4 us (12%)
    all_to_all x2, blocking collectives, exchanged(): rows = lax.all_to_all(rows, 'dp', split_axis=0, concat_axis=0, tiled=True)  47.4 us
    pallas_call x1, Pallas kernels, experts_here(): pl.pallas_call(expert_kernel, out_shape=[jax.ShapeDtypeStruct(rows.shape,...  12.6 us
    ppermute x7, waiting for transfers between devices, passed(): return lax.ppermute(x, axis, [(i, (i + k) % size) for i in range(size)])  11.4 us
    ppermute x7, starting transfers between devices, passed(): return lax.ppermute(x, axis, [(i, (i + k) % size) for i in range(size)])  11.4 us
    pallas_call x1, Pallas kernels, mixer(): pl.pallas_call(lambda *refs: mixer_kernel(heads, *refs), out_shape=[jax.S...  5.69 us
    pallas_call x1, Pallas kernels, first(): pl.pallas_call(first_kernel, out_shape=[pltpu.VMEM(w.shape, w.dtype) for...  4.29 us
  transfers between devices with their start and end apart: 7, of which 5 were waited for; matrix products, arithmetic and copies ran while one was open for 1% of the time, Pallas kernels for 7%

profile of v6, /device:TPU:1, one launch (start us, length us, event | category | flops | bytes accessed | tf_op | source)
XLA Modules:
  0.0 97.4 jit_solution(10885527801151061943)
XLA Ops:
  0.0 2.5 %collective-permute-start = (bf16[256,512]{1,0:T(8,128)(2,1)}, bf16[256,512]{1,0:T(8,128)(2,1)S(1)}, u32[]{:S(2)}, u32[]{:S(2)}) collective-permute-start(bf16[256,512]{1,0:T(8,128)(2,1)} %refs_0_.1), channel_id=1, source_target_pairs={{0,1},{1,2},{2,3},{3,0},{4,5},{5,6},{6,7},{7,4},{8,9},{9,10},{10,1... | collective-permute-start | bytes 786440 | tf_op jit(solution)/shard_map/ppermute | solution.py:476
  2.5 2.1 %collective-permute-start.2 = (bf16[256,512]{1,0:T(8,128)(2,1)}, bf16[256,512]{1,0:T(8,128)(2,1)S(1)}, u32[]{:S(2)}, u32[]{:S(2)}) collective-permute-start(bf16[256,512]{1,0:T(8,128)(2,1)} %refs_0_.1), channel_id=1, source_target_pairs={{0,3},{1,0},{2,1},{3,2},{4,7},{5,4},{6,5},{7,6},{8,11},{9,8},{10,9... | collective-permute-start | bytes 786440 | tf_op jit(solution)/shard_map/ppermute | solution.py:476
  4.6 0.7 reshape.25.gain_ref.refs_1_
  5.3 4.3 %first.1 = (bf16[256,512]{1,0:T(8,128)(2,1)S(1)}, bf16[2048,256]{1,0:T(8,128)(2,1)S(1)}, bf16[3,2048,256]{2,1,0:T(8,128)(2,1)S(1)}, bf16[3,2048,256]{2,1,0:T(8,1...) custom-call(s32[1]{0:T(128)} %bitcast.me_ref.refs_0_, ...), custom_call_target="tpu_custom_call" | custom-call | flops 2000000000 | bytes 1000000 | tf_op jit(solution)/shard_map/first/pallas_call | solution.py:89
  9.6 1.2 %collective-permute-done.refs_2_.refs_3_ = bf16[256,512]{1,0:T(8,128)(2,1)S(1)} collective-permute-done((bf16[256,512]{1,0:T(8,128)(2,1)}, bf16[256,512]{1,0:T(8,128)(2,1)S(1)}, u32[]{:S(2)}, u32[]{:S(2)}) %collective-permute-start) | collective-permute-done | bytes 262176 | tf_op jit(solution)/shard_map/ppermute | solution.py:476
  10.8 0.1 collective-permute-start.1
  10.9 0.0 collective-permute-done.2.refs_2_.refs_4_
  10.9 2.7 %collective-permute-start.3 = (bf16[128,512]{1,0:T(8,128)(2,1)S(1)}, bf16[128,512]{1,0:T(8,128)(2,1)S(1)}, u32[]{:S(2)}, u32[]{:S(2)}) collective-permute-start(bf16[128,512]{1,0:T(8,128)(2,1)S(1)} %slice.9), channel_id=1, source_target_pairs={{0,3},{1,0},{2,1},{3,2},{4,7},{5,4},{6,5},{7,6},{8,11},{9,8},{10,9... | collective-permute-start | bytes 393224 | tf_op jit(solution)/shard_map/ppermute | solution.py:476
  13.6 0.8 more.2
  14.5 0.9 more.3
  15.4 0.5 collective-permute-done.1.refs_2_.refs_5_
  15.9 0.0 collective-permute-done.3.refs_3_.refs_6_
  15.9 0.0 copy-start.1
  15.9 5.7 %mixer.1 = (bf16[64,2048]{1,0:T(8,128)(2,1)S(1)}, bf16[64,2048]{1,0:T(8,128)(2,1)S(1)}, bf16[64,2048]{1,0:T(8,128)(2,1)S(1)}, bf16[64,2048]{1,0:T(8,128)(2,1)S(1)}) custom-call(s32[1]{0:T(128)} %bitcast.me_ref.refs_0_, f32[4,512]{1,0:T(4,128)S(1)} %reshape.25.gain_ref.refs_1_, bf16[128,512]{1,0:T(8,128)(2,1)S(1)} %collective-permute-done.1.refs_2_.refs_5_, ...), custom_call_target="tpu_custom_call" | custom-call | flops 20000000000 | bytes 10000000 | tf_op jit(solution)/shard_map/mixer/pallas_call | solution.py:253
  21.6 0.1 collective-permute-start.4
  21.7 3.9 %collective-permute-start.5 = (bf16[64,2048]{1,0:T(8,128)(2,1)S(1)}, bf16[64,2048]{1,0:T(8,128)(2,1)S(1)}, u32[]{:S(2)}, u32[]{:S(2)}) collective-permute-start(bf16[64,2048]{1,0:T(8,128)(2,1)S(1)} %get-tuple-element.52), channel_id=1, source_target_pairs={{0,2},{1,3},{2,0},{3,1},{4,6},{5,7},{6,4},{7,5},{8,10},{9,11},{10,... | collective-permute-start | bytes 786440 | tf_op jit(solution)/shard_map/ppermute | solution.py:476
  25.6 0.0 collective-permute-start.6
  25.6 0.0 copy-done.1
  25.6 0.0 copy-start.2
  25.6 0.4 ready.1
  26.0 0.0 copy-start
  26.1 2.1 %collective-permute-done.4.p1 = bf16[64,2048]{1,0:T(8,128)(2,1)S(1)} collective-permute-done((bf16[64,2048]{1,0:T(8,128)(2,1)S(1)}, bf16[64,2048]{1,0:T(8,128)(2,1)S(1)}, u32[]{:S(2)}, u32[]{:S(2)}) %collective-permute-start.4) | collective-permute-done | bytes 262176 | tf_op jit(solution)/shard_map/ppermute | solution.py:476
  28.2 6.4 %collective-permute-done.5.p2 = bf16[64,2048]{1,0:T(8,128)(2,1)S(1)} collective-permute-done((bf16[64,2048]{1,0:T(8,128)(2,1)S(1)}, bf16[64,2048]{1,0:T(8,128)(2,1)S(1)}, u32[]{:S(2)}, u32[]{:S(2)}) %collective-permute-start.5) | collective-permute-done | bytes 262176 | tf_op jit(solution)/shard_map/ppermute | solution.py:476
  34.6 1.0 %collective-permute-done.6.p3 = bf16[64,2048]{1,0:T(8,128)(2,1)S(1)} collective-permute-done((bf16[64,2048]{1,0:T(8,128)(2,1)S(1)}, bf16[64,2048]{1,0:T(8,128)(2,1)S(1)}, u32[]{:S(2)}, u32[]{:S(2)}) %collective-permute-start.6) | collective-permute-done | bytes 262176 | tf_op jit(solution)/shard_map/ppermute | solution.py:476
  35.7 0.0 copy-done.2
  35.7 0.7 route.1
  36.3 26.8 %all_to_all.10 = bf16[32,8,2048]{2,1,0:T(8,128)(2,1)S(1)} all-to-all(bf16[32,8,2048]{2,1,0:T(8,128)(2,1)S(1)} %bitcast.11), channel_id=1, replica_groups=mesh['dp'=32,'head'=4] {'dp'}, dimensions={0} | all-to-all | bytes 2097152 | tf_op jit(solution)/shard_map/all_to_all | solution.py:503
  63.1 0.0 copy-done
  63.1 12.6 %experts.1 = (bf16[256,2048]{1,0:T(8,128)(2,1)S(1)}, bf16[128,256]{1,0:T(8,128)(2,1)S(1)}, f32[64,128]{1,0:T(8,128)S(1)}) custom-call(bf16[256,2048]{1,0:T(8,128)(2,1)S(1)} %bitcast.10, bf16[2,2048,1408]{2,1,0:T(8,128)(2,1)} %gate_hbm.1, bf16[2,2048,1408]{2,1,0:T(8,128)(2,1)} %up_hbm.1, bf16[2,1408,2048]{2,1,0:T(8,128)(2,1)} %down_hbm.1, ...), custom_call_target="tpu_custom_call" | custom-call | flops 5000000000 | bytes 10000000 | tf_op jit(solution)/shard_map/experts/pallas_call | solution.py:430
  75.7 20.7 %all_to_all.11 = bf16[32,8,2048]{2,1,0:T(8,128)(2,1)S(1)} all-to-all(bf16[32,8,2048]{2,1,0:T(8,128)(2,1)S(1)} %bitcast.13), channel_id=1, replica_groups=mesh['dp'=32,'head'=4] {'dp'}, dimensions={0} | all-to-all | bytes 2097152 | tf_op jit(solution)/shard_map/all_to_all | solution.py:503
  96.4 1.0 %combine.1 = bf16[64,2048]{1,0:T(8,128)(2,1)} custom-call(f32[64,2048]{1,0:T(8,128)S(1)} %get-tuple-element.55.residual_ref, f32[64,128]{1,0:T(8,128)S(1)} %get-tuple-element.58.leading_ref, bf16[128,256]{1,0:T(8,128)(2,1)S(1)} %get-tuple-element.59.pick_ref, bf16[256,2048]{1,0:T(8,128)(2,1)S(1)} %bitcast.12), custom_call_target="tpu_custom_call" | custom-call | flops 1000000000 | bytes 1000000 | tf_op jit(solution)/shard_map/combine/pallas_call | solution.py:463
  (2 shorter events, 0.0 us)
Async XLA Ops:
  0.0 10.8 %collective-permute-start = (bf16[256,512]{1,0:T(8,128)(2,1)}, bf16[256,512]{1,0:T(8,128)(2,1)S(1)}, u32[]{:S(2)}, u32[]{:S(2)}) collective-permute-start(bf16[256,512]{1,0:T(8,128)(2,1)} %refs_0_.1), channel_id=1, source_target_pairs={{0,1},{1,2},{2,3},{3,0},{4,5},{5,6},{6,7},{7,4},{8,9},{9,10},{10,1... | collective-permute-start | bytes 786440 | tf_op jit(solution)/shard_map/ppermute | solution.py:476
  2.5 8.4 %collective-permute-start.2 = (bf16[256,512]{1,0:T(8,128)(2,1)}, bf16[256,512]{1,0:T(8,128)(2,1)S(1)}, u32[]{:S(2)}, u32[]{:S(2)}) collective-permute-start(bf16[256,512]{1,0:T(8,128)(2,1)} %refs_0_.1), channel_id=1, source_target_pairs={{0,3},{1,0},{2,1},{3,2},{4,7},{5,4},{6,5},{7,6},{8,11},{9,8},{10,9... | collective-permute-start | bytes 786440 | tf_op jit(solution)/shard_map/ppermute | solution.py:476
  10.8 5.1 %collective-permute-start.1 = (bf16[128,512]{1,0:T(8,128)(2,1)S(1)}, bf16[128,512]{1,0:T(8,128)(2,1)S(1)}, u32[]{:S(2)}, u32[]{:S(2)}) collective-permute-start(bf16[128,512]{1,0:T(8,128)(2,1)S(1)} %slice.8), channel_id=1, source_target_pairs={{0,1},{1,2},{2,3},{3,0},{4,5},{5,6},{6,7},{7,4},{8,9},{9,10},{10,1... | collective-permute-start | bytes 393224 | tf_op jit(solution)/shard_map/ppermute | solution.py:476
  10.9 5.0 %collective-permute-start.3 = (bf16[128,512]{1,0:T(8,128)(2,1)S(1)}, bf16[128,512]{1,0:T(8,128)(2,1)S(1)}, u32[]{:S(2)}, u32[]{:S(2)}) collective-permute-start(bf16[128,512]{1,0:T(8,128)(2,1)S(1)} %slice.9), channel_id=1, source_target_pairs={{0,3},{1,0},{2,1},{3,2},{4,7},{5,4},{6,5},{7,6},{8,11},{9,8},{10,9... | collective-permute-start | bytes 393224 | tf_op jit(solution)/shard_map/ppermute | solution.py:476
  15.9 9.7 %copy-start.1 = (s32[64,2]{0,1:T(2,128)S(1)}, s32[64,2]{0,1:T(2,128)}, u32[]{:S(2)}) copy-start(s32[64,2]{0,1:T(2,128)} %param.24) | copy-start | bytes 1540
  21.6 6.6 %collective-permute-start.4 = (bf16[64,2048]{1,0:T(8,128)(2,1)S(1)}, bf16[64,2048]{1,0:T(8,128)(2,1)S(1)}, u32[]{:S(2)}, u32[]{:S(2)}) collective-permute-start(bf16[64,2048]{1,0:T(8,128)(2,1)S(1)} %get-tuple-element.51), channel_id=1, source_target_pairs={{0,1},{1,2},{2,3},{3,0},{4,5},{5,6},{6,7},{7,4},{8,9},{9,10},{10,1... | collective-permute-start | bytes 786440 | tf_op jit(solution)/shard_map/ppermute | solution.py:476
  21.7 12.9 %collective-permute-start.5 = (bf16[64,2048]{1,0:T(8,128)(2,1)S(1)}, bf16[64,2048]{1,0:T(8,128)(2,1)S(1)}, u32[]{:S(2)}, u32[]{:S(2)}) collective-permute-start(bf16[64,2048]{1,0:T(8,128)(2,1)S(1)} %get-tuple-element.52), channel_id=1, source_target_pairs={{0,2},{1,3},{2,0},{3,1},{4,6},{5,7},{6,4},{7,5},{8,10},{9,11},{10,... | collective-permute-start | bytes 786440 | tf_op jit(solution)/shard_map/ppermute | solution.py:476
  25.6 10.1 %collective-permute-start.6 = (bf16[64,2048]{1,0:T(8,128)(2,1)S(1)}, bf16[64,2048]{1,0:T(8,128)(2,1)S(1)}, u32[]{:S(2)}, u32[]{:S(2)}) collective-permute-start(bf16[64,2048]{1,0:T(8,128)(2,1)S(1)} %get-tuple-element.53), channel_id=1, source_target_pairs={{0,3},{1,0},{2,1},{3,2},{4,7},{5,4},{6,5},{7,6},{8,11},{9,8},{10,9... | collective-permute-start | bytes 786440 | tf_op jit(solution)/shard_map/ppermute | solution.py:476
  25.6 10.1 %copy-start.2 = (f32[2048]{0:T(1024)S(1)}, f32[2048]{0:T(1024)}, u32[]{:S(2)}) copy-start(f32[2048]{0:T(1024)} %param.22) | copy-start | bytes 24580
  26.0 37.1 %copy-start = (f32[2048,64]{0,1:T(8,128)S(1)}, f32[2048,64]{0,1:T(8,128)}, u32[]{:S(2)}) copy-start(f32[2048,64]{0,1:T(8,128)} %param.23) | copy-start | bytes 1572868

commit v7 on v6

--- a/solution.py
+++ b/solution.py
@@ -218,20 +218,30 @@
         qs = [queries[i] for i in at]
         attend = [jnp.where(seen, dot(q.astype(BF16), k[:SUB], ((1,), (1,))), 0.0).astype(BF16) for q, k in zip(qs, pairs)]
         effect = [dot(a, s) for a, s in zip(attend, solved)]
-        for i, g, q, e in zip(at, change, qs, effect):
-            state_map[i + (slice(0, CH),)] = (q - e[:, :DK]).astype(BF16)
-            state_map[i + (slice(CH, CH + DK),)] = g[:, :DK].astype(BF16)
-            added[i] = g[:, DK:]
-            out_add[i] = e[:, DK:]
+        reads = [(q - e[:, :DK]) for q, e in zip(qs, effect)]
+        for n in range(0, unroll, 2):
+            for h in range(heads):
+                one, two = n * heads + h, (n + 1) * heads + h
+                pair = (h, (start + n) // 2)
+                later = jnp.concatenate([reads[two], change[two][:, :DK]], 0).astype(BF16)
+                both_steps = dot(later, change[one].astype(BF16))
+                state_map[pair + (slice(0, CH),)] = reads[one].astype(BF16)
+                state_map[pair + (slice(CH, 2 * CH),)] = (reads[two] - both_steps[:CH, :DK]).astype(BF16)
+                state_map[pair + (slice(2 * CH, 2 * CH + DK),)] = (
+                    change[one][:, :DK] + (change[two][:, :DK] - both_steps[CH:, :DK])
+                ).astype(BF16)
+                added[pair] = change[one][:, DK:] + (change[two][:, DK:] - both_steps[CH:, DK:])
+                out_add[pair + (slice(0, CH),)] = effect[one][:, DK:]
+                out_add[pair + (slice(CH, 2 * CH),)] = effect[two][:, DK:] + both_steps[:CH, DK:]
 
     states = [jnp.zeros((DK, DK), F32) for _ in range(heads)]
-    for c in range(blocks):
+    for c in range(blocks // 2):
         for h in range(heads):
             moved = dot(state_map[h, c], states[h].astype(BF16))
-            out = moved[:CH] + out_add[h, c]
-            states[h] = states[h] - moved[CH:] + added[h, c]
+            out = moved[:2 * CH] + out_add[h, c]
+            states[h] = states[h] - moved[2 * CH:] + added[h, c]
             out = out * lax.rsqrt(jnp.mean(out * out, -1, keepdims=True) + EPSILON) * head_gain_ref[...]
-            mixed[c * CH:(c + 1) * CH, h * DK:(h + 1) * DK] = out.astype(BF16)
+            mixed[c * 2 * CH:(c + 1) * 2 * CH, h * DK:(h + 1) * DK] = out.astype(BF16)
     own = length // count
     targets = [me_ref[0]] + [lax.rem(me_ref[0] + shift, count) for shift in SENT]
     rolled = jnp.concatenate([mixed[rows_at(block, own), :] for block in targets], 0)
@@ -260,9 +270,9 @@
             pltpu.VMEM((heads, blocks, SUB, DK), F32),
             pltpu.VMEM((heads, blocks, SUB, 2 * DK), BF16),
             pltpu.VMEM((heads, blocks, CH, DK), F32),
-            pltpu.VMEM((heads, blocks, CH + DK, DK), BF16),
-            pltpu.VMEM((heads, blocks, DK, DK), F32),
-            pltpu.VMEM((heads, blocks, CH, DK), F32),
+            pltpu.VMEM((heads, blocks // 2, 2 * CH + DK, DK), BF16),
+            pltpu.VMEM((heads, blocks // 2, DK, DK), F32),
+            pltpu.VMEM((heads, blocks // 2, 2 * CH, DK), F32),
             pltpu.VMEM((length, heads * DK), BF16),
         ],
         compiler_params=pltpu.CompilerParams(vmem_limit_bytes=32 * MIB),

time: 97.6 us -> 97.3 us (level)
  no operation moved by 1% of the time
where the time goes in v7:
time: 97.3 us; the launch traced here: 97.1 us
  blocking collectives  47.4 us (49%)
  Pallas kernels  26 us (27%)
  starting transfers between devices  11.4 us (12%)
  waiting for transfers between devices  11.4 us (12%)
    all_to_all x2, blocking collectives, exchanged(): rows = lax.all_to_all(rows, 'dp', split_axis=0, concat_axis=0, tiled=True)  47.4 us
    pallas_call x1, Pallas kernels, experts_here(): pl.pallas_call(expert_kernel, out_shape=[jax.ShapeDtypeStruct(rows.shape,...  12.6 us
    ppermute x7, waiting for transfers between devices, passed(): return lax.ppermute(x, axis, [(i, (i + k) % size) for i in range(size)])  11.4 us
    ppermute x7, starting transfers between devices, passed(): return lax.ppermute(x, axis, [(i, (i + k) % size) for i in range(size)])  11.4 us
    pallas_call x1, Pallas kernels, mixer(): pl.pallas_call(lambda *refs: mixer_kernel(heads, *refs), out_shape=[jax.S...  5.34 us
    pallas_call x1, Pallas kernels, first(): pl.pallas_call(first_kernel, out_shape=[pltpu.VMEM(w.shape, w.dtype) for...  4.29 us
  transfers between devices with their start and end apart: 7, of which 5 were waited for; matrix products, arithmetic and copies ran while one was open for 1% of the time, Pallas kernels for 7%

profile of v7, /device:TPU:1, one launch (start us, length us, event | category | flops | bytes accessed | tf_op | source)
XLA Modules:
  0.0 97.1 jit_solution(7203999899570357712)
XLA Ops:
  0.0 2.5 %collective-permute-start = (bf16[256,512]{1,0:T(8,128)(2,1)}, bf16[256,512]{1,0:T(8,128)(2,1)S(1)}, u32[]{:S(2)}, u32[]{:S(2)}) collective-permute-start(bf16[256,512]{1,0:T(8,128)(2,1)} %refs_0_.1), channel_id=1, source_target_pairs={{0,1},{1,2},{2,3},{3,0},{4,5},{5,6},{6,7},{7,4},{8,9},{9,10},{10,1... | collective-permute-start | bytes 786440 | tf_op jit(solution)/shard_map/ppermute | solution.py:486
  2.5 2.1 %collective-permute-start.2 = (bf16[256,512]{1,0:T(8,128)(2,1)}, bf16[256,512]{1,0:T(8,128)(2,1)S(1)}, u32[]{:S(2)}, u32[]{:S(2)}) collective-permute-start(bf16[256,512]{1,0:T(8,128)(2,1)} %refs_0_.1), channel_id=1, source_target_pairs={{0,3},{1,0},{2,1},{3,2},{4,7},{5,4},{6,5},{7,6},{8,11},{9,8},{10,9... | collective-permute-start | bytes 786440 | tf_op jit(solution)/shard_map/ppermute | solution.py:486
  4.6 0.7 reshape.25.gain_ref.refs_1_
  5.3 4.3 %first.1 = (bf16[256,512]{1,0:T(8,128)(2,1)S(1)}, bf16[2048,256]{1,0:T(8,128)(2,1)S(1)}, bf16[3,2048,256]{2,1,0:T(8,128)(2,1)S(1)}, bf16[3,2048,256]{2,1,0:T(8,1...) custom-call(s32[1]{0:T(128)} %bitcast.me_ref.refs_0_, ...), custom_call_target="tpu_custom_call" | custom-call | flops 2000000000 | bytes 1000000 | tf_op jit(solution)/shard_map/first/pallas_call | solution.py:89
  9.6 1.2 %collective-permute-done.refs_2_.refs_3_ = bf16[256,512]{1,0:T(8,128)(2,1)S(1)} collective-permute-done((bf16[256,512]{1,0:T(8,128)(2,1)}, bf16[256,512]{1,0:T(8,128)(2,1)S(1)}, u32[]{:S(2)}, u32[]{:S(2)}) %collective-permute-start) | collective-permute-done | bytes 262176 | tf_op jit(solution)/shard_map/ppermute | solution.py:486
  10.8 0.1 collective-permute-start.1
  10.9 0.0 collective-permute-done.2.refs_2_.refs_4_
  10.9 2.7 %collective-permute-start.3 = (bf16[128,512]{1,0:T(8,128)(2,1)S(1)}, bf16[128,512]{1,0:T(8,128)(2,1)S(1)}, u32[]{:S(2)}, u32[]{:S(2)}) collective-permute-start(bf16[128,512]{1,0:T(8,128)(2,1)S(1)} %slice.9), channel_id=1, source_target_pairs={{0,3},{1,0},{2,1},{3,2},{4,7},{5,4},{6,5},{7,6},{8,11},{9,8},{10,9... | collective-permute-start | bytes 393224 | tf_op jit(solution)/shard_map/ppermute | solution.py:486
  13.6 0.8 more.2
  14.5 0.9 more.3
  15.4 0.5 collective-permute-done.1.refs_2_.refs_5_
  15.9 0.0 collective-permute-done.3.refs_3_.refs_6_
  15.9 0.0 copy-start.1
  15.9 5.3 %mixer.1 = (bf16[64,2048]{1,0:T(8,128)(2,1)S(1)}, bf16[64,2048]{1,0:T(8,128)(2,1)S(1)}, bf16[64,2048]{1,0:T(8,128)(2,1)S(1)}, bf16[64,2048]{1,0:T(8,128)(2,1)S(1)}) custom-call(s32[1]{0:T(128)} %bitcast.me_ref.refs_0_, f32[4,512]{1,0:T(4,128)S(1)} %reshape.25.gain_ref.refs_1_, bf16[128,512]{1,0:T(8,128)(2,1)S(1)} %collective-permute-done.1.refs_2_.refs_5_, ...), custom_call_target="tpu_custom_call" | custom-call | flops 20000000000 | bytes 10000000 | tf_op jit(solution)/shard_map/mixer/pallas_call | solution.py:263
  21.3 0.1 collective-permute-start.4
  21.3 3.9 %collective-permute-start.5 = (bf16[64,2048]{1,0:T(8,128)(2,1)S(1)}, bf16[64,2048]{1,0:T(8,128)(2,1)S(1)}, u32[]{:S(2)}, u32[]{:S(2)}) collective-permute-start(bf16[64,2048]{1,0:T(8,128)(2,1)S(1)} %get-tuple-element.52), channel_id=1, source_target_pairs={{0,2},{1,3},{2,0},{3,1},{4,6},{5,7},{6,4},{7,5},{8,10},{9,11},{10,... | collective-permute-start | bytes 786440 | tf_op jit(solution)/shard_map/ppermute | solution.py:486
  25.3 0.0 collective-permute-start.6
  25.3 0.0 copy-done.1
  25.3 0.0 copy-start.2
  25.3 0.4 ready.1
  25.7 0.0 copy-start
  25.7 2.1 %collective-permute-done.4.p1 = bf16[64,2048]{1,0:T(8,128)(2,1)S(1)} collective-permute-done((bf16[64,2048]{1,0:T(8,128)(2,1)S(1)}, bf16[64,2048]{1,0:T(8,128)(2,1)S(1)}, u32[]{:S(2)}, u32[]{:S(2)}) %collective-permute-start.4) | collective-permute-done | bytes 262176 | tf_op jit(solution)/shard_map/ppermute | solution.py:486
  27.9 6.5 %collective-permute-done.5.p2 = bf16[64,2048]{1,0:T(8,128)(2,1)S(1)} collective-permute-done((bf16[64,2048]{1,0:T(8,128)(2,1)S(1)}, bf16[64,2048]{1,0:T(8,128)(2,1)S(1)}, u32[]{:S(2)}, u32[]{:S(2)}) %collective-permute-start.5) | collective-permute-done | bytes 262176 | tf_op jit(solution)/shard_map/ppermute | solution.py:486
  34.3 1.0 %collective-permute-done.6.p3 = bf16[64,2048]{1,0:T(8,128)(2,1)S(1)} collective-permute-done((bf16[64,2048]{1,0:T(8,128)(2,1)S(1)}, bf16[64,2048]{1,0:T(8,128)(2,1)S(1)}, u32[]{:S(2)}, u32[]{:S(2)}) %collective-permute-start.6) | collective-permute-done | bytes 262176 | tf_op jit(solution)/shard_map/ppermute | solution.py:486
  35.4 0.0 copy-done.2
  35.4 0.7 route.1
  36.0 26.7 %all_to_all.10 = bf16[32,8,2048]{2,1,0:T(8,128)(2,1)S(1)} all-to-all(bf16[32,8,2048]{2,1,0:T(8,128)(2,1)S(1)} %bitcast.11), channel_id=1, replica_groups=mesh['dp'=32,'head'=4] {'dp'}, dimensions={0} | all-to-all | bytes 2097152 | tf_op jit(solution)/shard_map/all_to_all | solution.py:513
  62.8 0.0 copy-done
  62.8 12.6 %experts.1 = (bf16[256,2048]{1,0:T(8,128)(2,1)S(1)}, bf16[128,256]{1,0:T(8,128)(2,1)S(1)}, f32[64,128]{1,0:T(8,128)S(1)}) custom-call(bf16[256,2048]{1,0:T(8,128)(2,1)S(1)} %bitcast.10, bf16[2,2048,1408]{2,1,0:T(8,128)(2,1)} %gate_hbm.1, bf16[2,2048,1408]{2,1,0:T(8,128)(2,1)} %up_hbm.1, bf16[2,1408,2048]{2,1,0:T(8,128)(2,1)} %down_hbm.1, ...), custom_call_target="tpu_custom_call" | custom-call | flops 5000000000 | bytes 10000000 | tf_op jit(solution)/shard_map/experts/pallas_call | solution.py:440
  75.4 20.7 %all_to_all.11 = bf16[32,8,2048]{2,1,0:T(8,128)(2,1)S(1)} all-to-all(bf16[32,8,2048]{2,1,0:T(8,128)(2,1)S(1)} %bitcast.13), channel_id=1, replica_groups=mesh['dp'=32,'head'=4] {'dp'}, dimensions={0} | all-to-all | bytes 2097152 | tf_op jit(solution)/shard_map/all_to_all | solution.py:513
  96.1 1.0 %combine.1 = bf16[64,2048]{1,0:T(8,128)(2,1)} custom-call(f32[64,2048]{1,0:T(8,128)S(1)} %get-tuple-element.55.residual_ref, f32[64,128]{1,0:T(8,128)S(1)} %get-tuple-element.58.leading_ref, bf16[128,256]{1,0:T(8,128)(2,1)S(1)} %get-tuple-element.59.pick_ref, bf16[256,2048]{1,0:T(8,128)(2,1)S(1)} %bitcast.12), custom_call_target="tpu_custom_call" | custom-call | flops 1000000000 | bytes 1000000 | tf_op jit(solution)/shard_map/combine/pallas_call | solution.py:473
  (2 shorter events, 0.0 us)
Async XLA Ops:
  0.0 10.8 %collective-permute-start = (bf16[256,512]{1,0:T(8,128)(2,1)}, bf16[256,512]{1,0:T(8,128)(2,1)S(1)}, u32[]{:S(2)}, u32[]{:S(2)}) collective-permute-start(bf16[256,512]{1,0:T(8,128)(2,1)} %refs_0_.1), channel_id=1, source_target_pairs={{0,1},{1,2},{2,3},{3,0},{4,5},{5,6},{6,7},{7,4},{8,9},{9,10},{10,1... | collective-permute-start | bytes 786440 | tf_op jit(solution)/shard_map/ppermute | solution.py:486
  2.5 8.4 %collective-permute-start.2 = (bf16[256,512]{1,0:T(8,128)(2,1)}, bf16[256,512]{1,0:T(8,128)(2,1)S(1)}, u32[]{:S(2)}, u32[]{:S(2)}) collective-permute-start(bf16[256,512]{1,0:T(8,128)(2,1)} %refs_0_.1), channel_id=1, source_target_pairs={{0,3},{1,0},{2,1},{3,2},{4,7},{5,4},{6,5},{7,6},{8,11},{9,8},{10,9... | collective-permute-start | bytes 786440 | tf_op jit(solution)/shard_map/ppermute | solution.py:486
  10.8 5.1 %collective-permute-start.1 = (bf16[128,512]{1,0:T(8,128)(2,1)S(1)}, bf16[128,512]{1,0:T(8,128)(2,1)S(1)}, u32[]{:S(2)}, u32[]{:S(2)}) collective-permute-start(bf16[128,512]{1,0:T(8,128)(2,1)S(1)} %slice.8), channel_id=1, source_target_pairs={{0,1},{1,2},{2,3},{3,0},{4,5},{5,6},{6,7},{7,4},{8,9},{9,10},{10,1... | collective-permute-start | bytes 393224 | tf_op jit(solution)/shard_map/ppermute | solution.py:486
  10.9 5.0 %collective-permute-start.3 = (bf16[128,512]{1,0:T(8,128)(2,1)S(1)}, bf16[128,512]{1,0:T(8,128)(2,1)S(1)}, u32[]{:S(2)}, u32[]{:S(2)}) collective-permute-start(bf16[128,512]{1,0:T(8,128)(2,1)S(1)} %slice.9), channel_id=1, source_target_pairs={{0,3},{1,0},{2,1},{3,2},{4,7},{5,4},{6,5},{7,6},{8,11},{9,8},{10,9... | collective-permute-start | bytes 393224 | tf_op jit(solution)/shard_map/ppermute | solution.py:486
  15.9 9.4 %copy-start.1 = (s32[64,2]{0,1:T(2,128)S(1)}, s32[64,2]{0,1:T(2,128)}, u32[]{:S(2)}) copy-start(s32[64,2]{0,1:T(2,128)} %param.24) | copy-start | bytes 1540
  21.3 6.6 %collective-permute-start.4 = (bf16[64,2048]{1,0:T(8,128)(2,1)S(1)}, bf16[64,2048]{1,0:T(8,128)(2,1)S(1)}, u32[]{:S(2)}, u32[]{:S(2)}) collective-permute-start(bf16[64,2048]{1,0:T(8,128)(2,1)S(1)} %get-tuple-element.51), channel_id=1, source_target_pairs={{0,1},{1,2},{2,3},{3,0},{4,5},{5,6},{6,7},{7,4},{8,9},{9,10},{10,1... | collective-permute-start | bytes 786440 | tf_op jit(solution)/shard_map/ppermute | solution.py:486
  21.3 13.0 %collective-permute-start.5 = (bf16[64,2048]{1,0:T(8,128)(2,1)S(1)}, bf16[64,2048]{1,0:T(8,128)(2,1)S(1)}, u32[]{:S(2)}, u32[]{:S(2)}) collective-permute-start(bf16[64,2048]{1,0:T(8,128)(2,1)S(1)} %get-tuple-element.52), channel_id=1, source_target_pairs={{0,2},{1,3},{2,0},{3,1},{4,6},{5,7},{6,4},{7,5},{8,10},{9,11},{10,... | collective-permute-start | bytes 786440 | tf_op jit(solution)/shard_map/ppermute | solution.py:486
  25.3 10.1 %collective-permute-start.6 = (bf16[64,2048]{1,0:T(8,128)(2,1)S(1)}, bf16[64,2048]{1,0:T(8,128)(2,1)S(1)}, u32[]{:S(2)}, u32[]{:S(2)}) collective-permute-start(bf16[64,2048]{1,0:T(8,128)(2,1)S(1)} %get-tuple-element.53), channel_id=1, source_target_pairs={{0,3},{1,0},{2,1},{3,2},{4,7},{5,4},{6,5},{7,6},{8,11},{9,8},{10,9... | collective-permute-start | bytes 786440 | tf_op jit(solution)/shard_map/ppermute | solution.py:486
  25.3 10.1 %copy-start.2 = (f32[2048]{0:T(1024)S(1)}, f32[2048]{0:T(1024)}, u32[]{:S(2)}) copy-start(f32[2048]{0:T(1024)} %param.22) | copy-start | bytes 24580
  25.7 37.1 %copy-start = (f32[2048,64]{0,1:T(8,128)S(1)}, f32[2048,64]{0,1:T(8,128)}, u32[]{:S(2)}) copy-start(f32[2048,64]{0,1:T(8,128)} %param.23) | copy-start | bytes 1572868

commit v8 on v7

--- a/solution.py
+++ b/solution.py
@@ -39,7 +39,7 @@
 
 
 NEAR = (1, 3)
-SENT = (1, 2, 3)
+SENT = (2, 1, 3)
 
 
 def source_of(me_ref, shift, count):

time: 97.3 us -> 96.7 us (level)
  blocking collectives: 47.4 us -> 46.3 us
    all_to_all x2, blocking collectives: 47.4 us -> 46.3 us  [exchanged(): rows = lax.all_to_all(rows, 'dp', split_axis=0, concat_axis=0, tiled=True)]
  transfers between devices with their start and end apart: 7 -> 7, of which waited for: 5 -> 4; matrix products, arithmetic and copies ran while one was open for 1% -> 1% of each run, Pallas kernels for 7% -> 7%
where the time goes in v8:
time: 96.7 us; the launch traced here: 96.5 us
  blocking collectives  46.3 us (48%)
  Pallas kernels  26 us (27%)
  starting transfers between devices  11.7 us (12%)
  waiting for transfers between devices  11.6 us (12%)
    all_to_all x2, blocking collectives, exchanged(): rows = lax.all_to_all(rows, 'dp', split_axis=0, concat_axis=0, tiled=True)  46.3 us
    pallas_call x1, Pallas kernels, experts_here(): pl.pallas_call(expert_kernel, out_shape=[jax.ShapeDtypeStruct(rows.shape,...  12.6 us
    ppermute x7, starting transfers between devices, passed(): return lax.ppermute(x, axis, [(i, (i + k) % size) for i in range(size)])  11.7 us
    ppermute x7, waiting for transfers between devices, passed(): return lax.ppermute(x, axis, [(i, (i + k) % size) for i in range(size)])  11.6 us
    pallas_call x1, Pallas kernels, mixer(): pl.pallas_call(lambda *refs: mixer_kernel(heads, *refs), out_shape=[jax.S...  5.34 us
    pallas_call x1, Pallas kernels, first(): pl.pallas_call(first_kernel, out_shape=[pltpu.VMEM(w.shape, w.dtype) for...  4.29 us
  transfers between devices with their start and end apart: 7, of which 4 were waited for; matrix products, arithmetic and copies ran while one was open for 1% of the time, Pallas kernels for 7%

profile of v8, /device:TPU:1, one launch (start us, length us, event | category | flops | bytes accessed | tf_op | source)
XLA Modules:
  0.0 96.5 jit_solution(10167784015266185001)
XLA Ops:
  0.0 2.5 %collective-permute-start = (bf16[256,512]{1,0:T(8,128)(2,1)}, bf16[256,512]{1,0:T(8,128)(2,1)S(1)}, u32[]{:S(2)}, u32[]{:S(2)}) collective-permute-start(bf16[256,512]{1,0:T(8,128)(2,1)} %refs_0_.1), channel_id=1, source_target_pairs={{0,1},{1,2},{2,3},{3,0},{4,5},{5,6},{6,7},{7,4},{8,9},{9,10},{10,1... | collective-permute-start | bytes 786440 | tf_op jit(solution)/shard_map/ppermute | solution.py:486
  2.5 2.1 %collective-permute-start.2 = (bf16[256,512]{1,0:T(8,128)(2,1)}, bf16[256,512]{1,0:T(8,128)(2,1)S(1)}, u32[]{:S(2)}, u32[]{:S(2)}) collective-permute-start(bf16[256,512]{1,0:T(8,128)(2,1)} %refs_0_.1), channel_id=1, source_target_pairs={{0,3},{1,0},{2,1},{3,2},{4,7},{5,4},{6,5},{7,6},{8,11},{9,8},{10,9... | collective-permute-start | bytes 786440 | tf_op jit(solution)/shard_map/ppermute | solution.py:486
  4.6 0.7 reshape.25.gain_ref.refs_1_
  5.3 4.3 %first.1 = (bf16[256,512]{1,0:T(8,128)(2,1)S(1)}, bf16[2048,256]{1,0:T(8,128)(2,1)S(1)}, bf16[3,2048,256]{2,1,0:T(8,128)(2,1)S(1)}, bf16[3,2048,256]{2,1,0:T(8,1...) custom-call(s32[1]{0:T(128)} %bitcast.me_ref.refs_0_, ...), custom_call_target="tpu_custom_call" | custom-call | flops 2000000000 | bytes 1000000 | tf_op jit(solution)/shard_map/first/pallas_call | solution.py:89
  9.6 1.2 %collective-permute-done.refs_2_.refs_3_ = bf16[256,512]{1,0:T(8,128)(2,1)S(1)} collective-permute-done((bf16[256,512]{1,0:T(8,128)(2,1)}, bf16[256,512]{1,0:T(8,128)(2,1)S(1)}, u32[]{:S(2)}, u32[]{:S(2)}) %collective-permute-start) | collective-permute-done | bytes 262176 | tf_op jit(solution)/shard_map/ppermute | solution.py:486
  10.8 0.1 collective-permute-start.1
  10.9 0.0 collective-permute-done.2.refs_2_.refs_4_
  10.9 2.7 %collective-permute-start.3 = (bf16[128,512]{1,0:T(8,128)(2,1)S(1)}, bf16[128,512]{1,0:T(8,128)(2,1)S(1)}, u32[]{:S(2)}, u32[]{:S(2)}) collective-permute-start(bf16[128,512]{1,0:T(8,128)(2,1)S(1)} %slice.9), channel_id=1, source_target_pairs={{0,3},{1,0},{2,1},{3,2},{4,7},{5,4},{6,5},{7,6},{8,11},{9,8},{10,9... | collective-permute-start | bytes 393224 | tf_op jit(solution)/shard_map/ppermute | solution.py:486
  13.6 0.8 more.2
  14.5 0.9 more.3
  15.4 0.5 collective-permute-done.1.refs_2_.refs_5_
  15.9 0.0 collective-permute-done.3.refs_3_.refs_6_
  15.9 0.0 copy-start.1
  15.9 5.3 %mixer.1 = (bf16[64,2048]{1,0:T(8,128)(2,1)S(1)}, bf16[64,2048]{1,0:T(8,128)(2,1)S(1)}, bf16[64,2048]{1,0:T(8,128)(2,1)S(1)}, bf16[64,2048]{1,0:T(8,128)(2,1)S(1)}) custom-call(s32[1]{0:T(128)} %bitcast.me_ref.refs_0_, f32[4,512]{1,0:T(4,128)S(1)} %reshape.25.gain_ref.refs_1_, bf16[128,512]{1,0:T(8,128)(2,1)S(1)} %collective-permute-done.1.refs_2_.refs_5_, ...), custom_call_target="tpu_custom_call" | custom-call | flops 20000000000 | bytes 10000000 | tf_op jit(solution)/shard_map/mixer/pallas_call | solution.py:263
  21.3 1.6 %collective-permute-start.4 = (bf16[64,2048]{1,0:T(8,128)(2,1)S(1)}, bf16[64,2048]{1,0:T(8,128)(2,1)S(1)}, u32[]{:S(2)}, u32[]{:S(2)}) collective-permute-start(bf16[64,2048]{1,0:T(8,128)(2,1)S(1)} %get-tuple-element.51), channel_id=1, source_target_pairs={{0,2},{1,3},{2,0},{3,1},{4,6},{5,7},{6,4},{7,5},{8,10},{9,11},{10,... | collective-permute-start | bytes 786440 | tf_op jit(solution)/shard_map/ppermute | solution.py:486
  22.9 1.8 %collective-permute-start.5 = (bf16[64,2048]{1,0:T(8,128)(2,1)S(1)}, bf16[64,2048]{1,0:T(8,128)(2,1)S(1)}, u32[]{:S(2)}, u32[]{:S(2)}) collective-permute-start(bf16[64,2048]{1,0:T(8,128)(2,1)S(1)} %get-tuple-element.52), channel_id=1, source_target_pairs={{0,1},{1,2},{2,3},{3,0},{4,5},{5,6},{6,7},{7,4},{8,9},{9,10},{10,1... | collective-permute-start | bytes 786440 | tf_op jit(solution)/shard_map/ppermute | solution.py:486
  24.7 0.9 collective-permute-start.6
  25.6 0.0 copy-done.1
  25.6 0.0 copy-start.2
  25.6 0.4 ready.1
  26.0 0.0 copy-start
  26.0 2.2 %collective-permute-done.4.p1 = bf16[64,2048]{1,0:T(8,128)(2,1)S(1)} collective-permute-done((bf16[64,2048]{1,0:T(8,128)(2,1)S(1)}, bf16[64,2048]{1,0:T(8,128)(2,1)S(1)}, u32[]{:S(2)}, u32[]{:S(2)}) %collective-permute-start.4) | collective-permute-done | bytes 262176 | tf_op jit(solution)/shard_map/ppermute | solution.py:486
  28.2 7.7 %collective-permute-done.5.p2 = bf16[64,2048]{1,0:T(8,128)(2,1)S(1)} collective-permute-done((bf16[64,2048]{1,0:T(8,128)(2,1)S(1)}, bf16[64,2048]{1,0:T(8,128)(2,1)S(1)}, u32[]{:S(2)}, u32[]{:S(2)}) %collective-permute-start.5) | collective-permute-done | bytes 262176 | tf_op jit(solution)/shard_map/ppermute | solution.py:486
  35.8 0.0 collective-permute-done.6.p3
  35.8 0.0 copy-done.2
  35.8 0.7 route.1
  36.5 25.7 %all_to_all.10 = bf16[32,8,2048]{2,1,0:T(8,128)(2,1)S(1)} all-to-all(bf16[32,8,2048]{2,1,0:T(8,128)(2,1)S(1)} %bitcast.11), channel_id=1, replica_groups=mesh['dp'=32,'head'=4] {'dp'}, dimensions={0} | all-to-all | bytes 2097152 | tf_op jit(solution)/shard_map/all_to_all | solution.py:513
  62.2 0.0 copy-done
  62.2 12.6 %experts.1 = (bf16[256,2048]{1,0:T(8,128)(2,1)S(1)}, bf16[128,256]{1,0:T(8,128)(2,1)S(1)}, f32[64,128]{1,0:T(8,128)S(1)}) custom-call(bf16[256,2048]{1,0:T(8,128)(2,1)S(1)} %bitcast.10, bf16[2,2048,1408]{2,1,0:T(8,128)(2,1)} %gate_hbm.1, bf16[2,2048,1408]{2,1,0:T(8,128)(2,1)} %up_hbm.1, bf16[2,1408,2048]{2,1,0:T(8,128)(2,1)} %down_hbm.1, ...), custom_call_target="tpu_custom_call" | custom-call | flops 5000000000 | bytes 10000000 | tf_op jit(solution)/shard_map/experts/pallas_call | solution.py:440
  74.8 20.7 %all_to_all.11 = bf16[32,8,2048]{2,1,0:T(8,128)(2,1)S(1)} all-to-all(bf16[32,8,2048]{2,1,0:T(8,128)(2,1)S(1)} %bitcast.13), channel_id=1, replica_groups=mesh['dp'=32,'head'=4] {'dp'}, dimensions={0} | all-to-all | bytes 2097152 | tf_op jit(solution)/shard_map/all_to_all | solution.py:513
  95.5 1.0 %combine.1 = bf16[64,2048]{1,0:T(8,128)(2,1)} custom-call(f32[64,2048]{1,0:T(8,128)S(1)} %get-tuple-element.55.residual_ref, f32[64,128]{1,0:T(8,128)S(1)} %get-tuple-element.58.leading_ref, bf16[128,256]{1,0:T(8,128)(2,1)S(1)} %get-tuple-element.59.pick_ref, bf16[256,2048]{1,0:T(8,128)(2,1)S(1)} %bitcast.12), custom_call_target="tpu_custom_call" | custom-call | flops 1000000000 | bytes 1000000 | tf_op jit(solution)/shard_map/combine/pallas_call | solution.py:473
  (2 shorter events, 0.0 us)
Async XLA Ops:
  0.0 10.8 %collective-permute-start = (bf16[256,512]{1,0:T(8,128)(2,1)}, bf16[256,512]{1,0:T(8,128)(2,1)S(1)}, u32[]{:S(2)}, u32[]{:S(2)}) collective-permute-start(bf16[256,512]{1,0:T(8,128)(2,1)} %refs_0_.1), channel_id=1, source_target_pairs={{0,1},{1,2},{2,3},{3,0},{4,5},{5,6},{6,7},{7,4},{8,9},{9,10},{10,1... | collective-permute-start | bytes 786440 | tf_op jit(solution)/shard_map/ppermute | solution.py:486
  2.5 8.4 %collective-permute-start.2 = (bf16[256,512]{1,0:T(8,128)(2,1)}, bf16[256,512]{1,0:T(8,128)(2,1)S(1)}, u32[]{:S(2)}, u32[]{:S(2)}) collective-permute-start(bf16[256,512]{1,0:T(8,128)(2,1)} %refs_0_.1), channel_id=1, source_target_pairs={{0,3},{1,0},{2,1},{3,2},{4,7},{5,4},{6,5},{7,6},{8,11},{9,8},{10,9... | collective-permute-start | bytes 786440 | tf_op jit(solution)/shard_map/ppermute | solution.py:486
  10.8 5.1 %collective-permute-start.1 = (bf16[128,512]{1,0:T(8,128)(2,1)S(1)}, bf16[128,512]{1,0:T(8,128)(2,1)S(1)}, u32[]{:S(2)}, u32[]{:S(2)}) collective-permute-start(bf16[128,512]{1,0:T(8,128)(2,1)S(1)} %slice.8), channel_id=1, source_target_pairs={{0,1},{1,2},{2,3},{3,0},{4,5},{5,6},{6,7},{7,4},{8,9},{9,10},{10,1... | collective-permute-start | bytes 393224 | tf_op jit(solution)/shard_map/ppermute | solution.py:486
  10.9 5.0 %collective-permute-start.3 = (bf16[128,512]{1,0:T(8,128)(2,1)S(1)}, bf16[128,512]{1,0:T(8,128)(2,1)S(1)}, u32[]{:S(2)}, u32[]{:S(2)}) collective-permute-start(bf16[128,512]{1,0:T(8,128)(2,1)S(1)} %slice.9), channel_id=1, source_target_pairs={{0,3},{1,0},{2,1},{3,2},{4,7},{5,4},{6,5},{7,6},{8,11},{9,8},{10,9... | collective-permute-start | bytes 393224 | tf_op jit(solution)/shard_map/ppermute | solution.py:486
  15.9 9.7 %copy-start.1 = (s32[64,2]{0,1:T(2,128)S(1)}, s32[64,2]{0,1:T(2,128)}, u32[]{:S(2)}) copy-start(s32[64,2]{0,1:T(2,128)} %param.24) | copy-start | bytes 1540
  21.3 6.9 %collective-permute-start.4 = (bf16[64,2048]{1,0:T(8,128)(2,1)S(1)}, bf16[64,2048]{1,0:T(8,128)(2,1)S(1)}, u32[]{:S(2)}, u32[]{:S(2)}) collective-permute-start(bf16[64,2048]{1,0:T(8,128)(2,1)S(1)} %get-tuple-element.51), channel_id=1, source_target_pairs={{0,2},{1,3},{2,0},{3,1},{4,6},{5,7},{6,4},{7,5},{8,10},{9,11},{10,... | collective-permute-start | bytes 786440 | tf_op jit(solution)/shard_map/ppermute | solution.py:486
  22.9 12.9 %collective-permute-start.5 = (bf16[64,2048]{1,0:T(8,128)(2,1)S(1)}, bf16[64,2048]{1,0:T(8,128)(2,1)S(1)}, u32[]{:S(2)}, u32[]{:S(2)}) collective-permute-start(bf16[64,2048]{1,0:T(8,128)(2,1)S(1)} %get-tuple-element.52), channel_id=1, source_target_pairs={{0,1},{1,2},{2,3},{3,0},{4,5},{5,6},{6,7},{7,4},{8,9},{9,10},{10,1... | collective-permute-start | bytes 786440 | tf_op jit(solution)/shard_map/ppermute | solution.py:486
  24.7 11.2 %collective-permute-start.6 = (bf16[64,2048]{1,0:T(8,128)(2,1)S(1)}, bf16[64,2048]{1,0:T(8,128)(2,1)S(1)}, u32[]{:S(2)}, u32[]{:S(2)}) collective-permute-start(bf16[64,2048]{1,0:T(8,128)(2,1)S(1)} %get-tuple-element.53), channel_id=1, source_target_pairs={{0,3},{1,0},{2,1},{3,2},{4,7},{5,4},{6,5},{7,6},{8,11},{9,8},{10,9... | collective-permute-start | bytes 786440 | tf_op jit(solution)/shard_map/ppermute | solution.py:486
  25.6 10.3 %copy-start.2 = (f32[2048]{0:T(1024)S(1)}, f32[2048]{0:T(1024)}, u32[]{:S(2)}) copy-start(f32[2048]{0:T(1024)} %param.22) | copy-start | bytes 24580
  26.0 36.2 %copy-start = (f32[2048,64]{0,1:T(8,128)S(1)}, f32[2048,64]{0,1:T(8,128)}, u32[]{:S(2)}) copy-start(f32[2048,64]{0,1:T(8,128)} %param.23) | copy-start | bytes 1572868
